TPU v7x, 512 devices: a 4x2x32 block of a 4x8x32 slice. The times are simulated.
512 devices in a mesh: groups: 2 (over y), space: 32 (over z), rhs: 8 (over x, core).
Axes of the slice: x: 4, y: 2, z: 32, core: 2. Of those that a mesh axis runs over, the one named last changes fastest.
The devices are a block of a 4x8x32 slice.
Arguments:
- conductance: float32 [512, 1024], P(('groups', 'space')), parts along dimension 0, may hold values from 0.05 to 2
- nodata: int32 [512, 1024], P(('groups', 'space')), parts along dimension 0, may hold values 0 or 1
- ground_mask: int32 [512, 1024], P(('groups', 'space')), parts along dimension 0, may hold values 0 or 1
- ground_value: float32 [512, 1024], P(('groups', 'space')), parts along dimension 0, may hold values from 0.5 to 4
- source_mask: int32 [512, 1024], P(('groups', 'space')), parts along dimension 0, may hold values 0 or 1
- source_current: float32 [512, 1024], P(('groups', 'space')), parts along dimension 0, may hold values from 0.5 to 4
- tile_inverse: float32 [512, 8, 128, 128], P(('groups', 'space')), parts along dimension 0, may hold values from -0.04 to 8, as said below
- focal_cells: int32 [1024, 2], P(('groups', 'rhs')), parts along dimension 0, may hold values from 0 to 262143
Outputs:
- solution: float32 [512, 512, 1024], P('rhs', ('groups', 'space')), parts along dimension 1
- residual: float32 [512, 512, 1024], P('rhs', ('groups', 'space')), parts along dimension 1
There are 2 independent parts, one for each index of `groups`. A program takes and returns all parts, laid end to end along the dimension named above; each array names one. Nothing has to cross between parts.
Inputs may be any that keep to these rules, and one draw needn't show every extreme that they name: `tile_inverse`: each block is symmetric positive definite.
All inputs are finite; a program needn't handle non-finite values. No bound on the sum of `nodata` or of `ground_mask` or of `source_mask` on one device may be relied on, other than what follows from the above.
Results may differ from a plain program's by a relative error of at most 0.00025.
Values sent between devices are 32-bit elements; how exact they have to be, the bound alone decides.
No kernel may reach another device: no remote copies, remote signals or barrier semaphores. Data moves between devices by JAX's collectives and lax.ppermute only.
A program may use at most 64 MiB of HBM per device.

v0:
```python
import jax
import jax.numpy as jnp
from jax import lax
from jax.sharding import PartitionSpec as P

ITERS = 2


LEAKAGE = 0.05
FOCAL_CURRENT = 16.0


def with_halo(cells, sides, width):
    for axis, dim in sides:
        count = lax.axis_size(axis)
        ends = count - 1
        head = lax.slice_in_dim(cells, 0, width, axis=dim)
        tail = lax.slice_in_dim(cells, cells.shape[dim] - width, cells.shape[dim], axis=dim)
        cells = jnp.concatenate(
            [
                lax.ppermute(tail, axis, [(i, (i + 1) % count) for i in range(ends)]),
                cells,
                lax.ppermute(head, axis, [((i + 1) % count, i) for i in range(ends)]),
            ],
            axis=dim,
        )
    return cells


def from_everyone(x, axis):
    copies = jnp.broadcast_to(x, (lax.axis_size(axis), *x.shape))
    return lax.all_to_all(copies, axis, split_axis=0, concat_axis=0, tiled=True)


def over_copies(x, axis):
    everything = from_everyone(x, axis)
    return jnp.sum(everything, axis=0)


def in_one(arrays, axis):
    ends = [0]
    for a in arrays:
        ends.append(ends[-1] + a.size)
    total = over_copies(jnp.concatenate([a.ravel() for a in arrays]), axis)
    return tuple((total[b:e].reshape(a.shape) for a, b, e in zip(arrays, ends, ends[1:])))


def weights_from(padded_g, padded_v, valid_mask, ground_mask, ground_value):
    centre = padded_g[1:-1, 1:-1]
    north_w = 0.5 * (centre + padded_g[:-2, 1:-1]) * valid_mask * padded_v[:-2, 1:-1]
    south_w = 0.5 * (centre + padded_g[2:, 1:-1]) * valid_mask * padded_v[2:, 1:-1]
    west_w = 0.5 * (centre + padded_g[1:-1, :-2]) * valid_mask * padded_v[1:-1, :-2]
    east_w = 0.5 * (centre + padded_g[1:-1, 2:]) * valid_mask * padded_v[1:-1, 2:]
    grounded = ground_mask.astype(jnp.float32) * ground_value
    diagonal = (
        valid_mask * (LEAKAGE + grounded) + (1.0 - valid_mask) + north_w + south_w + west_w + east_w
    )
    return (diagonal, north_w, south_w, west_w, east_w)


def stencil(padded, weights):
    diagonal, north_w, south_w, west_w, east_w = weights
    centre = padded[:, 1:-1, 1:-1]
    return (
        diagonal * centre
        - north_w * padded[:, :-2, 1:-1]
        - south_w * padded[:, 2:, 1:-1]
        - west_w * padded[:, 1:-1, :-2]
        - east_w * padded[:, 1:-1, 2:]
    )


def pad_columns(rimmed):
    return jnp.pad(rimmed, ((0, 0), (0, 0), (1, 1)))


def precondition(field_in, tile_inverse):
    pair_count, row_count, col_count = field_in.shape
    blocks = field_in.reshape(pair_count, row_count, col_count // 128, 128)
    result = jnp.einsum(
        "rcij,prcj->prci",
        tile_inverse,
        blocks,
        precision=lax.Precision.HIGHEST,
        preferred_element_type=jnp.float32,
    )
    return result.reshape(pair_count, row_count, col_count)


def inner_sum(first, second):
    return jnp.sum(first * second, axis=(1, 2))


def search_image(precond, weights):
    rimmed = with_halo(precond, (("space", 1),), 1)
    return stencil(pad_columns(rimmed), weights)


def paired_sums(residual, precond, image):
    return in_one((inner_sum(residual, precond), inner_sum(image, precond)), "space")


def on_device(
    conductance,
    nodata,
    ground_mask,
    ground_value,
    source_mask,
    source_current,
    tile_inverse,
    focal_cells,
):
    valid_mask = (1 - nodata).astype(jnp.float32)
    active = conductance * valid_mask
    stacked = jnp.stack([active, valid_mask])
    rimmed = with_halo(stacked, (("space", 1),), 1)
    rimmed = pad_columns(rimmed)
    weights = weights_from(rimmed[0], rimmed[1], valid_mask, ground_mask, ground_value)
    row_count, col_count = conductance.shape
    offset = lax.axis_index("space") * (row_count * col_count)
    cell_ids = offset + jnp.arange(row_count * col_count, dtype=jnp.int32)
    onehot = (cell_ids[None, :] == focal_cells[:, 0:1]).astype(jnp.float32) - (
        cell_ids[None, :] == focal_cells[:, 1:2]
    ).astype(jnp.float32)
    onehot = onehot.reshape(focal_cells.shape[0], row_count, col_count)
    background = source_mask.astype(jnp.float32) * source_current
    right_side = background[None] + FOCAL_CURRENT * onehot
    solution = jnp.zeros_like(right_side)
    residual = right_side
    precond = precondition(residual, tile_inverse)
    image = search_image(precond, weights)
    gamma_now, curvature = paired_sums(residual, precond, image)
    step_len = gamma_now / curvature
    direction = precond
    along = image
    for iteration in range(ITERS):
        solution = solution + step_len[:, None, None] * direction
        residual = residual - step_len[:, None, None] * along
        if iteration + 1 < ITERS:
            precond = precondition(residual, tile_inverse)
            image = search_image(precond, weights)
            gamma_next, curvature = paired_sums(residual, precond, image)
            ratio_next = gamma_next / gamma_now
            step_len = gamma_next / (curvature - ratio_next * gamma_next / step_len)
            direction = precond + ratio_next[:, None, None] * direction
            along = image + ratio_next[:, None, None] * along
            gamma_now = gamma_next
    return (solution, residual)


def solution(mesh):
    return jax.shard_map(
        on_device,
        mesh=mesh,
        in_specs=(
            P(("groups", "space"), None),
            P(("groups", "space"), None),
            P(("groups", "space"), None),
            P(("groups", "space"), None),
            P(("groups", "space"), None),
            P(("groups", "space"), None),
            P(("groups", "space"), None, None, None),
            P(("groups", "rhs"), None),
        ),
        out_specs=(P("rhs", ("groups", "space"), None), P("rhs", ("groups", "space"), None)),
        check_vma=False,
    )
```

profile of v0, /device:TPU:40, one launch (start us, length us, event | category | flops | bytes accessed | tf_op | source)
XLA Modules:
  0.0 184.5 jit_solution(5197858267015392264)
XLA Ops:
  0.6 0.8 convert_bitcast_fusion
  1.4 0.8 multiply_bitcast_fusion
  2.2 4.7 %collective-permute-start = (f32[2,1,1024]{2,1,0:T(1,128)S(1)}, f32[2,1,1024]{2,1,0:T(1,128)S(1)}, u32[]{:S(2)}, u32[]{:S(2)}) collective-permute-start(f32[2,1,1024]{2,1,0:T(1,128)S(1)} %get-tuple-element.19), channel_id=1, source_target_pairs={{0,8},{8,16},{16,24},{24,32},{32,40},{40,48},{48,56},{56,64},{64,7... | collective-permute-start | bytes 24584 | tf_op jit(solution)/shard_map/ppermute | solution.py:21
  6.9 1.3 collective-permute-start.1
  8.2 0.8 slice_bitcast_fusion.3
  9.0 0.8 convert_multiply_fusion
  9.8 10.3 %multiply_reduce_fusion.3 = (f32[64]{0:T(128)S(1)}, f32[64,8,8,128]{3,0,2,1:T(8,128)S(1)}) fusion(s32[8,8,128]{2,1,0:T(8,128)S(1)} %add_add_fusion.2, f32[8,8,128]{2,1,0:T(8,128)S(1)} %copy.20, s32[64]{0:T(128)S(1)} %get-tuple-element.22, s32[64]{0:T(128)S(1)} %get-tuple-element.21, f32[8,8,128,128]{3,2,1,0:T(8,128)} %param.14), kind=kOutput, calls=%fused_computation.35 | convolution fusion | flops 813694912 | bytes 6357760 | tf_op jit(solution)/shard_map/rcij,prcj->prci/dot_general | solution.py:80
  20.1 2.5 %copy.21 = f32[64,8,8,128]{3,2,1,0:T(8,128)} copy(f32[64,8,8,128]{3,0,2,1:T(8,128)S(1)} %get-tuple-element.24) | data formatting | bytes 4194304 | tf_op jit(solution)/shard_map/rcij,prcj->prci/transpose | solution.py:80
  22.7 0.0 copy-start.5
  22.7 0.0 copy-start.6
  22.7 0.0 copy-start.7
  22.7 1.7 reshape.82
  24.4 0.0 copy-start
  24.4 0.3 fusion.40
  24.8 5.4 %collective-permute-start.2 = (f32[64,1,1024]{2,1,0:T(1,128)S(1)}, f32[64,1,1024]{2,1,0:T(1,128)S(1)}, u32[]{:S(2)}, u32[]{:S(2)}) collective-permute-start(f32[64,1,1024]{2,1,0:T(1,128)S(1)} %get-tuple-element.15), channel_id=1, source_target_pairs={{0,8},{8,16},{16,24},{24,32},{32,40},{40,48},{48,56},{56,64},{64,7... | collective-permute-start | bytes 786440 | tf_op jit(solution)/shard_map/ppermute | solution.py:21
  30.1 1.3 collective-permute-start.3
  31.4 0.0 collective-permute-done
  31.5 0.0 collective-permute-done.1
  31.5 0.1 select_maximum_fusion.4
  31.6 0.0 copy-done.5
  31.6 0.0 copy-done.6
  31.7 0.0 copy-done.7
  31.7 0.1 add_add_fusion.1
  31.8 3.6 %collective-permute-done.2 = f32[64,1,1024]{2,1,0:T(1,128)S(1)} collective-permute-done((f32[64,1,1024]{2,1,0:T(1,128)S(1)}, f32[64,1,1024]{2,1,0:T(1,128)S(1)}, u32[]{:S(2)}, u32[]{:S(2)}) %collective-permute-start.2) | collective-permute-done | bytes 262176 | tf_op jit(solution)/shard_map/ppermute | solution.py:21
  35.4 5.2 %collective-permute-done.3 = f32[64,1,1024]{2,1,0:T(1,128)S(1)} collective-permute-done((f32[64,1,1024]{2,1,0:T(1,128)S(1)}, f32[64,1,1024]{2,1,0:T(1,128)S(1)}, u32[]{:S(2)}, u32[]{:S(2)}) %collective-permute-start.3) | collective-permute-done | bytes 262176 | tf_op jit(solution)/shard_map/ppermute | solution.py:23
  40.6 3.4 %select_maximum_fusion.2 = f32[64,10,1026]{2,1,0:T(8,128)S(1)} fusion(f32[64,1,1024]{2,1,0:T(1,128)S(1)} %collective-permute-done.3, f32[64,8,1024]{2,1,0:T(8,128)S(1)} %reshape.82, f32[64,1,1024]{2,1,0:T(1,128)S(1)} %collective-permute-done.2), kind=kLoop, calls=%fused_computation.4 | loop fusion | flops 5253120 | bytes 5248000 | tf_op jit(solution)/shard_map/concatenate | solution.py:19
  44.0 0.0 copy-done
  44.0 3.0 %multiply_reduce_fusion.2 = (f32[64]{0:T(128)S(1)}, f32[64,8,1024]{2,1,0:T(8,128)}) fusion(f32[64,8,1024]{2,1,0:T(8,128)S(1)} %reshape.82, f32[64,10,1026]{2,1,0:T(8,128)S(1)} %select_maximum_fusion.2, f32[8,1024]{1,0:T(8,128)S(1)} %get-tuple-element.12, f32[8,1024]{1,0:T(8,128)S(1)} %get-tuple-element.11, f32[64,1,1024]{2,1,0:T(1,128)S(1)} %collective-permute-done.3, ...), kind=kLoop, calls=%fused_computation.34 | loop fusion | flops 6815680 | bytes 9076992 | tf_op jit(solution)/shard_map/reduce_sum | solution.py:91
  47.0 0.1 pad_maximum_fusion.6
  47.1 0.6 broadcast_in_dim.4
  47.7 44.9 %all-to-all-start = ((f32[32,1,128]{2,1,0:T(1,128)}), f32[32,1,128]{2,1,0:T(1,128)S(1)}, u32[]{:S(2)}, u32[]{:S(2)}) async-start(f32[32,1,128]{2,1,0:T(1,128)} %broadcast_in_dim.4), calls=%async_computation | async-start | bytes 32768 | tf_op jit(solution)/shard_map/all_to_all | solution.py:32
  92.6 21.5 %all-to-all-done = f32[32,1,128]{2,1,0:T(1,128)S(1)} async-done(((f32[32,1,128]{2,1,0:T(1,128)}), f32[32,1,128]{2,1,0:T(1,128)S(1)}, u32[]{:S(2)}, u32[]{:S(2)}) %all-to-all-start) | async-done | bytes 16416 | tf_op jit(solution)/shard_map/all_to_all | solution.py:32
  114.1 0.1 slice_divide_fusion.1
  114.2 0.0 copy-start.4
  114.2 2.4 %fusion.22 = f32[64,8,8,128]{3,1,2,0:T(8,128)S(1)} fusion(f32[64,8,1024]{2,1,0:T(8,128)} %get-tuple-element.7, s32[8,1024]{1,0:T(8,128)S(1)} %add_add_fusion, f32[8,1024]{1,0:T(8,128)S(1)} %convert_multiply_fusion, f32[64]{0:T(128)S(1)} %slice_divide_fusion.1, s32[64]{0:T(128)S(1)} %get-tuple-element.22, s32[64]{0:T(128)S(1)} %get-tuple-element.21), kind=kLoop, calls=%fused_computation.42 | loop fusion | flops 4718592 | bytes 4260608 | tf_op jit(solution)/shard_map/reshape | solution.py:79
  116.6 0.4 copy-done.4
  117.0 8.3 %fusion.18 = f32[64,8,8,128]{3,0,2,1:T(8,128)S(1)} fusion(f32[8,8,128,128]{3,2,1,0:T(8,128)S(1)} %copy-done.4, f32[64,8,8,128]{3,1,2,0:T(8,128)S(1)} %fusion.22), kind=kOutput, calls=%fused_computation.40 | convolution fusion | flops 805306368 | bytes 8388608 | tf_op jit(solution)/shard_map/rcij,prcj->prci/dot_general | solution.py:80
  125.3 2.5 %copy.24 = f32[64,8,8,128]{3,2,1,0:T(8,128)} copy(f32[64,8,8,128]{3,0,2,1:T(8,128)S(1)} %fusion.18) | data formatting | bytes 4194304 | tf_op jit(solution)/shard_map/rcij,prcj->prci/transpose | solution.py:80
  127.9 1.7 reshape.84
  129.6 0.3 fusion.39
  129.9 2.4 %collective-permute-start.4 = (f32[64,1,1024]{2,1,0:T(1,128)S(1)}, f32[64,1,1024]{2,1,0:T(1,128)S(1)}, u32[]{:S(2)}, u32[]{:S(2)}) collective-permute-start(f32[64,1,1024]{2,1,0:T(1,128)S(1)} %get-tuple-element.13), channel_id=1, source_target_pairs={{0,8},{8,16},{16,24},{24,32},{32,40},{40,48},{48,56},{56,64},{64,7... | collective-permute-start | bytes 786440 | tf_op jit(solution)/shard_map/ppermute | solution.py:21
  132.3 0.0 copy-start.3
  132.4 1.7 collective-permute-start.5
  134.0 2.2 %collective-permute-done.4 = f32[64,1,1024]{2,1,0:T(1,128)S(1)} collective-permute-done((f32[64,1,1024]{2,1,0:T(1,128)S(1)}, f32[64,1,1024]{2,1,0:T(1,128)S(1)}, u32[]{:S(2)}, u32[]{:S(2)}) %collective-permute-start.4) | collective-permute-done | bytes 262176 | tf_op jit(solution)/shard_map/ppermute | solution.py:21
  136.2 4.6 %collective-permute-done.5 = f32[64,1,1024]{2,1,0:T(1,128)S(1)} collective-permute-done((f32[64,1,1024]{2,1,0:T(1,128)S(1)}, f32[64,1,1024]{2,1,0:T(1,128)S(1)}, u32[]{:S(2)}, u32[]{:S(2)}) %collective-permute-start.5) | collective-permute-done | bytes 262176 | tf_op jit(solution)/shard_map/ppermute | solution.py:23
  140.8 3.4 %select_maximum_fusion = f32[64,10,1026]{2,1,0:T(8,128)S(1)} fusion(f32[64,1,1024]{2,1,0:T(1,128)S(1)} %collective-permute-done.5, f32[64,8,1024]{2,1,0:T(8,128)S(1)} %reshape.84, f32[64,1,1024]{2,1,0:T(1,128)S(1)} %collective-permute-done.4), kind=kLoop, calls=%fused_computation.2 | loop fusion | flops 5253120 | bytes 5248000 | tf_op jit(solution)/shard_map/concatenate | solution.py:19
  144.1 0.0 copy-done.3
  144.2 0.0 copy-start.1
  144.2 3.5 %multiply_reduce_fusion.1 = (f32[64]{0:T(128)S(1)}, f32[64]{0:T(128)S(1)}) fusion(f32[64,8,1024]{2,1,0:T(8,128)S(1)} %reshape.84, f32[64,8,1024]{2,1,0:T(8,128)S(1)} %copy-done.3, s32[8,1024]{1,0:T(8,128)S(1)} %add_add_fusion, f32[8,1024]{1,0:T(8,128)S(1)} %convert_multiply_fusion, f32[64]{0:T(128)S(1)} %slice_divide_fusion.1, s32[64]{0:T(128)S(1)} %get-tuple-element.22, ...), kind=kLoop, calls=%fused_computation.32 | loop fusion | flops 12582784 | bytes 9143552 | tf_op jit(solution)/shard_map/reduce_sum | solution.py:91
  147.6 0.0 copy-done.1
  147.6 0.1 pad_maximum_fusion.7
  147.7 27.9 %all_to_all.12 = f32[32,1,128]{2,1,0:T(1,128)S(1)} all-to-all(f32[32,1,128]{2,1,0:T(1,128)S(1)} %broadcast_in_dim.5), channel_id=1, replica_groups=mesh['groups'=2,'space'=32,'rhs'=8] {'space'}, dimensions={0} | all-to-all | bytes 32768 | tf_op jit(solution)/shard_map/all_to_all | solution.py:32
  175.6 0.1 subtract_divide_fusion
  175.7 0.0 copy-start.2
  175.7 3.5 %multiply_add_fusion = f32[64,8,1024]{2,1,0:T(8,128)} fusion(f32[64,8,1024]{2,1,0:T(8,128)S(1)} %reshape.84, f32[64,8,1024]{2,1,0:T(8,128)} %copy-done, f32[64]{0:T(128)S(1)} %get-tuple-element.5, f32[64]{0:T(128)S(1)} %get-tuple-element.4, f32[64]{0:T(128)S(1)} %slice_divide_fusion.1), kind=kLoop, calls=%fused_computation.30 | loop fusion | flops 2621440 | bytes 6292224 | tf_op jit(solution)/shard_map/add | solution.py:137
  179.2 0.0 copy-done.2
  179.2 5.3 %multiply_subtract_fusion = f32[64,8,1024]{2,1,0:T(8,128)} fusion(f32[64,8,1024]{2,1,0:T(8,128)} %get-tuple-element.7, f32[64]{0:T(128)S(1)} %get-tuple-element.5, f32[64]{0:T(128)S(1)} %get-tuple-element.4, s32[8,1024]{1,0:T(8,128)S(1)} %add_add_fusion, f32[8,1024]{1,0:T(8,128)S(1)} %convert_multiply_fusion, f32[64]{0:T(128)S(1)} %slice_divide_fusion.1, ...), kind=kLoop, calls=%fused_computation.29 | loop fusion | flops 12582912 | bytes 11240704 | tf_op jit(solution)/shard_map/sub | solution.py:138
  (8 shorter events, 0.1 us)
Async XLA Ops:
  2.2 29.3 %collective-permute-start = (f32[2,1,1024]{2,1,0:T(1,128)S(1)}, f32[2,1,1024]{2,1,0:T(1,128)S(1)}, u32[]{:S(2)}, u32[]{:S(2)}) collective-permute-start(f32[2,1,1024]{2,1,0:T(1,128)S(1)} %get-tuple-element.19), channel_id=1, source_target_pairs={{0,8},{8,16},{16,24},{24,32},{32,40},{40,48},{48,56},{56,64},{64,7... | collective-permute-start | bytes 24584 | tf_op jit(solution)/shard_map/ppermute | solution.py:21
  6.9 24.6 %collective-permute-start.1 = (f32[2,1,1024]{2,1,0:T(1,128)S(1)}, f32[2,1,1024]{2,1,0:T(1,128)S(1)}, u32[]{:S(2)}, u32[]{:S(2)}) collective-permute-start(f32[2,1,1024]{2,1,0:T(1,128)S(1)} %get-tuple-element.20), channel_id=1, source_target_pairs={{8,0},{16,8},{24,16},{32,24},{40,32},{48,40},{56,48},{64,56},{72,6... | collective-permute-start | bytes 24584 | tf_op jit(solution)/shard_map/ppermute | solution.py:23
  22.7 9.0 %copy-start.5 = (s32[8,1024]{1,0:T(8,128)S(1)}, s32[8,1024]{1,0:T(8,128)}, u32[]{:S(2)}) copy-start(s32[8,1024]{1,0:T(8,128)} %param.9) | copy-start | bytes 98308
  22.7 9.0 %copy-start.6 = (f32[8,1024]{1,0:T(8,128)S(1)}, f32[8,1024]{1,0:T(8,128)}, u32[]{:S(2)}) copy-start(f32[8,1024]{1,0:T(8,128)} %param.11) | copy-start | bytes 98308
  22.7 9.0 %copy-start.7 = (s32[8,1024]{1,0:T(8,128)S(1)}, s32[8,1024]{1,0:T(8,128)}, u32[]{:S(2)}) copy-start(s32[8,1024]{1,0:T(8,128)} %param.10) | copy-start | bytes 98308
  24.4 19.6 %copy-start = (f32[64,8,1024]{2,1,0:T(8,128)}, f32[64,8,1024]{2,1,0:T(8,128)S(1)}, u32[]{:S(2)}) copy-start(f32[64,8,1024]{2,1,0:T(8,128)S(1)} %reshape.82) | copy-start | bytes 6291460
  24.8 10.7 %collective-permute-start.2 = (f32[64,1,1024]{2,1,0:T(1,128)S(1)}, f32[64,1,1024]{2,1,0:T(1,128)S(1)}, u32[]{:S(2)}, u32[]{:S(2)}) collective-permute-start(f32[64,1,1024]{2,1,0:T(1,128)S(1)} %get-tuple-element.15), channel_id=1, source_target_pairs={{0,8},{8,16},{16,24},{24,32},{32,40},{40,48},{48,56},{56,64},{64,7... | collective-permute-start | bytes 786440 | tf_op jit(solution)/shard_map/ppermute | solution.py:21
  30.1 10.5 %collective-permute-start.3 = (f32[64,1,1024]{2,1,0:T(1,128)S(1)}, f32[64,1,1024]{2,1,0:T(1,128)S(1)}, u32[]{:S(2)}, u32[]{:S(2)}) collective-permute-start(f32[64,1,1024]{2,1,0:T(1,128)S(1)} %get-tuple-element.16), channel_id=1, source_target_pairs={{8,0},{16,8},{24,16},{32,24},{40,32},{48,40},{56,48},{64,56},{72,6... | collective-permute-start | bytes 786440 | tf_op jit(solution)/shard_map/ppermute | solution.py:23
  47.7 66.4 %all-to-all-start = ((f32[32,1,128]{2,1,0:T(1,128)}), f32[32,1,128]{2,1,0:T(1,128)S(1)}, u32[]{:S(2)}, u32[]{:S(2)}) async-start(f32[32,1,128]{2,1,0:T(1,128)} %broadcast_in_dim.4), calls=%async_computation | async-start | bytes 32768 | tf_op jit(solution)/shard_map/all_to_all | solution.py:32
  114.2 2.8 %copy-start.4 = (f32[8,8,128,128]{3,2,1,0:T(8,128)S(1)}, f32[8,8,128,128]{3,2,1,0:T(8,128)}, u32[]{:S(2)}) copy-start(f32[8,8,128,128]{3,2,1,0:T(8,128)} %param.14) | copy-start | bytes 12582916
  129.9 6.3 %collective-permute-start.4 = (f32[64,1,1024]{2,1,0:T(1,128)S(1)}, f32[64,1,1024]{2,1,0:T(1,128)S(1)}, u32[]{:S(2)}, u32[]{:S(2)}) collective-permute-start(f32[64,1,1024]{2,1,0:T(1,128)S(1)} %get-tuple-element.13), channel_id=1, source_target_pairs={{0,8},{8,16},{16,24},{24,32},{32,40},{40,48},{48,56},{56,64},{64,7... | collective-permute-start | bytes 786440 | tf_op jit(solution)/shard_map/ppermute | solution.py:21
  132.3 11.8 %copy-start.3 = (f32[64,8,1024]{2,1,0:T(8,128)S(1)}, f32[64,8,1024]{2,1,0:T(8,128)}, u32[]{:S(2)}) copy-start(f32[64,8,1024]{2,1,0:T(8,128)} %get-tuple-element.7) | copy-start | bytes 6291460
  132.4 8.4 %collective-permute-start.5 = (f32[64,1,1024]{2,1,0:T(1,128)S(1)}, f32[64,1,1024]{2,1,0:T(1,128)S(1)}, u32[]{:S(2)}, u32[]{:S(2)}) collective-permute-start(f32[64,1,1024]{2,1,0:T(1,128)S(1)} %get-tuple-element.14), channel_id=1, source_target_pairs={{8,0},{16,8},{24,16},{32,24},{40,32},{48,40},{56,48},{64,56},{72,6... | collective-permute-start | bytes 786440 | tf_op jit(solution)/shard_map/ppermute | solution.py:23
  144.2 3.5 %copy-start.1 = (f32[64,10,1026]{2,1,0:T(8,128)}, f32[64,10,1026]{2,1,0:T(8,128)S(1)}, u32[]{:S(2)}) copy-start(f32[64,10,1026]{2,1,0:T(8,128)S(1)} %select_maximum_fusion) | copy-start | bytes 7879684
  175.7 3.5 %copy-start.2 = (f32[64,10,1026]{2,1,0:T(8,128)S(1)}, f32[64,10,1026]{2,1,0:T(8,128)}, u32[]{:S(2)}) copy-start(f32[64,10,1026]{2,1,0:T(8,128)} %copy-done.1) | copy-start | bytes 7879684
where the time goes:
time: 185 us; the launch traced here: 184 us
  starting transfers between devices  61.7 us (33%)
  waiting for transfers between devices  37.1 us (20%)
  blocking collectives  27.9 us (15%)
  other arithmetic  27.3 us (15%)
  matrix products  18.6 us (10%)
  local copies, waits for them, and re-layouts  11 us (6%)
    all_to_all x1, starting transfers between devices, from_everyone(): return lax.all_to_all(copies, axis, split_axis=0, concat_axis=0, tiled=True)  44.9 us
    all_to_all x1, blocking collectives, from_everyone(): return lax.all_to_all(copies, axis, split_axis=0, concat_axis=0, tiled=True)  27.9 us
    all_to_all x1, waiting for transfers between devices, from_everyone(): return lax.all_to_all(copies, axis, split_axis=0, concat_axis=0, tiled=True)  21.5 us
    dot_general x2, matrix products, precondition(): jnp.einsum('rcij,prcj->prci', tile_inverse, blocks, precision=lax.Precisi...  18.6 us
    ppermute x3, starting transfers between devices, with_halo(): lax.ppermute(tail, axis, [(i, (i + 1) % count) for i in range(ends)])  12.5 us
    ppermute x3, waiting for transfers between devices, with_halo(): lax.ppermute(head, axis, [((i + 1) % count, i) for i in range(ends)])  9.78 us
    concatenate x3, other arithmetic, with_halo(): jnp.concatenate([lax.ppermute(tail, axis, [(i, (i + 1) % count) for i in...  6.85 us
    reduce_sum x2, other arithmetic, inner_sum(): return jnp.sum(first * second, axis=(1, 2))  6.42 us
  transfers between devices with their start and end apart: 7, of which 5 were waited for; matrix products, arithmetic and copies ran while one was open for 9% of the time, Pallas kernels for 0%

commit v1 on v0

v1 whole, which is shorter than its diff:
```python
import functools

import jax
import jax.numpy as jnp
from jax import lax
from jax.experimental import pallas as pl
from jax.experimental.pallas import tpu as pltpu
from jax.sharding import PartitionSpec as P

LEAKAGE = 0.05
FOCAL_CURRENT = 16.0
TILE = 128
CHUNK = 16
MIB = 1024 * 1024


def cut(x):
    high = x.astype(jnp.bfloat16)
    return high, (x - high.astype(jnp.float32)).astype(jnp.bfloat16)


def load(field, at):
    return jnp.concatenate([field[t, at, :] for t in range(field.shape[0])], axis=1)


def store(field, at, x):
    for t in range(field.shape[0]):
        field[t, at, :] = x[:, t * TILE : (t + 1) * TILE]


def apply_tiles(src, dst, tiles, row, rows, count):
    chunks = (count + CHUNK - 1) // CHUNK

    for t in range(src.shape[0]):
        high, low = cut(tiles[0, t])

        def one(c, _):
            at = pl.ds(c * (CHUNK * rows) + row, CHUNK, stride=rows)
            x_high, x_low = cut(src.at[t][at, :])
            x = jnp.concatenate([x_high, x_low], axis=0)
            a = jnp.dot(x, high, preferred_element_type=jnp.float32)
            b = jnp.dot(x, low, preferred_element_type=jnp.float32)
            dst.at[t][at, :] = (a[:CHUNK] + b[CHUNK:]) + (a[CHUNK:] + b[:CHUNK])
            return 0

        one(0, 0)
        lax.fori_loop(1, chunks, one, 0)


def shifted(x, above, below, rows, cols):
    row = lax.broadcasted_iota(jnp.int32, (rows, cols), 0)
    up = jnp.where(row == 0, above, pltpu.roll(x, 1, 0))
    down = jnp.where(row == rows - 1, below, pltpu.roll(x, rows - 1, 0))
    return up, down, pltpu.roll(x, 1, 1), pltpu.roll(x, cols - 1, 1)


def operator(x, above, below, weights, rows, cols):
    up, down, left, right = shifted(x, above, below, rows, cols)
    diag, north, south, west, east = weights
    return diag * x - north * up - south * down - west * left - east * right


def fill_rims(field, index, up_ref, down_ref, rows, pairs, count):
    cols = up_ref.shape[1]
    first, last = load(field, slice(0, 1)), load(field, slice(rows - 1, rows))
    up_ref[0 : pairs + 8, :] = jnp.broadcast_to(first, (pairs + 8, cols))
    down_ref[0 : pairs + 8, :] = jnp.broadcast_to(last, (pairs + 8, cols))

    def one(s, _):
        k = index[pairs + s]
        up_ref[pl.ds(k, 1), :] = load(field, pl.ds(s * rows, 1))
        down_ref[pl.ds(k, 1), :] = load(field, pl.ds(s * rows + rows - 1, 1))
        return 0

    lax.fori_loop(1, count, one, 0)


def start_kernel(
    where, focal, mask, current, cond, nodata, tiles, field, pre, index, up_ref, down_ref, *, rows, cols, pairs, slots
):
    r = pl.program_id(0)
    base_row = where[0]

    @pl.when(r == 0)
    def _():
        background = mask[...].astype(jnp.float32) * current[...]
        store(field, slice(0, rows), background)
        index[pairs] = pairs

        def listed(k, s):
            a = lax.div(focal[2 * k], cols) - base_row
            b = lax.div(focal[2 * k + 1], cols) - base_row
            near = ((a >= -2) & (a < rows + 2)) | ((b >= -2) & (b < rows + 2))
            index[k] = jnp.where(near, s, 0)

            @pl.when(near)
            def _():
                index[pairs + s] = k

            return s + near.astype(jnp.int32)

        count = lax.fori_loop(0, pairs, listed, jnp.int32(1))
        index[pairs + slots] = count
        lane = lax.broadcasted_iota(jnp.int32, (1, TILE), 1)

        def one(s, _):
            k = index[pairs + s]
            store(field, pl.ds(s * rows, rows), background)
            for end in range(2):
                cell = focal[2 * k + end]
                i = lax.div(cell, cols)
                j = cell - i * cols
                i = i - base_row

                @pl.when((i >= 0) & (i < rows))
                def _():
                    t = lax.div(j, TILE)
                    at = pl.ds(s * rows + i, 1)
                    sign = FOCAL_CURRENT * (1 - 2 * end)
                    field[t, at, :] = field[t, at, :] + jnp.where(lane == j - t * TILE, sign, 0.0)

            return 0

        lax.fori_loop(1, count, one, 0)

    count = index[pairs + slots]
    apply_tiles(field, pre, tiles, r, rows, count)

    @pl.when(r == rows - 1)
    def _():
        fill_rims(pre, index, up_ref, down_ref, rows, pairs, count)
        valid = (1 - nodata[...]).astype(jnp.float32)
        active = cond[...] * valid
        up_ref[pairs + 1 : pairs + 2, :] = active[0:1, :]
        up_ref[pairs + 2 : pairs + 3, :] = valid[0:1, :]
        down_ref[pairs + 1 : pairs + 2, :] = active[rows - 1 : rows, :]
        down_ref[pairs + 2 : pairs + 3, :] = valid[rows - 1 : rows, :]


def middle_kernel(
    index,
    cond,
    nodata,
    ground_mask,
    ground_value,
    pre,
    above,
    below,
    tiles,
    image,
    second,
    weights,
    up_ref,
    down_ref,
    *,
    rows,
    cols,
    pairs,
    slots,
):
    r = pl.program_id(0)
    count = index[pairs + slots]

    @pl.when(r == 0)
    def _():
        valid = (1 - nodata[...]).astype(jnp.float32)
        active = cond[...] * valid
        lane = lax.broadcasted_iota(jnp.int32, (rows, cols), 1)
        g = shifted(active, above[pairs + 1 : pairs + 2, :], below[pairs + 1 : pairs + 2, :], rows, cols)
        v = shifted(valid, above[pairs + 2 : pairs + 3, :], below[pairs + 2 : pairs + 3, :], rows, cols)
        inside = (None, None, lane > 0, lane < cols - 1)
        edges = []
        for n in range(4):
            edge = 0.5 * (active + g[n]) * valid * v[n]
            if inside[n] is not None:
                edge = jnp.where(inside[n], edge, 0.0)
            edges.append(edge)
        grounded = ground_mask[...].astype(jnp.float32) * ground_value[...]
        diag = valid * (LEAKAGE + grounded) + (1.0 - valid) + edges[0] + edges[1] + edges[2] + edges[3]
        for n, x in enumerate([diag, *edges]):
            weights[n * rows : (n + 1) * rows, :] = x

        def one(s, _):
            k = index[pairs + s]
            at = pl.ds(s * rows, rows)
            w = [weights[n * rows : (n + 1) * rows, :] for n in range(5)]
            store(image, at, operator(load(pre, at), above[pl.ds(k, 1), :], below[pl.ds(k, 1), :], w, rows, cols))
            return 0

        lax.fori_loop(0, count, one, 0)

    apply_tiles(image, second, tiles, r, rows, count)

    @pl.when(r == rows - 1)
    def _():
        fill_rims(second, index, up_ref, down_ref, rows, pairs, count)


def sums_kernel(
    index, field, pre, image, second, above, below, weights, last, sums, one_two, three_four, *, rows, cols, pairs, slots
):
    count = index[pairs + slots]

    def folded(x):
        acc = x[:, 0:TILE]
        for t in range(1, cols // TILE):
            acc = acc + x[:, t * TILE : (t + 1) * TILE]
        return jnp.sum(acc, axis=0, keepdims=True)

    def four(s):
        k = index[pairs + s]
        at = pl.ds(s * rows, rows)
        w = [weights[n * rows : (n + 1) * rows, :] for n in range(5)]
        u = load(second, at)
        v = operator(u, above[pl.ds(k, 1), :], below[pl.ds(k, 1), :], w, rows, cols)
        store(last, at, v)
        z, i = load(pre, at), load(image, at)
        return k, folded(load(field, at) * z), folded(z * i), folded(i * u), folded(u * v)

    _, a, b, c, d = four(0)
    one_two[0:pairs, :] = jnp.broadcast_to(a, (pairs, TILE))
    one_two[pairs : 2 * pairs, :] = jnp.broadcast_to(b, (pairs, TILE))
    three_four[0:pairs, :] = jnp.broadcast_to(c, (pairs, TILE))
    three_four[pairs : 2 * pairs, :] = jnp.broadcast_to(d, (pairs, TILE))

    def one(s, _):
        k, a, b, c, d = four(s)
        one_two[pl.ds(k, 1), :] = a
        one_two[pl.ds(pairs + k, 1), :] = b
        three_four[pl.ds(k, 1), :] = c
        three_four[pl.ds(pairs + k, 1), :] = d
        return 0

    lax.fori_loop(1, count, one, 0)
    sums[0:1, :] = jnp.sum(one_two[...].T, axis=0, keepdims=True)
    sums[1:2, :] = jnp.sum(three_four[...].T, axis=0, keepdims=True)


def finish_kernel(
    index, everyone, field, pre, image, second, last, solution, residual, first_c, second_c, *, rows, cols, pairs, block
):
    step = pl.program_id(0)

    @pl.when(step == 0)
    def _():
        total = jnp.sum(everyone[...], axis=0)
        ab, cd = total[0:1, :], total[1:2, :]
        gamma, delta = ab[:, :pairs], ab[:, pairs:]
        eta, theta = cd[:, :pairs], cd[:, pairs:]
        alpha = gamma / delta
        gamma_next = alpha * alpha * eta - gamma
        beta = 1.0 + gamma_next / gamma
        curvature = beta * beta * delta - 2.0 * beta * alpha * eta + alpha * alpha * theta
        step_next = gamma_next / curvature
        both = jnp.concatenate([alpha + step_next * beta, alpha * step_next], axis=1)
        spread = jnp.broadcast_to(both, (2 * pairs, 2 * pairs)).T
        first_c[...] = spread[:pairs, :]
        second_c[...] = spread[pairs:, :]

    def one(p, _):
        k = step * block + p
        s = index[k]
        at = pl.ds(s * rows, rows)
        a = jnp.broadcast_to(first_c[pl.ds(k, 1), :], (rows, TILE))
        b = jnp.broadcast_to(second_c[pl.ds(k, 1), :], (rows, TILE))
        for t in range(cols // TILE):
            lanes = slice(t * TILE, (t + 1) * TILE)
            solution[p, :, lanes] = a * pre[t, at, :] - b * second[t, at, :]
            residual[p, :, lanes] = field[t, at, :] - a * image[t, at, :] + b * last[t, at, :]
        return 0

    lax.fori_loop(0, block, one, 0, unroll=2)


def smem():
    return pl.BlockSpec(memory_space=pltpu.SMEM)


def whole(*shape):
    return pl.BlockSpec(shape, lambda *_: (0,) * len(shape))


def neighbours(up, down):
    count = lax.axis_size("space")
    ends = count - 1
    above = lax.ppermute(down, "space", [(i, (i + 1) % count) for i in range(ends)])
    below = lax.ppermute(up, "space", [((i + 1) % count, i) for i in range(ends)])
    return above, below


def on_device(conductance, nodata, ground_mask, ground_value, source_mask, source_current, tile_inverse, focal_cells):
    rows, cols = conductance.shape
    pairs = focal_cells.shape[0]
    slots = -(-(pairs + 1) // CHUNK) * CHUNK
    devices = lax.axis_size("space")
    f32 = jnp.float32
    sizes = dict(rows=rows, cols=cols, pairs=pairs, slots=slots)
    strip, fields, rim = (rows, cols), (cols // TILE, slots * rows, TILE), (pairs + 8, cols)
    tile_block = pl.BlockSpec((1, cols // TILE, TILE, TILE), lambda r: (r, 0, 0, 0))
    limit = pltpu.CompilerParams(vmem_limit_bytes=32 * MIB)
    base_row = (lax.axis_index("space") * rows).astype(jnp.int32).reshape(1)

    field, pre, index, up, down = pl.pallas_call(
        functools.partial(start_kernel, **sizes),
        grid=(rows,),
        in_specs=[smem(), smem(), whole(*strip), whole(*strip), whole(*strip), whole(*strip), tile_block],
        out_specs=[whole(*fields), whole(*fields), smem(), whole(*rim), whole(*rim)],
        out_shape=[
            jax.ShapeDtypeStruct(fields, f32),
            jax.ShapeDtypeStruct(fields, f32),
            jax.ShapeDtypeStruct((pairs + slots + 8,), jnp.int32),
            jax.ShapeDtypeStruct(rim, f32),
            jax.ShapeDtypeStruct(rim, f32),
        ],
        compiler_params=limit,
        name="start",
    )(base_row, focal_cells.reshape(-1), source_mask, source_current, conductance, nodata, tile_inverse)
    above, below = neighbours(up, down)

    image, second, weights, up, down = pl.pallas_call(
        functools.partial(middle_kernel, **sizes),
        grid=(rows,),
        in_specs=[smem(), *[whole(*strip)] * 4, whole(*fields), whole(*rim), whole(*rim), tile_block],
        out_specs=[whole(*fields), whole(*fields), whole(5 * rows, cols), whole(*rim), whole(*rim)],
        out_shape=[
            jax.ShapeDtypeStruct(fields, f32),
            jax.ShapeDtypeStruct(fields, f32),
            jax.ShapeDtypeStruct((5 * rows, cols), f32),
            jax.ShapeDtypeStruct(rim, f32),
            jax.ShapeDtypeStruct(rim, f32),
        ],
        compiler_params=limit,
        name="middle",
    )(index, conductance, nodata, ground_mask, ground_value, pre, above, below, tile_inverse)
    above, below = neighbours(up, down)

    last, sums = pl.pallas_call(
        functools.partial(sums_kernel, **sizes),
        grid=(1,),
        in_specs=[smem(), *[whole(*fields)] * 4, whole(*rim), whole(*rim), whole(5 * rows, cols)],
        out_specs=[whole(*fields), whole(2, 2 * pairs)],
        out_shape=[jax.ShapeDtypeStruct(fields, f32), jax.ShapeDtypeStruct((2, 2 * pairs), f32)],
        scratch_shapes=[pltpu.VMEM((2 * pairs, TILE), f32), pltpu.VMEM((2 * pairs, TILE), f32)],
        compiler_params=limit,
        name="sums",
    )(index, field, pre, image, second, above, below, weights)
    copies = jnp.broadcast_to(sums, (devices, *sums.shape))
    everyone = lax.all_to_all(copies, "space", split_axis=0, concat_axis=0, tiled=True)

    block = 8
    out = jax.ShapeDtypeStruct((pairs, rows, cols), f32)
    out_block = pl.BlockSpec((block, rows, cols), lambda p: (p, 0, 0))
    return pl.pallas_call(
        functools.partial(finish_kernel, rows=rows, cols=cols, pairs=pairs, block=block),
        grid=(pairs // block,),
        in_specs=[smem(), whole(devices, 2, 2 * pairs), *[whole(*fields)] * 5],
        out_specs=[out_block, out_block],
        out_shape=[out, out],
        scratch_shapes=[pltpu.VMEM((pairs, TILE), f32), pltpu.VMEM((pairs, TILE), f32)],
        compiler_params=limit,
        name="finish",
    )(index, everyone, field, pre, image, second, last)


def solution(mesh):
    cells = P(("groups", "space"), None)
    return jax.shard_map(
        on_device,
        mesh=mesh,
        in_specs=(*[cells] * 6, P(("groups", "space"), None, None, None), P(("groups", "rhs"), None)),
        out_specs=(P("rhs", ("groups", "space"), None), P("rhs", ("groups", "space"), None)),
        check_vma=False,
    )
```

time: 185 us -> 133 us (0.72)
  starting transfers between devices: 61.7 us -> 12 us
  blocking collectives: 27.9 us -> 63.5 us
  Pallas kernels: 0 us -> 28.2 us
  other arithmetic: 27.3 us -> 0 us
  matrix products: 18.6 us -> 0 us
  waiting for transfers between devices: 37.1 us -> 21.6 us
  local copies, waits for them, and re-layouts: 11 us -> 6.14 us
    all_to_all x1 -> x0, starting transfers between devices: 44.9 us -> none  [from_everyone(): return lax.all_to_all(copies, axis, split_axis=0, concat_axis=0, tiled=True)]
    all_to_all x1, blocking collectives: 27.9 us -> 63.5 us  [on_device(): lax.all_to_all(copies, 'space', split_axis=0, concat_axis=0, tiled=True)]
    pallas_call x0 -> x4, Pallas kernels: none -> 28.2 us  [the longest x1 11.8 us: on_device(): pl.pallas_call(functools.partial(start_kernel, **sizes), grid=(rows,), in...]
    all_to_all x1 -> x0, waiting for transfers between devices: 21.5 us -> none  [from_everyone(): return lax.all_to_all(copies, axis, split_axis=0, concat_axis=0, tiled=True)]
    dot_general x2 -> x0, matrix products: 18.6 us -> none  [precondition(): jnp.einsum('rcij,prcj->prci', tile_inverse, blocks, precision=lax.Precisi...]
    concatenate x5 -> x0, other arithmetic: 7 us -> none  [the longest x3 6.85 us: with_halo(): jnp.concatenate([lax.ppermute(tail, axis, [(i, (i + 1) % count) for i in...]
    reduce_sum x4 -> x0, other arithmetic: 6.46 us -> none  [the longest x2 6.42 us: inner_sum(): return jnp.sum(first * second, axis=(1, 2))]
    ppermute x6 -> x4, waiting for transfers between devices: 15.6 us -> 21.6 us  [the longest x2 12 us: neighbours(): lax.ppermute(up, 'space', [((i + 1) % count, i) for i in range(ends)])]
  transfers between devices with their start and end apart: 7 -> 4, of which waited for: 5 -> 4; matrix products, arithmetic and copies ran while one was open for 9% -> 0% of each run, Pallas kernels for 0% -> 0%
where the time goes in v1:
time: 133 us; the launch traced here: 132 us
  blocking collectives  63.5 us (48%)
  Pallas kernels  28.2 us (21%)
  waiting for transfers between devices  21.6 us (16%)
  starting transfers between devices  12 us (9%)
  local copies, waits for them, and re-layouts  6.14 us (5%)
    all_to_all x1, blocking collectives, on_device(): lax.all_to_all(copies, 'space', split_axis=0, concat_axis=0, tiled=True)  63.5 us
    ppermute x2, waiting for transfers between devices, neighbours(): lax.ppermute(up, 'space', [((i + 1) % count, i) for i in range(ends)])  12 us
    pallas_call x1, Pallas kernels, on_device(): pl.pallas_call(functools.partial(start_kernel, **sizes), grid=(rows,), in...  11.8 us
    pallas_call x1, Pallas kernels, on_device(): pl.pallas_call(functools.partial(middle_kernel, **sizes), grid=(rows,), i...  10.2 us
    ppermute x2, waiting for transfers between devices, neighbours(): lax.ppermute(down, 'space', [(i, (i + 1) % count) for i in range(ends)])  9.61 us
    ppermute x2, starting transfers between devices, neighbours(): lax.ppermute(down, 'space', [(i, (i + 1) % count) for i in range(ends)])  9.37 us
    unnamed x15, local copies, waits for them, and re-layouts  6 us
    pallas_call x1, Pallas kernels, on_device(): pl.pallas_call(functools.partial(finish_kernel, rows=rows, cols=cols, pai...  5.08 us
  transfers between devices with their start and end apart: 4, of which 4 were waited for; matrix products, arithmetic and copies ran while one was open for 0% of the time, Pallas kernels for 0%

profile of v1, /device:TPU:40, one launch (start us, length us, event | category | flops | bytes accessed | tf_op | source)
XLA Modules:
  0.0 132.1 jit_solution(896171954079662664)
XLA Ops:
  0.6 0.0 copy-start.6
  0.6 0.0 copy-start.5
  0.7 0.8 copy.11
  1.4 0.1 reshape.11.focal
  1.6 0.0 copy-start
  1.6 2.2 %copy-done = f32[8,8,128,128]{3,2,1,0:T(8,128)S(1)} copy-done((f32[8,8,128,128]{3,2,1,0:T(8,128)S(1)}, f32[8,8,128,128]{3,2,1,0:T(8,128)}, u32[]{:S(2)}) %copy-start) | copy-done | bytes 4194328
  3.8 0.0 copy-start.1
  3.8 0.8 copy-done.1
  4.5 0.0 copy-start.2
  4.5 0.8 copy-done.2
  5.3 0.0 copy-start.3
  5.3 0.8 copy-done.3
  6.0 0.0 copy-start.4
  6.0 0.8 copy-done.4
  6.8 11.8 %start.1 = (f32[8,640,128]{2,1,0:T(8,128)S(1)}, f32[8,640,128]{2,1,0:T(8,128)S(1)}, s32[152]{0:T(256)S(1)}, f32[72,1024]{1,0:T(8,128)S(1)}, f32[72,1024]{1,0:T(8,128)S(1)}) custom-call(s32[1]{0:T(128)} %bitcast.where, s32[128]{0:T(128)S(1)} %reshape.11.focal, s32[8,1024]{1,0:T(8,128)S(1)} %copy-done.3, f32[8,1024]{1,0:T(8,128)S(1)} %copy-done.4, ...), custom_call_target="tpu_custom_call" | custom-call | tf_op jit(solution)/shard_map/start/pallas_call | solution.py:303
  18.6 4.8 %collective-permute-start = (f32[72,1024]{1,0:T(8,128)S(1)}, f32[72,1024]{1,0:T(8,128)S(1)}, u32[]{:S(2)}, u32[]{:S(2)}) collective-permute-start(f32[72,1024]{1,0:T(8,128)S(1)} %get-tuple-element.17), channel_id=1, source_target_pairs={{0,8},{8,16},{16,24},{24,32},{32,40},{40,48},{48,56},{56,64},{64,7... | collective-permute-start | bytes 884744 | tf_op jit(solution)/shard_map/ppermute | solution.py:286
  23.4 1.3 collective-permute-start.1
  24.7 5.2 %collective-permute-done.above = f32[72,1024]{1,0:T(8,128)S(1)} collective-permute-done((f32[72,1024]{1,0:T(8,128)S(1)}, f32[72,1024]{1,0:T(8,128)S(1)}, u32[]{:S(2)}, u32[]{:S(2)}) %collective-permute-start) | collective-permute-done | bytes 294944 | tf_op jit(solution)/shard_map/ppermute | solution.py:286
  29.9 5.1 %collective-permute-done.1.below = f32[72,1024]{1,0:T(8,128)S(1)} collective-permute-done((f32[72,1024]{1,0:T(8,128)S(1)}, f32[72,1024]{1,0:T(8,128)S(1)}, u32[]{:S(2)}, u32[]{:S(2)}) %collective-permute-start.1) | collective-permute-done | bytes 294944 | tf_op jit(solution)/shard_map/ppermute | solution.py:287
  35.0 0.0 copy-done.6
  35.0 0.0 copy-done.5
  35.0 10.2 %middle.1 = (f32[8,640,128]{2,1,0:T(8,128)S(1)}, f32[8,640,128]{2,1,0:T(8,128)S(1)}, f32[40,1024]{1,0:T(8,128)S(1)}, f32[72,1024]{1,0:T(8,128)S(1)}, f32[72,1024]{1,0:T(8,128)S(1)}) custom-call(s32[152]{0:T(256)S(1)} %get-tuple-element.14.index, f32[8,1024]{1,0:T(8,128)S(1)} %copy-done.1, s32[8,1024]{1,0:T(8,128)S(1)} %copy-done.2, s32[8,1024]{1,0:T(8,128)S(1)} %copy-done.5, ...), custom_call_target="tpu_custom_call" | custom-call | tf_op jit(solution)/shard_map/middle/pallas_call | solution.py:320
  45.2 4.6 %collective-permute-start.2 = (f32[72,1024]{1,0:T(8,128)S(1)}, f32[72,1024]{1,0:T(8,128)S(1)}, u32[]{:S(2)}, u32[]{:S(2)}) collective-permute-start(f32[72,1024]{1,0:T(8,128)S(1)} %get-tuple-element.21), channel_id=1, source_target_pairs={{0,8},{8,16},{16,24},{24,32},{32,40},{40,48},{48,56},{56,64},{64,7... | collective-permute-start | bytes 884744 | tf_op jit(solution)/shard_map/ppermute | solution.py:286
  49.8 1.3 collective-permute-start.3
  51.1 4.4 %collective-permute-done.2.above = f32[72,1024]{1,0:T(8,128)S(1)} collective-permute-done((f32[72,1024]{1,0:T(8,128)S(1)}, f32[72,1024]{1,0:T(8,128)S(1)}, u32[]{:S(2)}, u32[]{:S(2)}) %collective-permute-start.2) | collective-permute-done | bytes 294944 | tf_op jit(solution)/shard_map/ppermute | solution.py:286
  55.5 6.8 %collective-permute-done.3.below = f32[72,1024]{1,0:T(8,128)S(1)} collective-permute-done((f32[72,1024]{1,0:T(8,128)S(1)}, f32[72,1024]{1,0:T(8,128)S(1)}, u32[]{:S(2)}, u32[]{:S(2)}) %collective-permute-start.3) | collective-permute-done | bytes 294944 | tf_op jit(solution)/shard_map/ppermute | solution.py:287
  62.4 1.2 sums.1
  63.6 63.5 %all_to_all.5.everyone = f32[32,2,128]{2,1,0:T(2,128)S(1)} all-to-all(f32[32,2,128]{2,1,0:T(2,128)S(1)} %broadcast_in_dim.3), channel_id=1, replica_groups=mesh['groups'=2,'space'=32,'rhs'=8] {'space'}, dimensions={0} | all-to-all | bytes 65536 | tf_op jit(solution)/shard_map/all_to_all | solution.py:348
  127.1 5.1 %finish.1 = (f32[64,8,1024]{2,1,0:T(8,128)}, f32[64,8,1024]{2,1,0:T(8,128)}) custom-call(s32[152]{0:T(256)S(1)} %get-tuple-element.14.index, f32[32,2,128]{2,1,0:T(2,128)S(1)} %all_to_all.5.everyone, f32[8,640,128]{2,1,0:T(8,128)S(1)} %get-tuple-element.15.field, f32[8,640,128]{2,1,0:T(8,128)S(1)} %get-tuple-element.16.pre, ...), custom_call_target="tpu_custom_call" | custom-call | tf_op jit(solution)/shard_map/finish/pallas_call | solution.py:353
  (1 shorter events, 0.0 us)
Async XLA Ops:
  0.6 34.4 %copy-start.6 = (f32[8,1024]{1,0:T(8,128)S(1)}, f32[8,1024]{1,0:T(8,128)}, u32[]{:S(2)}) copy-start(f32[8,1024]{1,0:T(8,128)} %ground_value.1) | copy-start | bytes 98308
  0.6 34.4 %copy-start.5 = (s32[8,1024]{1,0:T(8,128)S(1)}, s32[8,1024]{1,0:T(8,128)}, u32[]{:S(2)}) copy-start(s32[8,1024]{1,0:T(8,128)} %ground_mask.1) | copy-start | bytes 98308
  1.6 2.2 %copy-start = (f32[8,8,128,128]{3,2,1,0:T(8,128)S(1)}, f32[8,8,128,128]{3,2,1,0:T(8,128)}, u32[]{:S(2)}) copy-start(f32[8,8,128,128]{3,2,1,0:T(8,128)} %tiles.3) | copy-start | bytes 12582916
  3.8 0.8 copy-start.1
  4.5 0.8 copy-start.2
  5.3 0.8 copy-start.3
  6.0 0.8 copy-start.4
  18.6 11.3 %collective-permute-start = (f32[72,1024]{1,0:T(8,128)S(1)}, f32[72,1024]{1,0:T(8,128)S(1)}, u32[]{:S(2)}, u32[]{:S(2)}) collective-permute-start(f32[72,1024]{1,0:T(8,128)S(1)} %get-tuple-element.17), channel_id=1, source_target_pairs={{0,8},{8,16},{16,24},{24,32},{32,40},{40,48},{48,56},{56,64},{64,7... | collective-permute-start | bytes 884744 | tf_op jit(solution)/shard_map/ppermute | solution.py:286
  23.4 11.6 %collective-permute-start.1 = (f32[72,1024]{1,0:T(8,128)S(1)}, f32[72,1024]{1,0:T(8,128)S(1)}, u32[]{:S(2)}, u32[]{:S(2)}) collective-permute-start(f32[72,1024]{1,0:T(8,128)S(1)} %get-tuple-element.18), channel_id=1, source_target_pairs={{8,0},{16,8},{24,16},{32,24},{40,32},{48,40},{56,48},{64,56},{72,6... | collective-permute-start | bytes 884744 | tf_op jit(solution)/shard_map/ppermute | solution.py:287
  45.2 10.3 %collective-permute-start.2 = (f32[72,1024]{1,0:T(8,128)S(1)}, f32[72,1024]{1,0:T(8,128)S(1)}, u32[]{:S(2)}, u32[]{:S(2)}) collective-permute-start(f32[72,1024]{1,0:T(8,128)S(1)} %get-tuple-element.21), channel_id=1, source_target_pairs={{0,8},{8,16},{16,24},{24,32},{32,40},{40,48},{48,56},{56,64},{64,7... | collective-permute-start | bytes 884744 | tf_op jit(solution)/shard_map/ppermute | solution.py:286
  49.8 12.6 %collective-permute-start.3 = (f32[72,1024]{1,0:T(8,128)S(1)}, f32[72,1024]{1,0:T(8,128)S(1)}, u32[]{:S(2)}, u32[]{:S(2)}) collective-permute-start(f32[72,1024]{1,0:T(8,128)S(1)} %get-tuple-element.22), channel_id=1, source_target_pairs={{8,0},{16,8},{24,16},{32,24},{40,32},{48,40},{56,48},{64,56},{72,6... | collective-permute-start | bytes 884744 | tf_op jit(solution)/shard_map/ppermute | solution.py:287

commit v2 on v1

v2 whole, which is shorter than its diff:
```python
import functools

import jax
import jax.numpy as jnp
from jax import lax
from jax.experimental import pallas as pl
from jax.experimental.pallas import tpu as pltpu
from jax.sharding import PartitionSpec as P

LEAKAGE = 0.05
FOCAL_CURRENT = 16.0
TILE = 128
CHUNK = 16
MIB = 1024 * 1024


def cut(x):
    high = x.astype(jnp.bfloat16)
    return high, (x - high.astype(jnp.float32)).astype(jnp.bfloat16)


def load(field, at):
    return jnp.concatenate([field[t, at, :] for t in range(field.shape[0])], axis=1)


def store(field, at, x):
    for t in range(field.shape[0]):
        field[t, at, :] = x[:, t * TILE : (t + 1) * TILE]


def times_tile(x, pair):
    x_high, x_low = cut(x)
    y = jnp.dot(jnp.concatenate([x_high, x_low], axis=0), pair, preferred_element_type=jnp.float32)
    n = x.shape[0]
    return (y[:n, :TILE] + y[n:, TILE:]) + (y[n:, :TILE] + y[:n, TILE:])


def apply_tiles(src, dst, parts, rows, chunks, first):
    def one(i, _):
        c = lax.div(i, rows)
        r = i - c * rows
        at = pl.ds(c * (CHUNK * rows) + r, CHUNK, stride=rows)
        for t in range(src.shape[0]):
            dst.at[t][at, :] = times_tile(src.at[t][at, :], parts[r, t])
        return 0

    lax.fori_loop(first * rows, chunks * rows, one, 0)


def shifted(x, above, below, rows, cols):
    row = lax.broadcasted_iota(jnp.int32, (rows, cols), 0)
    up = jnp.where(row == 0, above, pltpu.roll(x, 1, 0))
    down = jnp.where(row == rows - 1, below, pltpu.roll(x, rows - 1, 0))
    return up, down, pltpu.roll(x, 1, 1), pltpu.roll(x, cols - 1, 1)


def operator(x, above, below, weights, rows, cols):
    up, down, left, right = shifted(x, above, below, rows, cols)
    diag, north, south, west, east = weights
    return diag * x - north * up - south * down - west * left - east * right


def fill_rims(field, index, up_ref, down_ref, rows, pairs, count):
    cols = up_ref.shape[1]
    first, last = load(field, slice(0, 1)), load(field, slice(rows - 1, rows))
    up_ref[0 : pairs + 8, :] = jnp.broadcast_to(first, (pairs + 8, cols))
    down_ref[0 : pairs + 8, :] = jnp.broadcast_to(last, (pairs + 8, cols))

    def one(s, _):
        k = index[pairs + s]
        up_ref[pl.ds(k, 1), :] = load(field, pl.ds(s * rows, 1))
        down_ref[pl.ds(k, 1), :] = load(field, pl.ds(s * rows + rows - 1, 1))
        return 0

    lax.fori_loop(1, count, one, 0)


def start_kernel(
    where,
    focal_hbm,
    mask_hbm,
    current_hbm,
    cond_hbm,
    nodata_hbm,
    ground_mask_hbm,
    ground_value_hbm,
    tiles_hbm,
    field,
    pre,
    index,
    parts,
    cells,
    up_ref,
    down_ref,
    focal,
    mask,
    current,
    cond,
    nodata,
    ground_mask,
    ground_value,
    tiles,
    focal_sem,
    small_sems,
    tile_sems,
    *,
    rows,
    cols,
    pairs,
    slots,
):
    cells_of_pairs = pltpu.make_async_copy(focal_hbm, focal, focal_sem)
    cells_of_pairs.start()
    arrivals = [
        pltpu.make_async_copy(src, dst, small_sems.at[n])
        for n, (src, dst) in enumerate(
            [
                (mask_hbm, mask),
                (current_hbm, current),
                (cond_hbm, cond),
                (nodata_hbm, nodata),
                (ground_mask_hbm, ground_mask),
                (ground_value_hbm, ground_value),
            ]
        )
    ]
    for copy in arrivals:
        copy.start()
    for r in range(rows):
        pltpu.make_async_copy(tiles_hbm.at[r], tiles.at[r], tile_sems.at[r]).start()

    base_row = where[0]
    index[pairs] = pairs
    cells_of_pairs.wait()

    def listed(k, s):
        a = lax.div(focal[0, k], cols) - base_row
        b = lax.div(focal[1, k], cols) - base_row
        near = ((a >= -2) & (a < rows + 2)) | ((b >= -2) & (b < rows + 2))
        index[k] = jnp.where(near, s, 0)

        @pl.when(near)
        def _():
            index[pairs + s] = k

        return s + near.astype(jnp.int32)

    count = lax.fori_loop(0, pairs, listed, jnp.int32(1))
    index[pairs + slots] = count
    chunks = (count + CHUNK - 1) // CHUNK

    for copy in arrivals:
        copy.wait()
    background = mask[...].astype(jnp.float32) * current[...]
    store(field, slice(0, rows), background)
    lane = lax.broadcasted_iota(jnp.int32, (1, TILE), 1)

    def one(s, _):
        k = index[pairs + s]
        store(field, pl.ds(s * rows, rows), background)
        for end in range(2):
            cell = focal[end, k]
            i = lax.div(cell, cols)
            j = cell - i * cols
            i = i - base_row

            @pl.when((i >= 0) & (i < rows))
            def _():
                t = lax.div(j, TILE)
                at = pl.ds(s * rows + i, 1)
                sign = FOCAL_CURRENT * (1 - 2 * end)
                field[t, at, :] = field[t, at, :] + jnp.where(lane == j - t * TILE, sign, 0.0)

        return 0

    lax.fori_loop(1, count, one, 0)

    valid = (1 - nodata[...]).astype(jnp.float32)
    active = cond[...] * valid
    cells[0:rows, :] = active
    cells[rows : 2 * rows, :] = valid
    cells[2 * rows : 3 * rows, :] = ground_mask[...].astype(jnp.float32) * ground_value[...]

    def row(r, _):
        pltpu.make_async_copy(tiles_hbm.at[r], tiles.at[r], tile_sems.at[r]).wait()
        at = pl.ds(r, CHUNK, stride=rows)
        for t in range(cols // TILE):
            pair = jnp.concatenate(cut(tiles[r, t]), axis=1)
            parts[r, t] = pair
            pre.at[t][at, :] = times_tile(field.at[t][at, :], pair)
        return 0

    lax.fori_loop(0, rows, row, 0)
    apply_tiles(field, pre, parts, rows, chunks, 1)

    fill_rims(pre, index, up_ref, down_ref, rows, pairs, count)
    up_ref[pairs + 1 : pairs + 2, :] = active[0:1, :]
    up_ref[pairs + 2 : pairs + 3, :] = valid[0:1, :]
    down_ref[pairs + 1 : pairs + 2, :] = active[rows - 1 : rows, :]
    down_ref[pairs + 2 : pairs + 3, :] = valid[rows - 1 : rows, :]


def middle_kernel(
    index, cells, pre, parts, above, below, image, second, weights, up_ref, down_ref, *, rows, cols, pairs, slots
):
    count = index[pairs + slots]
    active, valid, grounded = (cells[n * rows : (n + 1) * rows, :] for n in range(3))
    lane = lax.broadcasted_iota(jnp.int32, (rows, cols), 1)
    g = shifted(active, above[pairs + 1 : pairs + 2, :], below[pairs + 1 : pairs + 2, :], rows, cols)
    v = shifted(valid, above[pairs + 2 : pairs + 3, :], below[pairs + 2 : pairs + 3, :], rows, cols)
    inside = (None, None, lane > 0, lane < cols - 1)
    edges = []
    for n in range(4):
        edge = 0.5 * (active + g[n]) * valid * v[n]
        if inside[n] is not None:
            edge = jnp.where(inside[n], edge, 0.0)
        edges.append(edge)
    diag = valid * (LEAKAGE + grounded) + (1.0 - valid) + edges[0] + edges[1] + edges[2] + edges[3]
    for n, x in enumerate([diag, *edges]):
        weights[n * rows : (n + 1) * rows, :] = x

    def one(s, _):
        k = index[pairs + s]
        at = pl.ds(s * rows, rows)
        w = [weights[n * rows : (n + 1) * rows, :] for n in range(5)]
        store(image, at, operator(load(pre, at), above[pl.ds(k, 1), :], below[pl.ds(k, 1), :], w, rows, cols))
        return 0

    lax.fori_loop(0, count, one, 0)
    apply_tiles(image, second, parts, rows, (count + CHUNK - 1) // CHUNK, 0)
    fill_rims(second, index, up_ref, down_ref, rows, pairs, count)


def sums_kernel(
    index, field, pre, image, second, above, below, weights, last, sums, one_two, three_four, *, rows, cols, pairs, slots
):
    count = index[pairs + slots]

    def folded(x):
        acc = x[:, 0:TILE]
        for t in range(1, cols // TILE):
            acc = acc + x[:, t * TILE : (t + 1) * TILE]
        return jnp.sum(acc, axis=0, keepdims=True)

    def four(s):
        k = index[pairs + s]
        at = pl.ds(s * rows, rows)
        w = [weights[n * rows : (n + 1) * rows, :] for n in range(5)]
        u = load(second, at)
        v = operator(u, above[pl.ds(k, 1), :], below[pl.ds(k, 1), :], w, rows, cols)
        store(last, at, v)
        z, i = load(pre, at), load(image, at)
        return k, folded(load(field, at) * z), folded(z * i), folded(i * u), folded(u * v)

    _, a, b, c, d = four(0)
    one_two[0:pairs, :] = jnp.broadcast_to(a, (pairs, TILE))
    one_two[pairs : 2 * pairs, :] = jnp.broadcast_to(b, (pairs, TILE))
    three_four[0:pairs, :] = jnp.broadcast_to(c, (pairs, TILE))
    three_four[pairs : 2 * pairs, :] = jnp.broadcast_to(d, (pairs, TILE))

    def one(s, _):
        k, a, b, c, d = four(s)
        one_two[pl.ds(k, 1), :] = a
        one_two[pl.ds(pairs + k, 1), :] = b
        three_four[pl.ds(k, 1), :] = c
        three_four[pl.ds(pairs + k, 1), :] = d
        return 0

    lax.fori_loop(1, count, one, 0)
    sums[0:1, :] = jnp.sum(one_two[...].T, axis=0, keepdims=True)
    sums[1:2, :] = jnp.sum(three_four[...].T, axis=0, keepdims=True)


def finish_kernel(
    index, everyone, field, pre, image, second, last, solution, residual, first_c, second_c, *, rows, cols, pairs, block
):
    step = pl.program_id(0)

    @pl.when(step == 0)
    def _():
        total = jnp.sum(everyone[...], axis=0)
        ab, cd = total[0:1, :], total[1:2, :]
        gamma, delta = ab[:, :pairs], ab[:, pairs:]
        eta, theta = cd[:, :pairs], cd[:, pairs:]
        alpha = gamma / delta
        gamma_next = alpha * alpha * eta - gamma
        beta = 1.0 + gamma_next / gamma
        curvature = beta * beta * delta - 2.0 * beta * alpha * eta + alpha * alpha * theta
        step_next = gamma_next / curvature
        both = jnp.concatenate([alpha + step_next * beta, alpha * step_next], axis=1)
        spread = jnp.broadcast_to(both, (2 * pairs, 2 * pairs)).T
        first_c[...] = spread[:pairs, :]
        second_c[...] = spread[pairs:, :]

    def one(p, _):
        k = step * block + p
        s = index[k]
        at = pl.ds(s * rows, rows)
        a = jnp.broadcast_to(first_c[pl.ds(k, 1), :], (rows, TILE))
        b = jnp.broadcast_to(second_c[pl.ds(k, 1), :], (rows, TILE))
        for t in range(cols // TILE):
            lanes = slice(t * TILE, (t + 1) * TILE)
            solution[p, :, lanes] = a * pre[t, at, :] - b * second[t, at, :]
            residual[p, :, lanes] = field[t, at, :] - a * image[t, at, :] + b * last[t, at, :]
        return 0

    lax.fori_loop(0, block, one, 0, unroll=4)


def smem():
    return pl.BlockSpec(memory_space=pltpu.SMEM)


def vmem():
    return pl.BlockSpec(memory_space=pltpu.VMEM)


def hbm():
    return pl.BlockSpec(memory_space=pltpu.HBM)


def neighbours(up, down):
    count = lax.axis_size("space")
    ends = count - 1
    above = lax.ppermute(down, "space", [(i, (i + 1) % count) for i in range(ends)])
    below = lax.ppermute(up, "space", [((i + 1) % count, i) for i in range(ends)])
    return above, below


def on_device(conductance, nodata, ground_mask, ground_value, source_mask, source_current, tile_inverse, focal_cells):
    rows, cols = conductance.shape
    pairs = focal_cells.shape[0]
    slots = -(-(pairs + 1) // CHUNK) * CHUNK
    devices = lax.axis_size("space")
    f32 = jnp.float32
    sizes = dict(rows=rows, cols=cols, pairs=pairs, slots=slots)
    strip, fields, rim = (rows, cols), (cols // TILE, slots * rows, TILE), (pairs + 8, cols)
    per_row = tile_inverse.shape[1:]
    limit = pltpu.CompilerParams(vmem_limit_bytes=24 * MIB)
    base_row = (lax.axis_index("space") * rows).astype(jnp.int32).reshape(1)

    def shaped(shape, dtype=f32):
        return jax.ShapeDtypeStruct(shape, dtype)

    field, pre, index, parts, cells, up, down = pl.pallas_call(
        functools.partial(start_kernel, **sizes),
        in_specs=[smem(), *[hbm()] * 8],
        out_specs=[vmem(), vmem(), smem(), *[vmem()] * 4],
        out_shape=[
            shaped(fields),
            shaped(fields),
            shaped((pairs + slots + 8,), jnp.int32),
            shaped((rows, *per_row[:2], 2 * TILE), jnp.bfloat16),
            shaped((3 * rows, cols)),
            shaped(rim),
            shaped(rim),
        ],
        scratch_shapes=[
            pltpu.SMEM(focal_cells.shape[::-1], jnp.int32),
            pltpu.VMEM(strip, jnp.int32),
            pltpu.VMEM(strip, f32),
            pltpu.VMEM(strip, f32),
            pltpu.VMEM(strip, jnp.int32),
            pltpu.VMEM(strip, jnp.int32),
            pltpu.VMEM(strip, f32),
            pltpu.VMEM((rows, *per_row), f32),
            pltpu.SemaphoreType.DMA,
            pltpu.SemaphoreType.DMA((6,)),
            pltpu.SemaphoreType.DMA((rows,)),
        ],
        compiler_params=limit,
        name="start",
    )(
        base_row,
        *(
            pltpu.with_memory_space_constraint(x, pltpu.HBM)
            for x in (
                focal_cells.T,
                source_mask,
                source_current,
                conductance,
                nodata,
                ground_mask,
                ground_value,
                tile_inverse,
            )
        ),
    )
    above, below = neighbours(up, down)

    image, second, weights, up, down = pl.pallas_call(
        functools.partial(middle_kernel, **sizes),
        in_specs=[smem(), *[vmem()] * 5],
        out_specs=[vmem()] * 5,
        out_shape=[shaped(fields), shaped(fields), shaped((5 * rows, cols)), shaped(rim), shaped(rim)],
        compiler_params=limit,
        name="middle",
    )(index, cells, pre, parts, above, below)
    above, below = neighbours(up, down)

    last, sums = pl.pallas_call(
        functools.partial(sums_kernel, **sizes),
        in_specs=[smem(), *[vmem()] * 7],
        out_specs=[vmem()] * 2,
        out_shape=[shaped(fields), shaped((2, 2 * pairs))],
        scratch_shapes=[pltpu.VMEM((2 * pairs, TILE), f32), pltpu.VMEM((2 * pairs, TILE), f32)],
        compiler_params=limit,
        name="sums",
    )(index, field, pre, image, second, above, below, weights)
    copies = jnp.broadcast_to(sums, (devices, *sums.shape))
    everyone = lax.all_to_all(copies, "space", split_axis=0, concat_axis=0, tiled=True)

    block = 8
    out = jax.ShapeDtypeStruct((pairs, rows, cols), f32)
    out_block = pl.BlockSpec((block, rows, cols), lambda p: (p, 0, 0))
    return pl.pallas_call(
        functools.partial(finish_kernel, rows=rows, cols=cols, pairs=pairs, block=block),
        grid=(pairs // block,),
        in_specs=[smem(), *[vmem()] * 6],
        out_specs=[out_block, out_block],
        out_shape=[out, out],
        scratch_shapes=[pltpu.VMEM((pairs, TILE), f32), pltpu.VMEM((pairs, TILE), f32)],
        compiler_params=limit,
        name="finish",
    )(index, everyone, field, pre, image, second, last)


def solution(mesh):
    cells = P(("groups", "space"), None)
    return jax.shard_map(
        on_device,
        mesh=mesh,
        in_specs=(*[cells] * 6, P(("groups", "space"), None, None, None), P(("groups", "rhs"), None)),
        out_specs=(P("rhs", ("groups", "space"), None), P("rhs", ("groups", "space"), None)),
        check_vma=False,
    )
```

time: 133 us -> 113 us (0.85)
  Pallas kernels: 28.2 us -> 14.6 us
  local copies, waits for them, and re-layouts: 6.14 us -> 0.01 us
  waiting for transfers between devices: 21.6 us -> 19.9 us
    pallas_call x3, Pallas kernels: 23.1 us -> 9.58 us  [the longest x1 5.11 us: on_device(): pl.pallas_call(functools.partial(start_kernel, **sizes), in_specs=[smem()...]
    unnamed x15 -> x0, local copies, waits for them, and re-layouts: 6 us -> none
where the time goes in v2:
time: 113 us; the launch traced here: 112 us
  blocking collectives  64.5 us (57%)
  waiting for transfers between devices  19.9 us (18%)
  Pallas kernels  14.6 us (13%)
  starting transfers between devices  12.6 us (11%)
    all_to_all x1, blocking collectives, on_device(): lax.all_to_all(copies, 'space', split_axis=0, concat_axis=0, tiled=True)  64.5 us
    ppermute x2, waiting for transfers between devices, neighbours(): lax.ppermute(up, 'space', [((i + 1) % count, i) for i in range(ends)])  11.5 us
    ppermute x2, starting transfers between devices, neighbours(): lax.ppermute(down, 'space', [(i, (i + 1) % count) for i in range(ends)])  9.99 us
    ppermute x2, waiting for transfers between devices, neighbours(): lax.ppermute(down, 'space', [(i, (i + 1) % count) for i in range(ends)])  8.41 us
    pallas_call x1, Pallas kernels, on_device(): pl.pallas_call(functools.partial(start_kernel, **sizes), in_specs=[smem()...  5.11 us
    pallas_call x1, Pallas kernels, on_device(): pl.pallas_call(functools.partial(finish_kernel, rows=rows, cols=cols, pai...  5.01 us
    pallas_call x1, Pallas kernels, on_device(): pl.pallas_call(functools.partial(middle_kernel, **sizes), in_specs=[smem(...  3.1 us
    ppermute x2, starting transfers between devices, neighbours(): lax.ppermute(up, 'space', [((i + 1) % count, i) for i in range(ends)])  2.62 us
  transfers between devices with their start and end apart: 4, of which 4 were waited for; matrix products, arithmetic and copies ran while one was open for 0% of the time, Pallas kernels for 0%

profile of v2, /device:TPU:40, one launch (start us, length us, event | category | flops | bytes accessed | tf_op | source)
XLA Modules:
  0.0 112.3 jit_solution(15760391583399828887)
XLA Ops:
  0.6 5.1 %start.1 = (f32[8,640,128]{2,1,0:T(8,128)S(1)}, f32[8,640,128]{2,1,0:T(8,128)S(1)}, s32[152]{0:T(256)S(1)}, bf16[8,8,128,256]{3,2,1,0:T(8,128)(2,1)S(1)}, f32[24...) custom-call(s32[1]{0:T(128)} %bitcast.where, s32[2,64]{1,0:T(2,128)} %bitcast.2, ...), custom_call_target="tpu_custom_call" | custom-call | tf_op jit(solution)/shard_map/start/pallas_call | solution.py:345
  5.8 4.9 %collective-permute-start = (f32[72,1024]{1,0:T(8,128)S(1)}, f32[72,1024]{1,0:T(8,128)S(1)}, u32[]{:S(2)}, u32[]{:S(2)}) collective-permute-start(f32[72,1024]{1,0:T(8,128)S(1)} %get-tuple-element.21), channel_id=1, source_target_pairs={{0,8},{8,16},{16,24},{24,32},{32,40},{40,48},{48,56},{56,64},{64,7... | collective-permute-start | bytes 884744 | tf_op jit(solution)/shard_map/ppermute | solution.py:325
  10.6 1.3 %collective-permute-start.1 = (f32[72,1024]{1,0:T(8,128)S(1)}, f32[72,1024]{1,0:T(8,128)S(1)}, u32[]{:S(2)}, u32[]{:S(2)}) collective-permute-start(f32[72,1024]{1,0:T(8,128)S(1)} %get-tuple-element.22), channel_id=1, source_target_pairs={{8,0},{16,8},{24,16},{32,24},{40,32},{48,40},{56,48},{64,56},{72,6... | collective-permute-start | bytes 884744 | tf_op jit(solution)/shard_map/ppermute | solution.py:326
  12.0 4.7 %collective-permute-done.above = f32[72,1024]{1,0:T(8,128)S(1)} collective-permute-done((f32[72,1024]{1,0:T(8,128)S(1)}, f32[72,1024]{1,0:T(8,128)S(1)}, u32[]{:S(2)}, u32[]{:S(2)}) %collective-permute-start) | collective-permute-done | bytes 294944 | tf_op jit(solution)/shard_map/ppermute | solution.py:325
  16.6 5.2 %collective-permute-done.1.below = f32[72,1024]{1,0:T(8,128)S(1)} collective-permute-done((f32[72,1024]{1,0:T(8,128)S(1)}, f32[72,1024]{1,0:T(8,128)S(1)}, u32[]{:S(2)}, u32[]{:S(2)}) %collective-permute-start.1) | collective-permute-done | bytes 294944 | tf_op jit(solution)/shard_map/ppermute | solution.py:326
  21.8 3.1 %middle.1 = (f32[8,640,128]{2,1,0:T(8,128)S(1)}, f32[8,640,128]{2,1,0:T(8,128)S(1)}, f32[40,1024]{1,0:T(8,128)S(1)}, f32[72,1024]{1,0:T(8,128)S(1)}, f32[72,1024]{1,0:T(8,128)S(1)}) custom-call(s32[152]{0:T(256)S(1)} %get-tuple-element.16.index, f32[24,1024]{1,0:T(8,128)S(1)} %get-tuple-element.19.cells, f32[8,640,128]{2,1,0:T(8,128)S(1)} %get-tuple-element.18.pre, ...), custom_call_target="tpu_custom_call" | custom-call | tf_op jit(solution)/shard_map/middle/pallas_call | solution.py:391
  24.9 5.1 %collective-permute-start.2 = (f32[72,1024]{1,0:T(8,128)S(1)}, f32[72,1024]{1,0:T(8,128)S(1)}, u32[]{:S(2)}, u32[]{:S(2)}) collective-permute-start(f32[72,1024]{1,0:T(8,128)S(1)} %get-tuple-element.25), channel_id=1, source_target_pairs={{0,8},{8,16},{16,24},{24,32},{32,40},{40,48},{48,56},{56,64},{64,7... | collective-permute-start | bytes 884744 | tf_op jit(solution)/shard_map/ppermute | solution.py:325
  30.1 1.3 %collective-permute-start.3 = (f32[72,1024]{1,0:T(8,128)S(1)}, f32[72,1024]{1,0:T(8,128)S(1)}, u32[]{:S(2)}, u32[]{:S(2)}) collective-permute-start(f32[72,1024]{1,0:T(8,128)S(1)} %get-tuple-element.26), channel_id=1, source_target_pairs={{8,0},{16,8},{24,16},{32,24},{40,32},{48,40},{56,48},{64,56},{72,6... | collective-permute-start | bytes 884744 | tf_op jit(solution)/shard_map/ppermute | solution.py:326
  31.4 3.7 %collective-permute-done.2.above = f32[72,1024]{1,0:T(8,128)S(1)} collective-permute-done((f32[72,1024]{1,0:T(8,128)S(1)}, f32[72,1024]{1,0:T(8,128)S(1)}, u32[]{:S(2)}, u32[]{:S(2)}) %collective-permute-start.2) | collective-permute-done | bytes 294944 | tf_op jit(solution)/shard_map/ppermute | solution.py:325
  35.1 6.3 %collective-permute-done.3.below = f32[72,1024]{1,0:T(8,128)S(1)} collective-permute-done((f32[72,1024]{1,0:T(8,128)S(1)}, f32[72,1024]{1,0:T(8,128)S(1)}, u32[]{:S(2)}, u32[]{:S(2)}) %collective-permute-start.3) | collective-permute-done | bytes 294944 | tf_op jit(solution)/shard_map/ppermute | solution.py:326
  41.4 1.4 %sums.1 = (f32[8,640,128]{2,1,0:T(8,128)S(1)}, f32[2,128]{1,0:T(2,128)S(1)}) custom-call(s32[152]{0:T(256)S(1)} %get-tuple-element.16.index, f32[8,640,128]{2,1,0:T(8,128)S(1)} %get-tuple-element.17.field, f32[8,640,128]{2,1,0:T(8,128)S(1)} %get-tuple-element.18.pre, f32[8,640,128]{2,1,0:T(8,128)S(1)} %get-tuple-element.23.image, ...), custom_call_target="tpu_custom_call" | custom-call | tf_op jit(solution)/shard_map/sums/pallas_call | solution.py:401
  42.8 64.5 %all_to_all.5.everyone = f32[32,2,128]{2,1,0:T(2,128)S(1)} all-to-all(f32[32,2,128]{2,1,0:T(2,128)S(1)} %broadcast_in_dim.3), channel_id=1, replica_groups=mesh['groups'=2,'space'=32,'rhs'=8] {'space'}, dimensions={0} | all-to-all | bytes 65536 | tf_op jit(solution)/shard_map/all_to_all | solution.py:411
  107.3 5.0 %finish.1 = (f32[64,8,1024]{2,1,0:T(8,128)}, f32[64,8,1024]{2,1,0:T(8,128)}) custom-call(s32[152]{0:T(256)S(1)} %get-tuple-element.16.index, f32[32,2,128]{2,1,0:T(2,128)S(1)} %all_to_all.5.everyone, f32[8,640,128]{2,1,0:T(8,128)S(1)} %get-tuple-element.17.field, f32[8,640,128]{2,1,0:T(8,128)S(1)} %get-tuple-element.18.pre, ...), custom_call_target="tpu_custom_call" | custom-call | tf_op jit(solution)/shard_map/finish/pallas_call | solution.py:416
  (1 shorter events, 0.0 us)
Async XLA Ops:
  5.8 10.9 %collective-permute-start = (f32[72,1024]{1,0:T(8,128)S(1)}, f32[72,1024]{1,0:T(8,128)S(1)}, u32[]{:S(2)}, u32[]{:S(2)}) collective-permute-start(f32[72,1024]{1,0:T(8,128)S(1)} %get-tuple-element.21), channel_id=1, source_target_pairs={{0,8},{8,16},{16,24},{24,32},{32,40},{40,48},{48,56},{56,64},{64,7... | collective-permute-start | bytes 884744 | tf_op jit(solution)/shard_map/ppermute | solution.py:325
  10.6 11.2 %collective-permute-start.1 = (f32[72,1024]{1,0:T(8,128)S(1)}, f32[72,1024]{1,0:T(8,128)S(1)}, u32[]{:S(2)}, u32[]{:S(2)}) collective-permute-start(f32[72,1024]{1,0:T(8,128)S(1)} %get-tuple-element.22), channel_id=1, source_target_pairs={{8,0},{16,8},{24,16},{32,24},{40,32},{48,40},{56,48},{64,56},{72,6... | collective-permute-start | bytes 884744 | tf_op jit(solution)/shard_map/ppermute | solution.py:326
  24.9 10.2 %collective-permute-start.2 = (f32[72,1024]{1,0:T(8,128)S(1)}, f32[72,1024]{1,0:T(8,128)S(1)}, u32[]{:S(2)}, u32[]{:S(2)}) collective-permute-start(f32[72,1024]{1,0:T(8,128)S(1)} %get-tuple-element.25), channel_id=1, source_target_pairs={{0,8},{8,16},{16,24},{24,32},{32,40},{40,48},{48,56},{56,64},{64,7... | collective-permute-start | bytes 884744 | tf_op jit(solution)/shard_map/ppermute | solution.py:325
  30.1 11.4 %collective-permute-start.3 = (f32[72,1024]{1,0:T(8,128)S(1)}, f32[72,1024]{1,0:T(8,128)S(1)}, u32[]{:S(2)}, u32[]{:S(2)}) collective-permute-start(f32[72,1024]{1,0:T(8,128)S(1)} %get-tuple-element.26), channel_id=1, source_target_pairs={{8,0},{16,8},{24,16},{32,24},{40,32},{48,40},{56,48},{64,56},{72,6... | collective-permute-start | bytes 884744 | tf_op jit(solution)/shard_map/ppermute | solution.py:326

commit v3 on v2

--- a/solution.py
+++ b/solution.py
@@ -12,6 +12,8 @@
 TILE = 128
 CHUNK = 16
 MIB = 1024 * 1024
+
+RIM = 8
 
 
 def cut(x):
@@ -47,32 +49,36 @@
     lax.fori_loop(first * rows, chunks * rows, one, 0)
 
 
-def shifted(x, above, below, rows, cols):
-    row = lax.broadcasted_iota(jnp.int32, (rows, cols), 0)
+def beside(x):
+    cols = x.shape[1]
+    return pltpu.roll(x, 1, 1), pltpu.roll(x, cols - 1, 1)
+
+
+def stacked(x, above, below):
+    rows = x.shape[0]
+    row = lax.broadcasted_iota(jnp.int32, x.shape, 0)
     up = jnp.where(row == 0, above, pltpu.roll(x, 1, 0))
     down = jnp.where(row == rows - 1, below, pltpu.roll(x, rows - 1, 0))
-    return up, down, pltpu.roll(x, 1, 1), pltpu.roll(x, cols - 1, 1)
-
-
-def operator(x, above, below, weights, rows, cols):
-    up, down, left, right = shifted(x, above, below, rows, cols)
+    return up, down
+
+
+def operator(x, up, down, weights):
+    left, right = beside(x)
     diag, north, south, west, east = weights
     return diag * x - north * up - south * down - west * left - east * right
 
 
-def fill_rims(field, index, up_ref, down_ref, rows, pairs, count):
-    cols = up_ref.shape[1]
-    first, last = load(field, slice(0, 1)), load(field, slice(rows - 1, rows))
-    up_ref[0 : pairs + 8, :] = jnp.broadcast_to(first, (pairs + 8, cols))
-    down_ref[0 : pairs + 8, :] = jnp.broadcast_to(last, (pairs + 8, cols))
-
-    def one(s, _):
-        k = index[pairs + s]
-        up_ref[pl.ds(k, 1), :] = load(field, pl.ds(s * rows, 1))
-        down_ref[pl.ds(k, 1), :] = load(field, pl.ds(s * rows + rows - 1, 1))
-        return 0
-
-    lax.fori_loop(1, count, one, 0)
+def weights_of(active, valid, grounded, active_beside, valid_beside):
+    cols = active.shape[1]
+    lane = lax.broadcasted_iota(jnp.int32, active.shape, 1)
+    inside = (None, None, lane > 0, lane < cols - 1)
+    edges = []
+    for g, v, keep in zip((*active_beside, *beside(active)), (*valid_beside, *beside(valid)), inside):
+        edge = 0.5 * (active + g) * valid * v
+        edges.append(edge if keep is None else jnp.where(keep, edge, 0.0))
+    north, south, west, east = edges
+    diag = valid * (LEAKAGE + grounded) + (1.0 - valid) + north + south + west + east
+    return diag, north, south, west, east
 
 
 def start_kernel(
@@ -130,23 +136,26 @@
         pltpu.make_async_copy(tiles_hbm.at[r], tiles.at[r], tile_sems.at[r]).start()
 
     base_row = where[0]
-    index[pairs] = pairs
     cells_of_pairs.wait()
 
     def listed(k, s):
-        a = lax.div(focal[0, k], cols) - base_row
-        b = lax.div(focal[1, k], cols) - base_row
+        row = [lax.div(focal[end, k], cols) for end in range(2)]
+        a, b = row[0] - base_row, row[1] - base_row
         near = ((a >= -2) & (a < rows + 2)) | ((b >= -2) & (b < rows + 2))
         index[k] = jnp.where(near, s, 0)
 
         @pl.when(near)
         def _():
             index[pairs + s] = k
+            index[pairs + slots + 2 * s] = a
+            index[pairs + slots + 2 * s + 1] = b
+            index[pairs + 3 * slots + 2 * s] = focal[0, k] - row[0] * cols
+            index[pairs + 3 * slots + 2 * s + 1] = focal[1, k] - row[1] * cols
 
         return s + near.astype(jnp.int32)
 
     count = lax.fori_loop(0, pairs, listed, jnp.int32(1))
-    index[pairs + slots] = count
+    index[pairs + 5 * slots] = count
     chunks = (count + CHUNK - 1) // CHUNK
 
     for copy in arrivals:
@@ -156,13 +165,10 @@
     lane = lax.broadcasted_iota(jnp.int32, (1, TILE), 1)
 
     def one(s, _):
-        k = index[pairs + s]
         store(field, pl.ds(s * rows, rows), background)
         for end in range(2):
-            cell = focal[end, k]
-            i = lax.div(cell, cols)
-            j = cell - i * cols
-            i = i - base_row
+            i = index[pairs + slots + 2 * s + end]
+            j = index[pairs + 3 * slots + 2 * s + end]
 
             @pl.when((i >= 0) & (i < rows))
             def _():
@@ -179,7 +185,8 @@
     active = cond[...] * valid
     cells[0:rows, :] = active
     cells[rows : 2 * rows, :] = valid
-    cells[2 * rows : 3 * rows, :] = ground_mask[...].astype(jnp.float32) * ground_value[...]
+    grounded = ground_mask[...].astype(jnp.float32) * ground_value[...]
+    cells[2 * rows : 3 * rows, :] = grounded
 
     def row(r, _):
         pltpu.make_async_copy(tiles_hbm.at[r], tiles.at[r], tile_sems.at[r]).wait()
@@ -193,48 +200,137 @@
     lax.fori_loop(0, rows, row, 0)
     apply_tiles(field, pre, parts, rows, chunks, 1)
 
-    fill_rims(pre, index, up_ref, down_ref, rows, pairs, count)
-    up_ref[pairs + 1 : pairs + 2, :] = active[0:1, :]
-    up_ref[pairs + 2 : pairs + 3, :] = valid[0:1, :]
-    down_ref[pairs + 1 : pairs + 2, :] = active[rows - 1 : rows, :]
-    down_ref[pairs + 2 : pairs + 3, :] = valid[rows - 1 : rows, :]
+    for rim, first, outermost in ((up_ref, 0, 0), (down_ref, rows - 2, rows - 1)):
+        two = slice(first, first + 2)
+        for t in range(cols // TILE):
+            lanes = slice(t * TILE, (t + 1) * TILE)
+            at = 2 * pairs + t * RIM
+            rim[at : at + 2, :] = pre[t, two, :]
+            rim[at + 2 : at + 4, :] = active[two, lanes]
+            rim[at + 4 : at + 6, :] = valid[two, lanes]
+            rim[at + 6 : at + 7, :] = grounded[outermost : outermost + 1, lanes]
+
+    def selected(s, _):
+        k = index[pairs + s]
+        for end in range(2):
+            i = index[pairs + slots + 2 * s + end]
+            j = index[pairs + 3 * slots + 2 * s + end]
+            t = lax.div(j, TILE)
+            for rim, first in ((up_ref, 0), (down_ref, rows - 2)):
+
+                @pl.when((i >= first) & (i < first + 2))
+                def _():
+                    rim[pl.ds(end * pairs + k, 1), :] = tiles[i, t, pl.ds(j - t * TILE, 1), :]
+
+        return 0
+
+    lax.fori_loop(1, count, selected, 0)
 
 
 def middle_kernel(
-    index, cells, pre, parts, above, below, image, second, weights, up_ref, down_ref, *, rows, cols, pairs, slots
+    index,
+    cells,
+    field,
+    pre,
+    parts,
+    above,
+    below,
+    tiles_above,
+    tiles_below,
+    image,
+    second,
+    last,
+    sums,
+    outer,
+    weights,
+    rim_weights,
+    one_two,
+    three_four,
+    *,
+    rows,
+    cols,
+    pairs,
+    slots,
 ):
-    count = index[pairs + slots]
+    count = index[pairs + 5 * slots]
+    chunks = (count + CHUNK - 1) // CHUNK
     active, valid, grounded = (cells[n * rows : (n + 1) * rows, :] for n in range(3))
-    lane = lax.broadcasted_iota(jnp.int32, (rows, cols), 1)
-    g = shifted(active, above[pairs + 1 : pairs + 2, :], below[pairs + 1 : pairs + 2, :], rows, cols)
-    v = shifted(valid, above[pairs + 2 : pairs + 3, :], below[pairs + 2 : pairs + 3, :], rows, cols)
-    inside = (None, None, lane > 0, lane < cols - 1)
-    edges = []
-    for n in range(4):
-        edge = 0.5 * (active + g[n]) * valid * v[n]
-        if inside[n] is not None:
-            edge = jnp.where(inside[n], edge, 0.0)
-        edges.append(edge)
-    diag = valid * (LEAKAGE + grounded) + (1.0 - valid) + edges[0] + edges[1] + edges[2] + edges[3]
-    for n, x in enumerate([diag, *edges]):
-        weights[n * rows : (n + 1) * rows, :] = x
-
-    def one(s, _):
+
+    def told(rim, n):
+        first = [2 * pairs + t * RIM + n for t in range(cols // TILE)]
+        return jnp.concatenate([rim[i : i + 1, :] for i in first], axis=1)
+
+    def own(x, i):
+        return x[i : i + 1, :]
+
+    def two(x, y):
+        return jnp.concatenate([x, y], axis=0)
+
+    active_a, active_b = (told(above, 2), told(above, 3)), (told(below, 2), told(below, 3))
+    valid_a, valid_b = (told(above, 4), told(above, 5)), (told(below, 4), told(below, 5))
+    all_weights = weights_of(
+        active,
+        valid,
+        grounded,
+        stacked(active, active_a[1], active_b[0]),
+        stacked(valid, valid_a[1], valid_b[0]),
+    )
+    all_rim_weights = weights_of(
+        two(active_a[1], active_b[0]),
+        two(valid_a[1], valid_b[0]),
+        two(told(above, 6), told(below, 6)),
+        (two(active_a[0], own(active, rows - 1)), two(own(active, 0), active_b[1])),
+        (two(valid_a[0], own(valid, rows - 1)), two(own(valid, 0), valid_b[1])),
+    )
+    for n in range(5):
+        weights[n * rows : (n + 1) * rows, :] = all_weights[n]
+        rim_weights[n * 8 : n * 8 + 2, :] = all_rim_weights[n]
+    shared = jnp.concatenate([told(above, 0), told(above, 1), told(below, 0), told(below, 1)], axis=0)
+
+    def first_image(s, _):
+        at = s * RIM
+        z = load(pre, pl.ds(s * rows, rows))
+        z_two = load(outer, pl.ds(at + 1, 2))
+        w = [weights[n * rows : (n + 1) * rows, :] for n in range(5)]
+        store(image, pl.ds(s * rows, rows), operator(z, *stacked(z, own(z_two, 0), own(z_two, 1)), w))
+        w = [rim_weights[n * 8 : n * 8 + 2, :] for n in range(5)]
+        up = two(load(outer, pl.ds(at, 1)), own(z, rows - 1))
+        down = two(own(z, 0), load(outer, pl.ds(at + 3, 1)))
+        store(outer, pl.ds(at + 4, 2), operator(z_two, up, down, w))
+        return 0
+
+    def near(s, _):
         k = index[pairs + s]
-        at = pl.ds(s * rows, rows)
-        w = [weights[n * rows : (n + 1) * rows, :] for n in range(5)]
-        store(image, at, operator(load(pre, at), above[pl.ds(k, 1), :], below[pl.ds(k, 1), :], w, rows, cols))
-        return 0
-
-    lax.fori_loop(0, count, one, 0)
-    apply_tiles(image, second, parts, rows, (count + CHUNK - 1) // CHUNK, 0)
-    fill_rims(second, index, up_ref, down_ref, rows, pairs, count)
-
-
-def sums_kernel(
-    index, field, pre, image, second, above, below, weights, last, sums, one_two, three_four, *, rows, cols, pairs, slots
-):
-    count = index[pairs + slots]
+        store(outer, pl.ds(s * RIM, 4), shared)
+        for end in range(2):
+            i = index[pairs + slots + 2 * s + end]
+            t = lax.div(index[pairs + 3 * slots + 2 * s + end], TILE)
+            sign = FOCAL_CURRENT * (1 - 2 * end)
+            for rim, first, place in ((above, -2, 0), (below, rows, 2)):
+
+                @pl.when((i >= first) & (i < first + 2))
+                def _():
+                    at = pl.ds(s * RIM + i - first + place, 1)
+                    outer[t, at, :] = outer[t, at, :] + sign * rim[pl.ds(end * pairs + k, 1), :]
+
+        return first_image(s, 0)
+
+    store(outer, slice(0, 4), shared)
+    first_image(0, 0)
+    lax.fori_loop(1, count, near, 0)
+
+    apply_tiles(image, second, parts, rows, chunks, 0)
+
+    def outer_tiles(c, _):
+        for tiles, row in ((tiles_above, 4), (tiles_below, 5)):
+            at = pl.ds(c * (CHUNK * RIM) + row, CHUNK, stride=RIM)
+            to = pl.ds(c * (CHUNK * RIM) + row + 2, CHUNK, stride=RIM)
+            for t in range(cols // TILE):
+                pair = jnp.concatenate(cut(tiles[0, t]), axis=1)
+                outer.at[t][to, :] = times_tile(outer.at[t][at, :], pair)
+        return 0
+
+    lax.fori_loop(0, chunks, outer_tiles, 0)
 
     def folded(x):
         acc = x[:, 0:TILE]
@@ -243,23 +339,23 @@
         return jnp.sum(acc, axis=0, keepdims=True)
 
     def four(s):
-        k = index[pairs + s]
         at = pl.ds(s * rows, rows)
         w = [weights[n * rows : (n + 1) * rows, :] for n in range(5)]
-        u = load(second, at)
-        v = operator(u, above[pl.ds(k, 1), :], below[pl.ds(k, 1), :], w, rows, cols)
+        u, u_two = load(second, at), load(outer, pl.ds(s * RIM + 6, 2))
+        v = operator(u, *stacked(u, own(u_two, 0), own(u_two, 1)), w)
         store(last, at, v)
         z, i = load(pre, at), load(image, at)
-        return k, folded(load(field, at) * z), folded(z * i), folded(i * u), folded(u * v)
-
-    _, a, b, c, d = four(0)
+        return folded(load(field, at) * z), folded(z * i), folded(i * u), folded(u * v)
+
+    a, b, c, d = four(0)
     one_two[0:pairs, :] = jnp.broadcast_to(a, (pairs, TILE))
     one_two[pairs : 2 * pairs, :] = jnp.broadcast_to(b, (pairs, TILE))
     three_four[0:pairs, :] = jnp.broadcast_to(c, (pairs, TILE))
     three_four[pairs : 2 * pairs, :] = jnp.broadcast_to(d, (pairs, TILE))
 
     def one(s, _):
-        k, a, b, c, d = four(s)
+        k = index[pairs + s]
+        a, b, c, d = four(s)
         one_two[pl.ds(k, 1), :] = a
         one_two[pl.ds(pairs + k, 1), :] = b
         three_four[pl.ds(k, 1), :] = c
@@ -334,7 +430,7 @@
     devices = lax.axis_size("space")
     f32 = jnp.float32
     sizes = dict(rows=rows, cols=cols, pairs=pairs, slots=slots)
-    strip, fields, rim = (rows, cols), (cols // TILE, slots * rows, TILE), (pairs + 8, cols)
+    strip, fields, rim = (rows, cols), (cols // TILE, slots * rows, TILE), (2 * pairs + cols // TILE * RIM, TILE)
     per_row = tile_inverse.shape[1:]
     limit = pltpu.CompilerParams(vmem_limit_bytes=24 * MIB)
     base_row = (lax.axis_index("space") * rows).astype(jnp.int32).reshape(1)
@@ -342,6 +438,7 @@
     def shaped(shape, dtype=f32):
         return jax.ShapeDtypeStruct(shape, dtype)
 
+    tiles_above, tiles_below = neighbours(tile_inverse[:1], tile_inverse[rows - 1 :])
     field, pre, index, parts, cells, up, down = pl.pallas_call(
         functools.partial(start_kernel, **sizes),
         in_specs=[smem(), *[hbm()] * 8],
@@ -349,7 +446,7 @@
         out_shape=[
             shaped(fields),
             shaped(fields),
-            shaped((pairs + slots + 8,), jnp.int32),
+            shaped((pairs + 5 * slots + 8,), jnp.int32),
             shaped((rows, *per_row[:2], 2 * TILE), jnp.bfloat16),
             shaped((3 * rows, cols)),
             shaped(rim),
@@ -388,25 +485,21 @@
     )
     above, below = neighbours(up, down)
 
-    image, second, weights, up, down = pl.pallas_call(
+    image, second, last, sums = pl.pallas_call(
         functools.partial(middle_kernel, **sizes),
-        in_specs=[smem(), *[vmem()] * 5],
-        out_specs=[vmem()] * 5,
-        out_shape=[shaped(fields), shaped(fields), shaped((5 * rows, cols)), shaped(rim), shaped(rim)],
+        in_specs=[smem(), *[vmem()] * 8],
+        out_specs=[vmem()] * 4,
+        out_shape=[shaped(fields), shaped(fields), shaped(fields), shaped((2, 2 * pairs))],
+        scratch_shapes=[
+            pltpu.VMEM((cols // TILE, slots * RIM, TILE), f32),
+            pltpu.VMEM((5 * rows, cols), f32),
+            pltpu.VMEM((5 * 8, cols), f32),
+            pltpu.VMEM((2 * pairs, TILE), f32),
+            pltpu.VMEM((2 * pairs, TILE), f32),
+        ],
         compiler_params=limit,
         name="middle",
-    )(index, cells, pre, parts, above, below)
-    above, below = neighbours(up, down)
-
-    last, sums = pl.pallas_call(
-        functools.partial(sums_kernel, **sizes),
-        in_specs=[smem(), *[vmem()] * 7],
-        out_specs=[vmem()] * 2,
-        out_shape=[shaped(fields), shaped((2, 2 * pairs))],
-        scratch_shapes=[pltpu.VMEM((2 * pairs, TILE), f32), pltpu.VMEM((2 * pairs, TILE), f32)],
-        compiler_params=limit,
-        name="sums",
-    )(index, field, pre, image, second, above, below, weights)
+    )(index, cells, field, pre, parts, above, below, tiles_above, tiles_below)
     copies = jnp.broadcast_to(sums, (devices, *sums.shape))
     everyone = lax.all_to_all(copies, "space", split_axis=0, concat_axis=0, tiled=True)
 

time: 113 us -> 103 us (0.912)
  waiting for transfers between devices: 19.9 us -> 6.13 us
  blocking collectives: 64.5 us -> 66.5 us
  local copies, waits for them, and re-layouts: 0.01 us -> 1.28 us
    ppermute x2, waiting for transfers between devices: 11.5 us -> 4.09 us  [neighbours(): lax.ppermute(up, 'space', [((i + 1) % count, i) for i in range(ends)])]
    ppermute x2, waiting for transfers between devices: 8.41 us -> 2.04 us  [neighbours(): lax.ppermute(down, 'space', [(i, (i + 1) % count) for i in range(ends)])]
    all_to_all x1, blocking collectives: 64.5 us -> 66.5 us  [on_device(): lax.all_to_all(copies, 'space', split_axis=0, concat_axis=0, tiled=True)]
    pallas_call x1 -> x0, Pallas kernels: 1.37 us -> none  [on_device(): pl.pallas_call(functools.partial(sums_kernel, **sizes), in_specs=[smem(),...]
    slice x0 -> x1, local copies, waits for them, and re-layouts: none -> 1.27 us  [on_device(): tile_inverse[:1]]
  transfers between devices with their start and end apart: 4 -> 4, of which waited for: 4 -> 2; matrix products, arithmetic and copies ran while one was open for 0% -> 0% of each run, Pallas kernels for 0% -> 5%
where the time goes in v3:
time: 103 us; the launch traced here: 101 us
  blocking collectives  66.5 us (65%)
  Pallas kernels  14.1 us (14%)
  starting transfers between devices  12.7 us (12%)
  waiting for transfers between devices  6.13 us (6%)
  local copies, waits for them, and re-layouts  1.28 us (1%)
    all_to_all x1, blocking collectives, on_device(): lax.all_to_all(copies, 'space', split_axis=0, concat_axis=0, tiled=True)  66.5 us
    ppermute x2, starting transfers between devices, neighbours(): lax.ppermute(down, 'space', [(i, (i + 1) % count) for i in range(ends)])  10.1 us
    pallas_call x1, Pallas kernels, on_device(): pl.pallas_call(functools.partial(start_kernel, **sizes), in_specs=[smem()...  5.19 us
    pallas_call x1, Pallas kernels, on_device(): pl.pallas_call(functools.partial(finish_kernel, rows=rows, cols=cols, pai...  5.03 us
    ppermute x2, waiting for transfers between devices, neighbours(): lax.ppermute(up, 'space', [((i + 1) % count, i) for i in range(ends)])  4.09 us
    pallas_call x1, Pallas kernels, on_device(): pl.pallas_call(functools.partial(middle_kernel, **sizes), in_specs=[smem(...  3.87 us
    ppermute x2, starting transfers between devices, neighbours(): lax.ppermute(up, 'space', [((i + 1) % count, i) for i in range(ends)])  2.62 us
  transfers between devices with their start and end apart: 4, of which 2 were waited for; matrix products, arithmetic and copies ran while one was open for 0% of the time, Pallas kernels for 5%

profile of v3, /device:TPU:40, one launch (start us, length us, event | category | flops | bytes accessed | tf_op | source)
XLA Modules:
  0.0 101.5 jit_solution(9933798096701327985)
XLA Ops:
  0.6 1.3 %fusion = (f32[1,8,128,128]{3,2,1,0:T(8,128)S(1)}, f32[1,8,128,128]{3,2,1,0:T(8,128)S(1)}) fusion(f32[8,8,128,128]{3,2,1,0:T(8,128)} %tiles_hbm.1), kind=kLoop, calls=%fused_computation | loop fusion | bytes 2097152 | tf_op jit(solution)/shard_map/slice | solution.py:441
  1.9 1.3 %collective-permute-start.3 = (f32[1,8,128,128]{3,2,1,0:T(8,128)S(1)}, f32[1,8,128,128]{3,2,1,0:T(8,128)S(1)}, u32[]{:S(2)}, u32[]{:S(2)}) collective-permute-start(f32[1,8,128,128]{3,2,1,0:T(8,128)S(1)} %get-tuple-element.24), channel_id=1, source_target_pairs={{8,0},{16,8},{24,16},{32,24},{40,32},{48,40},{56,48},{64,56},{72,6... | collective-permute-start | bytes 1572872 | tf_op jit(solution)/shard_map/ppermute | solution.py:422
  3.2 5.4 %collective-permute-start.2 = (f32[1,8,128,128]{3,2,1,0:T(8,128)S(1)}, f32[1,8,128,128]{3,2,1,0:T(8,128)S(1)}, u32[]{:S(2)}, u32[]{:S(2)}) collective-permute-start(f32[1,8,128,128]{3,2,1,0:T(8,128)S(1)} %get-tuple-element.25), channel_id=1, source_target_pairs={{0,8},{8,16},{16,24},{24,32},{32,40},{40,48},{48,56},{56,64},{64,7... | collective-permute-start | bytes 1572872 | tf_op jit(solution)/shard_map/ppermute | solution.py:421
  8.6 5.2 %start.1 = (f32[8,640,128]{2,1,0:T(8,128)S(1)}, f32[8,640,128]{2,1,0:T(8,128)S(1)}, s32[472]{0:T(512)S(1)}, bf16[8,8,128,256]{3,2,1,0:T(8,128)(2,1)S(1)}, f32[24...) custom-call(s32[1]{0:T(128)} %bitcast.where, s32[2,64]{1,0:T(2,128)} %bitcast.2, ...), custom_call_target="tpu_custom_call" | custom-call | tf_op jit(solution)/shard_map/start/pallas_call | solution.py:442
  13.8 4.7 %collective-permute-start = (f32[192,128]{1,0:T(8,128)S(1)}, f32[192,128]{1,0:T(8,128)S(1)}, u32[]{:S(2)}, u32[]{:S(2)}) collective-permute-start(f32[192,128]{1,0:T(8,128)S(1)} %get-tuple-element.18), channel_id=1, source_target_pairs={{0,8},{8,16},{16,24},{24,32},{32,40},{40,48},{48,56},{56,64},{64,7... | collective-permute-start | bytes 294920 | tf_op jit(solution)/shard_map/ppermute | solution.py:421
  18.6 1.3 %collective-permute-start.1 = (f32[192,128]{1,0:T(8,128)S(1)}, f32[192,128]{1,0:T(8,128)S(1)}, u32[]{:S(2)}, u32[]{:S(2)}) collective-permute-start(f32[192,128]{1,0:T(8,128)S(1)} %get-tuple-element.19), channel_id=1, source_target_pairs={{8,0},{16,8},{24,16},{32,24},{40,32},{48,40},{56,48},{64,56},{72,6... | collective-permute-start | bytes 294920 | tf_op jit(solution)/shard_map/ppermute | solution.py:422
  19.9 2.0 %collective-permute-done.above = f32[192,128]{1,0:T(8,128)S(1)} collective-permute-done((f32[192,128]{1,0:T(8,128)S(1)}, f32[192,128]{1,0:T(8,128)S(1)}, u32[]{:S(2)}, u32[]{:S(2)}) %collective-permute-start) | collective-permute-done | bytes 98336 | tf_op jit(solution)/shard_map/ppermute | solution.py:421
  21.9 4.1 %collective-permute-done.1.below = f32[192,128]{1,0:T(8,128)S(1)} collective-permute-done((f32[192,128]{1,0:T(8,128)S(1)}, f32[192,128]{1,0:T(8,128)S(1)}, u32[]{:S(2)}, u32[]{:S(2)}) %collective-permute-start.1) | collective-permute-done | bytes 98336 | tf_op jit(solution)/shard_map/ppermute | solution.py:422
  26.0 0.0 collective-permute-done.3.tiles_below
  26.0 0.0 collective-permute-done.2.tiles_above
  26.0 3.9 %middle.1 = (f32[8,640,128]{2,1,0:T(8,128)S(1)}, f32[8,640,128]{2,1,0:T(8,128)S(1)}, f32[8,640,128]{2,1,0:T(8,128)S(1)}, f32[2,128]{1,0:T(2,128)S(1)}) custom-call(s32[472]{0:T(512)S(1)} %get-tuple-element.13.index, f32[24,1024]{1,0:T(8,128)S(1)} %get-tuple-element.14.cells, f32[8,640,128]{2,1,0:T(8,128)S(1)} %get-tuple-element.15.field, ...), custom_call_target="tpu_custom_call" | custom-call | tf_op jit(solution)/shard_map/middle/pallas_call | solution.py:488
  29.9 66.5 %all_to_all.5.everyone = f32[32,2,128]{2,1,0:T(2,128)S(1)} all-to-all(f32[32,2,128]{2,1,0:T(2,128)S(1)} %broadcast_in_dim.3), channel_id=1, replica_groups=mesh['groups'=2,'space'=32,'rhs'=8] {'space'}, dimensions={0} | all-to-all | bytes 65536 | tf_op jit(solution)/shard_map/all_to_all | solution.py:504
  96.4 5.0 %finish.1 = (f32[64,8,1024]{2,1,0:T(8,128)}, f32[64,8,1024]{2,1,0:T(8,128)}) custom-call(s32[472]{0:T(512)S(1)} %get-tuple-element.13.index, f32[32,2,128]{2,1,0:T(2,128)S(1)} %all_to_all.5.everyone, f32[8,640,128]{2,1,0:T(8,128)S(1)} %get-tuple-element.15.field, f32[8,640,128]{2,1,0:T(8,128)S(1)} %get-tuple-element.16.pre, ...), custom_call_target="tpu_custom_call" | custom-call | tf_op jit(solution)/shard_map/finish/pallas_call | solution.py:509
  (1 shorter events, 0.0 us)
Async XLA Ops:
  1.9 24.1 %collective-permute-start.3 = (f32[1,8,128,128]{3,2,1,0:T(8,128)S(1)}, f32[1,8,128,128]{3,2,1,0:T(8,128)S(1)}, u32[]{:S(2)}, u32[]{:S(2)}) collective-permute-start(f32[1,8,128,128]{3,2,1,0:T(8,128)S(1)} %get-tuple-element.24), channel_id=1, source_target_pairs={{8,0},{16,8},{24,16},{32,24},{40,32},{48,40},{56,48},{64,56},{72,6... | collective-permute-start | bytes 1572872 | tf_op jit(solution)/shard_map/ppermute | solution.py:422
  3.2 22.8 %collective-permute-start.2 = (f32[1,8,128,128]{3,2,1,0:T(8,128)S(1)}, f32[1,8,128,128]{3,2,1,0:T(8,128)S(1)}, u32[]{:S(2)}, u32[]{:S(2)}) collective-permute-start(f32[1,8,128,128]{3,2,1,0:T(8,128)S(1)} %get-tuple-element.25), channel_id=1, source_target_pairs={{0,8},{8,16},{16,24},{24,32},{32,40},{40,48},{48,56},{56,64},{64,7... | collective-permute-start | bytes 1572872 | tf_op jit(solution)/shard_map/ppermute | solution.py:421
  13.8 8.1 %collective-permute-start = (f32[192,128]{1,0:T(8,128)S(1)}, f32[192,128]{1,0:T(8,128)S(1)}, u32[]{:S(2)}, u32[]{:S(2)}) collective-permute-start(f32[192,128]{1,0:T(8,128)S(1)} %get-tuple-element.18), channel_id=1, source_target_pairs={{0,8},{8,16},{16,24},{24,32},{32,40},{40,48},{48,56},{56,64},{64,7... | collective-permute-start | bytes 294920 | tf_op jit(solution)/shard_map/ppermute | solution.py:421
  18.6 7.4 %collective-permute-start.1 = (f32[192,128]{1,0:T(8,128)S(1)}, f32[192,128]{1,0:T(8,128)S(1)}, u32[]{:S(2)}, u32[]{:S(2)}) collective-permute-start(f32[192,128]{1,0:T(8,128)S(1)} %get-tuple-element.19), channel_id=1, source_target_pairs={{8,0},{16,8},{24,16},{32,24},{40,32},{48,40},{56,48},{64,56},{72,6... | collective-permute-start | bytes 294920 | tf_op jit(solution)/shard_map/ppermute | solution.py:422

commit v4 on v3

--- a/solution.py
+++ b/solution.py
@@ -37,16 +37,40 @@
     return (y[:n, :TILE] + y[n:, TILE:]) + (y[n:, :TILE] + y[:n, TILE:])
 
 
-def apply_tiles(src, dst, parts, rows, chunks, first):
-    def one(i, _):
-        c = lax.div(i, rows)
-        r = i - c * rows
-        at = pl.ds(c * (CHUNK * rows) + r, CHUNK, stride=rows)
+def apply_tiles(src, dst, which, rows, chunks, first=0):
+    def one(c, _):
+        for r, parts, n in which:
+            at = pl.ds(c * (CHUNK * rows) + r, CHUNK, stride=rows)
+            for t in range(src.shape[0]):
+                dst.at[t][at, :] = times_tile(src.at[t][at, :], parts[n, t])
+        return 0
+
+    lax.fori_loop(first, chunks, one, 0)
+
+
+def keep_rows(src, dst, which, rows, chunks):
+    def one(c, _):
+        for r in which:
+            at = pl.ds(c * (CHUNK * rows) + r, CHUNK, stride=rows)
+            for t in range(src.shape[0]):
+                dst.at[t][at, :] = src.at[t][at, :]
+        return 0
+
+    lax.fori_loop(0, chunks, one, 0)
+
+
+def split_rows(src, dst, which, tiles_hbm, tiles, sems, parts, rows):
+    for n, r in enumerate(which):
+        pltpu.make_async_copy(tiles_hbm.at[r], tiles.at[n], sems.at[n]).wait()
+        at = pl.ds(r, CHUNK, stride=rows)
         for t in range(src.shape[0]):
-            dst.at[t][at, :] = times_tile(src.at[t][at, :], parts[r, t])
-        return 0
-
-    lax.fori_loop(first * rows, chunks * rows, one, 0)
+            pair = jnp.concatenate(cut(tiles[n, t]), axis=1)
+            parts[n, t] = pair
+            dst.at[t][at, :] = times_tile(src.at[t][at, :], pair)
+
+
+def outer_rows(rows):
+    return (0, 1, rows - 2, rows - 1)
 
 
 def beside(x):
@@ -132,8 +156,8 @@
     ]
     for copy in arrivals:
         copy.start()
-    for r in range(rows):
-        pltpu.make_async_copy(tiles_hbm.at[r], tiles.at[r], tile_sems.at[r]).start()
+    for n, r in enumerate(outer_rows(rows)):
+        pltpu.make_async_copy(tiles_hbm.at[r], tiles.at[n], tile_sems.at[n]).start()
 
     base_row = where[0]
     cells_of_pairs.wait()
@@ -188,17 +212,8 @@
     grounded = ground_mask[...].astype(jnp.float32) * ground_value[...]
     cells[2 * rows : 3 * rows, :] = grounded
 
-    def row(r, _):
-        pltpu.make_async_copy(tiles_hbm.at[r], tiles.at[r], tile_sems.at[r]).wait()
-        at = pl.ds(r, CHUNK, stride=rows)
-        for t in range(cols // TILE):
-            pair = jnp.concatenate(cut(tiles[r, t]), axis=1)
-            parts[r, t] = pair
-            pre.at[t][at, :] = times_tile(field.at[t][at, :], pair)
-        return 0
-
-    lax.fori_loop(0, rows, row, 0)
-    apply_tiles(field, pre, parts, rows, chunks, 1)
+    split_rows(field, pre, outer_rows(rows), tiles_hbm, tiles, tile_sems, parts, rows)
+    apply_tiles(field, pre, [(r, parts, n) for n, r in enumerate(outer_rows(rows))], rows, chunks, 1)
 
     for rim, first, outermost in ((up_ref, 0, 0), (down_ref, rows - 2, rows - 1)):
         two = slice(first, first + 2)
@@ -216,15 +231,42 @@
             i = index[pairs + slots + 2 * s + end]
             j = index[pairs + 3 * slots + 2 * s + end]
             t = lax.div(j, TILE)
-            for rim, first in ((up_ref, 0), (down_ref, rows - 2)):
+            for rim, first, place in ((up_ref, 0, 0), (down_ref, rows - 2, 2)):
 
                 @pl.when((i >= first) & (i < first + 2))
                 def _():
-                    rim[pl.ds(end * pairs + k, 1), :] = tiles[i, t, pl.ds(j - t * TILE, 1), :]
+                    rim[pl.ds(end * pairs + k, 1), :] = tiles[i - first + place, t, pl.ds(j - t * TILE, 1), :]
 
         return 0
 
     lax.fori_loop(1, count, selected, 0)
+
+
+def inner_kernel(
+    index, cells, field, parts, tiles_hbm, outer_pre, pre, second, image, tiles, inner_parts, sems, *, rows, cols, pairs, slots
+):
+    rest = range(2, rows - 2)
+    for n, r in enumerate(rest):
+        pltpu.make_async_copy(tiles_hbm.at[r], tiles.at[n], sems.at[n]).start()
+    count = index[pairs + 5 * slots]
+    chunks = (count + CHUNK - 1) // CHUNK
+    active, valid, grounded = (cells[n * rows : (n + 1) * rows, :] for n in range(3))
+    zero = jnp.zeros((1, cols), jnp.float32)
+    weights = weights_of(active, valid, grounded, stacked(active, zero, zero), stacked(valid, zero, zero))
+
+    keep_rows(outer_pre, pre, outer_rows(rows), rows, chunks)
+    split_rows(field, pre, rest, tiles_hbm, tiles, sems, inner_parts, rows)
+    inner = [(r, inner_parts, n) for n, r in enumerate(rest)]
+    apply_tiles(field, pre, inner, rows, chunks, 1)
+
+    def one(s, _):
+        at = pl.ds(s * rows, rows)
+        z = load(pre, at)
+        store(image, at, operator(z, *stacked(z, zero, zero), weights))
+        return 0
+
+    lax.fori_loop(0, count, one, 0)
+    apply_tiles(image, second, [(1, parts, 1), *inner, (rows - 2, parts, 2)], rows, chunks)
 
 
 def middle_kernel(
@@ -237,6 +279,7 @@
     below,
     tiles_above,
     tiles_below,
+    inner_second,
     image,
     second,
     last,
@@ -319,7 +362,8 @@
     first_image(0, 0)
     lax.fori_loop(1, count, near, 0)
 
-    apply_tiles(image, second, parts, rows, chunks, 0)
+    keep_rows(inner_second, second, range(1, rows - 1), rows, chunks)
+    apply_tiles(image, second, [(0, parts, 0), (rows - 1, parts, 3)], rows, chunks)
 
     def outer_tiles(c, _):
         for tiles, row in ((tiles_above, 4), (tiles_below, 5)):
@@ -368,39 +412,70 @@
 
 
 def finish_kernel(
-    index, everyone, field, pre, image, second, last, solution, residual, first_c, second_c, *, rows, cols, pairs, block
+    index,
+    everyone,
+    field,
+    pre,
+    image,
+    second,
+    last,
+    solution_hbm,
+    residual_hbm,
+    first_c,
+    second_c,
+    solution,
+    residual,
+    solution_sems,
+    residual_sems,
+    *,
+    rows,
+    cols,
+    pairs,
+    block,
 ):
-    step = pl.program_id(0)
-
-    @pl.when(step == 0)
-    def _():
-        total = jnp.sum(everyone[...], axis=0)
-        ab, cd = total[0:1, :], total[1:2, :]
-        gamma, delta = ab[:, :pairs], ab[:, pairs:]
-        eta, theta = cd[:, :pairs], cd[:, pairs:]
-        alpha = gamma / delta
-        gamma_next = alpha * alpha * eta - gamma
-        beta = 1.0 + gamma_next / gamma
-        curvature = beta * beta * delta - 2.0 * beta * alpha * eta + alpha * alpha * theta
-        step_next = gamma_next / curvature
-        both = jnp.concatenate([alpha + step_next * beta, alpha * step_next], axis=1)
-        spread = jnp.broadcast_to(both, (2 * pairs, 2 * pairs)).T
-        first_c[...] = spread[:pairs, :]
-        second_c[...] = spread[pairs:, :]
-
-    def one(p, _):
-        k = step * block + p
-        s = index[k]
-        at = pl.ds(s * rows, rows)
-        a = jnp.broadcast_to(first_c[pl.ds(k, 1), :], (rows, TILE))
-        b = jnp.broadcast_to(second_c[pl.ds(k, 1), :], (rows, TILE))
-        for t in range(cols // TILE):
-            lanes = slice(t * TILE, (t + 1) * TILE)
-            solution[p, :, lanes] = a * pre[t, at, :] - b * second[t, at, :]
-            residual[p, :, lanes] = field[t, at, :] - a * image[t, at, :] + b * last[t, at, :]
-        return 0
-
-    lax.fori_loop(0, block, one, 0, unroll=4)
+    total = jnp.sum(everyone[...], axis=0)
+    ab, cd = total[0:1, :], total[1:2, :]
+    gamma, delta = ab[:, :pairs], ab[:, pairs:]
+    eta, theta = cd[:, :pairs], cd[:, pairs:]
+    alpha = gamma / delta
+    gamma_next = alpha * alpha * eta - gamma
+    beta = 1.0 + gamma_next / gamma
+    curvature = beta * beta * delta - 2.0 * beta * alpha * eta + alpha * alpha * theta
+    step_next = gamma_next / curvature
+    both = jnp.concatenate([alpha + step_next * beta, alpha * step_next], axis=1)
+    spread = jnp.broadcast_to(both, (2 * pairs, 2 * pairs)).T
+    first_c[...] = spread[:pairs, :]
+    second_c[...] = spread[pairs:, :]
+
+    def copies(n):
+        at = pl.ds(n * block, block)
+        return (
+            pltpu.make_async_copy(solution.at[at], solution_hbm.at[at], solution_sems.at[n]),
+            pltpu.make_async_copy(residual.at[at], residual_hbm.at[at], residual_sems.at[n]),
+        )
+
+    def one(n, _):
+        for p in range(block):
+            k = n * block + p
+            at = pl.ds(pl.multiple_of(index[k] * rows, 8), rows)
+            a = jnp.broadcast_to(first_c[pl.ds(k, 1), :], (rows, TILE))
+            b = jnp.broadcast_to(second_c[pl.ds(k, 1), :], (rows, TILE))
+            for t in range(cols // TILE):
+                lanes = slice(t * TILE, (t + 1) * TILE)
+                solution[k, :, lanes] = a * pre[t, at, :] - b * second[t, at, :]
+                residual[k, :, lanes] = field[t, at, :] - a * image[t, at, :] + b * last[t, at, :]
+        for copy in copies(n):
+            copy.start()
+        return 0
+
+    lax.fori_loop(0, pairs // block, one, 0)
+
+    def arrived(n, _):
+        for copy in copies(n):
+            copy.wait()
+        return 0
+
+    lax.fori_loop(0, pairs // block, arrived, 0)
 
 
 def smem():
@@ -447,7 +522,7 @@
             shaped(fields),
             shaped(fields),
             shaped((pairs + 5 * slots + 8,), jnp.int32),
-            shaped((rows, *per_row[:2], 2 * TILE), jnp.bfloat16),
+            shaped((4, *per_row[:2], 2 * TILE), jnp.bfloat16),
             shaped((3 * rows, cols)),
             shaped(rim),
             shaped(rim),
@@ -460,10 +535,10 @@
             pltpu.VMEM(strip, jnp.int32),
             pltpu.VMEM(strip, jnp.int32),
             pltpu.VMEM(strip, f32),
-            pltpu.VMEM((rows, *per_row), f32),
+            pltpu.VMEM((4, *per_row), f32),
             pltpu.SemaphoreType.DMA,
             pltpu.SemaphoreType.DMA((6,)),
-            pltpu.SemaphoreType.DMA((rows,)),
+            pltpu.SemaphoreType.DMA((4,)),
         ],
         compiler_params=limit,
         name="start",
@@ -485,11 +560,26 @@
     )
     above, below = neighbours(up, down)
 
+    pre, inner_second = pl.pallas_call(
+        functools.partial(inner_kernel, **sizes),
+        in_specs=[smem(), *[vmem()] * 3, hbm(), vmem()],
+        out_specs=[vmem()] * 2,
+        out_shape=[shaped(fields)] * 2,
+        scratch_shapes=[
+            pltpu.VMEM(fields, f32),
+            pltpu.VMEM((rows - 4, *per_row), f32),
+            pltpu.VMEM((rows - 4, *per_row[:2], 2 * TILE), jnp.bfloat16),
+            pltpu.SemaphoreType.DMA((rows - 4,)),
+        ],
+        compiler_params=limit,
+        name="inner",
+    )(index, cells, field, parts, pltpu.with_memory_space_constraint(tile_inverse, pltpu.HBM), pre)
+
     image, second, last, sums = pl.pallas_call(
         functools.partial(middle_kernel, **sizes),
-        in_specs=[smem(), *[vmem()] * 8],
+        in_specs=[smem(), *[vmem()] * 9],
         out_specs=[vmem()] * 4,
-        out_shape=[shaped(fields), shaped(fields), shaped(fields), shaped((2, 2 * pairs))],
+        out_shape=[*[shaped(fields)] * 3, shaped((2, 2 * pairs))],
         scratch_shapes=[
             pltpu.VMEM((cols // TILE, slots * RIM, TILE), f32),
             pltpu.VMEM((5 * rows, cols), f32),
@@ -499,20 +589,25 @@
         ],
         compiler_params=limit,
         name="middle",
-    )(index, cells, field, pre, parts, above, below, tiles_above, tiles_below)
+    )(index, cells, field, pre, parts, above, below, tiles_above, tiles_below, inner_second)
     copies = jnp.broadcast_to(sums, (devices, *sums.shape))
     everyone = lax.all_to_all(copies, "space", split_axis=0, concat_axis=0, tiled=True)
 
     block = 8
-    out = jax.ShapeDtypeStruct((pairs, rows, cols), f32)
-    out_block = pl.BlockSpec((block, rows, cols), lambda p: (p, 0, 0))
+    out = (pairs, rows, cols)
     return pl.pallas_call(
         functools.partial(finish_kernel, rows=rows, cols=cols, pairs=pairs, block=block),
-        grid=(pairs // block,),
         in_specs=[smem(), *[vmem()] * 6],
-        out_specs=[out_block, out_block],
-        out_shape=[out, out],
-        scratch_shapes=[pltpu.VMEM((pairs, TILE), f32), pltpu.VMEM((pairs, TILE), f32)],
+        out_specs=[hbm()] * 2,
+        out_shape=[shaped(out)] * 2,
+        scratch_shapes=[
+            pltpu.VMEM((pairs, TILE), f32),
+            pltpu.VMEM((pairs, TILE), f32),
+            pltpu.VMEM(out, f32),
+            pltpu.VMEM(out, f32),
+            pltpu.SemaphoreType.DMA((pairs // block,)),
+            pltpu.SemaphoreType.DMA((pairs // block,)),
+        ],
         compiler_params=limit,
         name="finish",
     )(index, everyone, field, pre, image, second, last)

time: 103 us -> 98.6 us (0.957)
  waiting for transfers between devices: 6.13 us -> 2.32 us
    pallas_call x0 -> x1, Pallas kernels: none -> 3.85 us  [on_device(): pl.pallas_call(functools.partial(inner_kernel, **sizes), in_specs=[smem()...]
    ppermute x2, waiting for transfers between devices: 2.04 us -> 0.01 us  [neighbours(): lax.ppermute(down, 'space', [(i, (i + 1) % count) for i in range(ends)])]
    pallas_call x1, Pallas kernels: 5.03 us -> 3.25 us  [on_device(): pl.pallas_call(functools.partial(finish_kernel, rows=rows, cols=cols, pai...]
    ppermute x2, waiting for transfers between devices: 4.09 us -> 2.32 us  [neighbours(): lax.ppermute(up, 'space', [((i + 1) % count, i) for i in range(ends)])]
  transfers between devices with their start and end apart: 4 -> 4, of which waited for: 2 -> 1; matrix products, arithmetic and copies ran while one was open for 0% -> 0% of each run, Pallas kernels for 5% -> 8%
where the time goes in v4:
time: 98.6 us; the launch traced here: 98.1 us
  blocking collectives  66.3 us (67%)
  Pallas kernels  14.7 us (15%)
  starting transfers between devices  12.7 us (13%)
  waiting for transfers between devices  2.32 us (2%)
  local copies, waits for them, and re-layouts  1.28 us (1%)
    all_to_all x1, blocking collectives, on_device(): lax.all_to_all(copies, 'space', split_axis=0, concat_axis=0, tiled=True)  66.3 us
    ppermute x2, starting transfers between devices, neighbours(): lax.ppermute(down, 'space', [(i, (i + 1) % count) for i in range(ends)])  10.1 us
    pallas_call x1, Pallas kernels, on_device(): pl.pallas_call(functools.partial(start_kernel, **sizes), in_specs=[smem()...  4.39 us
    pallas_call x1, Pallas kernels, on_device(): pl.pallas_call(functools.partial(inner_kernel, **sizes), in_specs=[smem()...  3.85 us
    pallas_call x1, Pallas kernels, on_device(): pl.pallas_call(functools.partial(middle_kernel, **sizes), in_specs=[smem(...  3.25 us
    pallas_call x1, Pallas kernels, on_device(): pl.pallas_call(functools.partial(finish_kernel, rows=rows, cols=cols, pai...  3.25 us
    ppermute x2, starting transfers between devices, neighbours(): lax.ppermute(up, 'space', [((i + 1) % count, i) for i in range(ends)])  2.62 us
    ppermute x2, waiting for transfers between devices, neighbours(): lax.ppermute(up, 'space', [((i + 1) % count, i) for i in range(ends)])  2.32 us
  transfers between devices with their start and end apart: 4, of which 1 were waited for; matrix products, arithmetic and copies ran while one was open for 0% of the time, Pallas kernels for 8%

profile of v4, /device:TPU:40, one launch (start us, length us, event | category | flops | bytes accessed | tf_op | source)
XLA Modules:
  0.0 98.1 jit_solution(15878761056150769121)
XLA Ops:
  0.6 1.3 %fusion = (f32[1,8,128,128]{3,2,1,0:T(8,128)S(1)}, f32[1,8,128,128]{3,2,1,0:T(8,128)S(1)}) fusion(f32[8,8,128,128]{3,2,1,0:T(8,128)} %tiles_hbm.3), kind=kLoop, calls=%fused_computation | loop fusion | bytes 2097152 | tf_op jit(solution)/shard_map/slice | solution.py:516
  1.9 1.3 %collective-permute-start.3 = (f32[1,8,128,128]{3,2,1,0:T(8,128)S(1)}, f32[1,8,128,128]{3,2,1,0:T(8,128)S(1)}, u32[]{:S(2)}, u32[]{:S(2)}) collective-permute-start(f32[1,8,128,128]{3,2,1,0:T(8,128)S(1)} %get-tuple-element.28), channel_id=1, source_target_pairs={{8,0},{16,8},{24,16},{32,24},{40,32},{48,40},{56,48},{64,56},{72,6... | collective-permute-start | bytes 1572872 | tf_op jit(solution)/shard_map/ppermute | solution.py:497
  3.2 5.4 %collective-permute-start.2 = (f32[1,8,128,128]{3,2,1,0:T(8,128)S(1)}, f32[1,8,128,128]{3,2,1,0:T(8,128)S(1)}, u32[]{:S(2)}, u32[]{:S(2)}) collective-permute-start(f32[1,8,128,128]{3,2,1,0:T(8,128)S(1)} %get-tuple-element.29), channel_id=1, source_target_pairs={{0,8},{8,16},{16,24},{24,32},{32,40},{40,48},{48,56},{56,64},{64,7... | collective-permute-start | bytes 1572872 | tf_op jit(solution)/shard_map/ppermute | solution.py:496
  8.6 4.4 %start.1 = (f32[8,640,128]{2,1,0:T(8,128)S(1)}, f32[8,640,128]{2,1,0:T(8,128)S(1)}, s32[472]{0:T(512)S(1)}, bf16[4,8,128,256]{3,2,1,0:T(8,128)(2,1)S(1)}, f32[24...) custom-call(s32[1]{0:T(128)} %bitcast.where, s32[2,64]{1,0:T(2,128)} %bitcast.2, ...), custom_call_target="tpu_custom_call" | custom-call | tf_op jit(solution)/shard_map/start/pallas_call | solution.py:517
  13.0 4.7 %collective-permute-start = (f32[192,128]{1,0:T(8,128)S(1)}, f32[192,128]{1,0:T(8,128)S(1)}, u32[]{:S(2)}, u32[]{:S(2)}) collective-permute-start(f32[192,128]{1,0:T(8,128)S(1)} %get-tuple-element.21), channel_id=1, source_target_pairs={{0,8},{8,16},{16,24},{24,32},{32,40},{40,48},{48,56},{56,64},{64,7... | collective-permute-start | bytes 294920 | tf_op jit(solution)/shard_map/ppermute | solution.py:496
  17.8 1.3 %collective-permute-start.1 = (f32[192,128]{1,0:T(8,128)S(1)}, f32[192,128]{1,0:T(8,128)S(1)}, u32[]{:S(2)}, u32[]{:S(2)}) collective-permute-start(f32[192,128]{1,0:T(8,128)S(1)} %get-tuple-element.22), channel_id=1, source_target_pairs={{8,0},{16,8},{24,16},{32,24},{40,32},{48,40},{56,48},{64,56},{72,6... | collective-permute-start | bytes 294920 | tf_op jit(solution)/shard_map/ppermute | solution.py:497
  19.1 3.8 %inner.1 = (f32[8,640,128]{2,1,0:T(8,128)S(1)}, f32[8,640,128]{2,1,0:T(8,128)S(1)}) custom-call(s32[472]{0:T(512)S(1)} %get-tuple-element.15.index, f32[24,1024]{1,0:T(8,128)S(1)} %get-tuple-element.16.cells, f32[8,640,128]{2,1,0:T(8,128)S(1)} %get-tuple-element.17.field, bf16[4,8,128,256]{3,2,1,0:T(8,128)(2,1)S(1)} %get-tuple-element.18.parts, ...), custom_call_target="tpu_custom_call" | custom-call | tf_op jit(solution)/shard_map/inner/pallas_call | solution.py:563
  22.9 0.0 collective-permute-done.above
  23.0 2.3 %collective-permute-done.1.below = f32[192,128]{1,0:T(8,128)S(1)} collective-permute-done((f32[192,128]{1,0:T(8,128)S(1)}, f32[192,128]{1,0:T(8,128)S(1)}, u32[]{:S(2)}, u32[]{:S(2)}) %collective-permute-start.1) | collective-permute-done | bytes 98336 | tf_op jit(solution)/shard_map/ppermute | solution.py:497
  25.3 0.0 collective-permute-done.3.tiles_below
  25.3 0.0 collective-permute-done.2.tiles_above
  25.3 3.2 %middle.1 = (f32[8,640,128]{2,1,0:T(8,128)S(1)}, f32[8,640,128]{2,1,0:T(8,128)S(1)}, f32[8,640,128]{2,1,0:T(8,128)S(1)}, f32[2,128]{1,0:T(2,128)S(1)}) custom-call(s32[472]{0:T(512)S(1)} %get-tuple-element.15.index, f32[24,1024]{1,0:T(8,128)S(1)} %get-tuple-element.16.cells, f32[8,640,128]{2,1,0:T(8,128)S(1)} %get-tuple-element.17.field, ...), custom_call_target="tpu_custom_call" | custom-call | tf_op jit(solution)/shard_map/middle/pallas_call | solution.py:578
  28.6 66.3 %all_to_all.5.everyone = f32[32,2,128]{2,1,0:T(2,128)S(1)} all-to-all(f32[32,2,128]{2,1,0:T(2,128)S(1)} %broadcast_in_dim.3), channel_id=1, replica_groups=mesh['groups'=2,'space'=32,'rhs'=8] {'space'}, dimensions={0} | all-to-all | bytes 65536 | tf_op jit(solution)/shard_map/all_to_all | solution.py:594
  94.8 3.2 %finish.1 = (f32[64,8,1024]{2,1,0:T(8,128)}, f32[64,8,1024]{2,1,0:T(8,128)}) custom-call(s32[472]{0:T(512)S(1)} %get-tuple-element.15.index, f32[32,2,128]{2,1,0:T(2,128)S(1)} %all_to_all.5.everyone, f32[8,640,128]{2,1,0:T(8,128)S(1)} %get-tuple-element.17.field, f32[8,640,128]{2,1,0:T(8,128)S(1)} %get-tuple-element.20.pre, ...), custom_call_target="tpu_custom_call" | custom-call | tf_op jit(solution)/shard_map/finish/pallas_call | solution.py:598
  (1 shorter events, 0.0 us)
Async XLA Ops:
  1.9 23.4 %collective-permute-start.3 = (f32[1,8,128,128]{3,2,1,0:T(8,128)S(1)}, f32[1,8,128,128]{3,2,1,0:T(8,128)S(1)}, u32[]{:S(2)}, u32[]{:S(2)}) collective-permute-start(f32[1,8,128,128]{3,2,1,0:T(8,128)S(1)} %get-tuple-element.28), channel_id=1, source_target_pairs={{8,0},{16,8},{24,16},{32,24},{40,32},{48,40},{56,48},{64,56},{72,6... | collective-permute-start | bytes 1572872 | tf_op jit(solution)/shard_map/ppermute | solution.py:497
  3.2 22.1 %collective-permute-start.2 = (f32[1,8,128,128]{3,2,1,0:T(8,128)S(1)}, f32[1,8,128,128]{3,2,1,0:T(8,128)S(1)}, u32[]{:S(2)}, u32[]{:S(2)}) collective-permute-start(f32[1,8,128,128]{3,2,1,0:T(8,128)S(1)} %get-tuple-element.29), channel_id=1, source_target_pairs={{0,8},{8,16},{16,24},{24,32},{32,40},{40,48},{48,56},{56,64},{64,7... | collective-permute-start | bytes 1572872 | tf_op jit(solution)/shard_map/ppermute | solution.py:496
  13.0 9.9 %collective-permute-start = (f32[192,128]{1,0:T(8,128)S(1)}, f32[192,128]{1,0:T(8,128)S(1)}, u32[]{:S(2)}, u32[]{:S(2)}) collective-permute-start(f32[192,128]{1,0:T(8,128)S(1)} %get-tuple-element.21), channel_id=1, source_target_pairs={{0,8},{8,16},{16,24},{24,32},{32,40},{40,48},{48,56},{56,64},{64,7... | collective-permute-start | bytes 294920 | tf_op jit(solution)/shard_map/ppermute | solution.py:496
  17.8 7.5 %collective-permute-start.1 = (f32[192,128]{1,0:T(8,128)S(1)}, f32[192,128]{1,0:T(8,128)S(1)}, u32[]{:S(2)}, u32[]{:S(2)}) collective-permute-start(f32[192,128]{1,0:T(8,128)S(1)} %get-tuple-element.22), channel_id=1, source_target_pairs={{8,0},{16,8},{24,16},{32,24},{40,32},{48,40},{56,48},{64,56},{72,6... | collective-permute-start | bytes 294920 | tf_op jit(solution)/shard_map/ppermute | solution.py:497

commit v5 on v4

--- a/solution.py
+++ b/solution.py
@@ -11,6 +11,7 @@
 FOCAL_CURRENT = 16.0
 TILE = 128
 CHUNK = 16
+GROUP = 4
 MIB = 1024 * 1024
 
 RIM = 8
@@ -48,7 +49,7 @@
     lax.fori_loop(first, chunks, one, 0)
 
 
-def keep_rows(src, dst, which, rows, chunks):
+def keep_rows(src, dst, which, rows, chunks, first=0):
     def one(c, _):
         for r in which:
             at = pl.ds(c * (CHUNK * rows) + r, CHUNK, stride=rows)
@@ -56,7 +57,7 @@
                 dst.at[t][at, :] = src.at[t][at, :]
         return 0
 
-    lax.fori_loop(0, chunks, one, 0)
+    lax.fori_loop(first, chunks, one, 0)
 
 
 def split_rows(src, dst, which, tiles_hbm, tiles, sems, parts, rows):
@@ -162,24 +163,20 @@
     base_row = where[0]
     cells_of_pairs.wait()
 
+    def is_near(cell):
+        return (cell >= (base_row - 2) * cols) & (cell < (base_row + rows + 2) * cols)
+
     def listed(k, s):
-        row = [lax.div(focal[end, k], cols) for end in range(2)]
-        a, b = row[0] - base_row, row[1] - base_row
-        near = ((a >= -2) & (a < rows + 2)) | ((b >= -2) & (b < rows + 2))
+        near = is_near(focal[0, k]) | is_near(focal[1, k])
         index[k] = jnp.where(near, s, 0)
-
-        @pl.when(near)
-        def _():
-            index[pairs + s] = k
-            index[pairs + slots + 2 * s] = a
-            index[pairs + slots + 2 * s + 1] = b
-            index[pairs + 3 * slots + 2 * s] = focal[0, k] - row[0] * cols
-            index[pairs + 3 * slots + 2 * s + 1] = focal[1, k] - row[1] * cols
-
+        index[pairs + s] = k
         return s + near.astype(jnp.int32)
 
-    count = lax.fori_loop(0, pairs, listed, jnp.int32(1))
+    index[pairs] = pairs
+    count = lax.fori_loop(0, pairs, listed, jnp.int32(1), unroll=8)
     index[pairs + 5 * slots] = count
+    for n in range(GROUP):
+        index[pairs + count + n] = pairs
     chunks = (count + CHUNK - 1) // CHUNK
 
     for copy in arrivals:
@@ -191,8 +188,12 @@
     def one(s, _):
         store(field, pl.ds(s * rows, rows), background)
         for end in range(2):
-            i = index[pairs + slots + 2 * s + end]
-            j = index[pairs + 3 * slots + 2 * s + end]
+            cell = focal[end, index[pairs + s]]
+            i = lax.div(cell, cols)
+            j = cell - i * cols
+            i = i - base_row
+            index[pairs + slots + 2 * s + end] = i
+            index[pairs + 3 * slots + 2 * s + end] = j
 
             @pl.when((i >= 0) & (i < rows))
             def _():
@@ -287,14 +288,16 @@
     outer,
     weights,
     rim_weights,
-    one_two,
-    three_four,
-    *,
+    kept_sem,
+    *by_pair,
     rows,
     cols,
     pairs,
     slots,
 ):
+    first_chunk = pl.ds(0, CHUNK * rows)
+    kept = pltpu.make_async_copy(inner_second.at[:, first_chunk, :], second.at[:, first_chunk, :], kept_sem)
+    kept.start()
     count = index[pairs + 5 * slots]
     chunks = (count + CHUNK - 1) // CHUNK
     active, valid, grounded = (cells[n * rows : (n + 1) * rows, :] for n in range(3))
@@ -330,18 +333,6 @@
         rim_weights[n * 8 : n * 8 + 2, :] = all_rim_weights[n]
     shared = jnp.concatenate([told(above, 0), told(above, 1), told(below, 0), told(below, 1)], axis=0)
 
-    def first_image(s, _):
-        at = s * RIM
-        z = load(pre, pl.ds(s * rows, rows))
-        z_two = load(outer, pl.ds(at + 1, 2))
-        w = [weights[n * rows : (n + 1) * rows, :] for n in range(5)]
-        store(image, pl.ds(s * rows, rows), operator(z, *stacked(z, own(z_two, 0), own(z_two, 1)), w))
-        w = [rim_weights[n * 8 : n * 8 + 2, :] for n in range(5)]
-        up = two(load(outer, pl.ds(at, 1)), own(z, rows - 1))
-        down = two(own(z, 0), load(outer, pl.ds(at + 3, 1)))
-        store(outer, pl.ds(at + 4, 2), operator(z_two, up, down, w))
-        return 0
-
     def near(s, _):
         k = index[pairs + s]
         store(outer, pl.ds(s * RIM, 4), shared)
@@ -356,14 +347,29 @@
                     at = pl.ds(s * RIM + i - first + place, 1)
                     outer[t, at, :] = outer[t, at, :] + sign * rim[pl.ds(end * pairs + k, 1), :]
 
-        return first_image(s, 0)
+        return 0
 
     store(outer, slice(0, 4), shared)
-    first_image(0, 0)
     lax.fori_loop(1, count, near, 0)
 
-    keep_rows(inner_second, second, range(1, rows - 1), rows, chunks)
-    apply_tiles(image, second, [(0, parts, 0), (rows - 1, parts, 3)], rows, chunks)
+    def first_image(g, _):
+        for s in [g * GROUP + n for n in range(GROUP)]:
+            at = s * RIM
+            z = load(pre, pl.ds(s * rows, rows))
+            z_two = load(outer, pl.ds(at + 1, 2))
+            w = [weights[n * rows : (n + 1) * rows, :] for n in range(5)]
+            store(image, pl.ds(s * rows, rows), operator(z, *stacked(z, own(z_two, 0), own(z_two, 1)), w))
+            w = [rim_weights[n * 8 : n * 8 + 2, :] for n in range(5)]
+            up = two(load(outer, pl.ds(at, 1)), own(z, rows - 1))
+            down = two(own(z, 0), load(outer, pl.ds(at + 3, 1)))
+            store(outer, pl.ds(at + 4, 2), operator(z_two, up, down, w))
+        return 0
+
+    groups = (count + GROUP - 1) // GROUP
+    lax.fori_loop(0, groups, first_image, 0)
+
+    kept.wait()
+    keep_rows(inner_second, second, range(1, rows - 1), rows, chunks, 1)
 
     def outer_tiles(c, _):
         for tiles, row in ((tiles_above, 4), (tiles_below, 5)):
@@ -372,6 +378,10 @@
             for t in range(cols // TILE):
                 pair = jnp.concatenate(cut(tiles[0, t]), axis=1)
                 outer.at[t][to, :] = times_tile(outer.at[t][at, :], pair)
+        for r, n in ((0, 0), (rows - 1, 3)):
+            at = pl.ds(c * (CHUNK * rows) + r, CHUNK, stride=rows)
+            for t in range(cols // TILE):
+                second.at[t][at, :] = times_tile(image.at[t][at, :], parts[n, t])
         return 0
 
     lax.fori_loop(0, chunks, outer_tiles, 0)
@@ -391,24 +401,25 @@
         z, i = load(pre, at), load(image, at)
         return folded(load(field, at) * z), folded(z * i), folded(i * u), folded(u * v)
 
-    a, b, c, d = four(0)
-    one_two[0:pairs, :] = jnp.broadcast_to(a, (pairs, TILE))
-    one_two[pairs : 2 * pairs, :] = jnp.broadcast_to(b, (pairs, TILE))
-    three_four[0:pairs, :] = jnp.broadcast_to(c, (pairs, TILE))
-    three_four[pairs : 2 * pairs, :] = jnp.broadcast_to(d, (pairs, TILE))
-
-    def one(s, _):
-        k = index[pairs + s]
-        a, b, c, d = four(s)
-        one_two[pl.ds(k, 1), :] = a
-        one_two[pl.ds(pairs + k, 1), :] = b
-        three_four[pl.ds(k, 1), :] = c
-        three_four[pl.ds(pairs + k, 1), :] = d
-        return 0
-
-    lax.fori_loop(1, count, one, 0)
-    sums[0:1, :] = jnp.sum(one_two[...].T, axis=0, keepdims=True)
-    sums[1:2, :] = jnp.sum(three_four[...].T, axis=0, keepdims=True)
+    def group(g, shared):
+        members = [g * GROUP + n for n in range(GROUP)]
+        sums_of = [four(s) for s in members]
+        if shared:
+            for part, x in zip(by_pair, sums_of[0]):
+                part[...] = jnp.broadcast_to(x, part.shape)
+        for s, four_sums in zip(members, sums_of):
+            for part, x in zip(by_pair, four_sums):
+                part[pl.ds(index[pairs + s], 1), :] = x
+
+    def later(g, _):
+        group(g, False)
+        return 0
+
+    group(0, True)
+    lax.fori_loop(1, groups, later, 0)
+    for n in range(2):
+        both = jnp.concatenate([by_pair[2 * n + m][0:pairs, :] for m in range(2)], axis=0)
+        sums[n : n + 1, :] = jnp.sum(both.T, axis=0, keepdims=True)
 
 
 def finish_kernel(
@@ -584,8 +595,8 @@
             pltpu.VMEM((cols // TILE, slots * RIM, TILE), f32),
             pltpu.VMEM((5 * rows, cols), f32),
             pltpu.VMEM((5 * 8, cols), f32),
-            pltpu.VMEM((2 * pairs, TILE), f32),
-            pltpu.VMEM((2 * pairs, TILE), f32),
+            pltpu.SemaphoreType.DMA,
+            *[pltpu.VMEM((pairs + 8, TILE), f32)] * 4,
         ],
         compiler_params=limit,
         name="middle",

time: 98.6 us -> 97 us (0.984)
  Pallas kernels: 14.7 us -> 12.3 us
    pallas_call x1, Pallas kernels: 3.25 us -> 2.17 us  [on_device(): pl.pallas_call(functools.partial(middle_kernel, **sizes), in_specs=[smem(...]
    pallas_call x1, Pallas kernels: 4.39 us -> 3.33 us  [on_device(): pl.pallas_call(functools.partial(start_kernel, **sizes), in_specs=[smem()...]
  transfers between devices with their start and end apart: 4 -> 4, of which waited for: 1 -> 2; matrix products, arithmetic and copies ran while one was open for 0% -> 0% of each run, Pallas kernels for 8% -> 7%
where the time goes in v5:
time: 97 us; the launch traced here: 96.3 us
  blocking collectives  66.9 us (69%)
  starting transfers between devices  12.7 us (13%)
  Pallas kernels  12.3 us (13%)
  waiting for transfers between devices  2.39 us (2%)
  local copies, waits for them, and re-layouts  1.28 us (1%)
    all_to_all x1, blocking collectives, on_device(): lax.all_to_all(copies, 'space', split_axis=0, concat_axis=0, tiled=True)  66.9 us
    ppermute x2, starting transfers between devices, neighbours(): lax.ppermute(down, 'space', [(i, (i + 1) % count) for i in range(ends)])  10.1 us
    pallas_call x1, Pallas kernels, on_device(): pl.pallas_call(functools.partial(inner_kernel, **sizes), in_specs=[smem()...  3.59 us
    pallas_call x1, Pallas kernels, on_device(): pl.pallas_call(functools.partial(start_kernel, **sizes), in_specs=[smem()...  3.33 us
    pallas_call x1, Pallas kernels, on_device(): pl.pallas_call(functools.partial(finish_kernel, rows=rows, cols=cols, pai...  3.25 us
    ppermute x2, starting transfers between devices, neighbours(): lax.ppermute(up, 'space', [((i + 1) % count, i) for i in range(ends)])  2.62 us
    pallas_call x1, Pallas kernels, on_device(): pl.pallas_call(functools.partial(middle_kernel, **sizes), in_specs=[smem(...  2.17 us
    ppermute x2, waiting for transfers between devices, neighbours(): lax.ppermute(up, 'space', [((i + 1) % count, i) for i in range(ends)])  2.04 us
  transfers between devices with their start and end apart: 4, of which 2 were waited for; matrix products, arithmetic and copies ran while one was open for 0% of the time, Pallas kernels for 7%

profile of v5, /device:TPU:40, one launch (start us, length us, event | category | flops | bytes accessed | tf_op | source)
XLA Modules:
  0.0 96.3 jit_solution(8285630745310869279)
XLA Ops:
  0.6 1.3 %fusion = (f32[1,8,128,128]{3,2,1,0:T(8,128)S(1)}, f32[1,8,128,128]{3,2,1,0:T(8,128)S(1)}) fusion(f32[8,8,128,128]{3,2,1,0:T(8,128)} %tiles_hbm.3), kind=kLoop, calls=%fused_computation | loop fusion | bytes 2097152 | tf_op jit(solution)/shard_map/slice | solution.py:527
  1.9 1.3 %collective-permute-start.3 = (f32[1,8,128,128]{3,2,1,0:T(8,128)S(1)}, f32[1,8,128,128]{3,2,1,0:T(8,128)S(1)}, u32[]{:S(2)}, u32[]{:S(2)}) collective-permute-start(f32[1,8,128,128]{3,2,1,0:T(8,128)S(1)} %get-tuple-element.28), channel_id=1, source_target_pairs={{8,0},{16,8},{24,16},{32,24},{40,32},{48,40},{56,48},{64,56},{72,6... | collective-permute-start | bytes 1572872 | tf_op jit(solution)/shard_map/ppermute | solution.py:508
  3.2 5.4 %collective-permute-start.2 = (f32[1,8,128,128]{3,2,1,0:T(8,128)S(1)}, f32[1,8,128,128]{3,2,1,0:T(8,128)S(1)}, u32[]{:S(2)}, u32[]{:S(2)}) collective-permute-start(f32[1,8,128,128]{3,2,1,0:T(8,128)S(1)} %get-tuple-element.29), channel_id=1, source_target_pairs={{0,8},{8,16},{16,24},{24,32},{32,40},{40,48},{48,56},{56,64},{64,7... | collective-permute-start | bytes 1572872 | tf_op jit(solution)/shard_map/ppermute | solution.py:507
  8.6 3.3 %start.1 = (f32[8,640,128]{2,1,0:T(8,128)S(1)}, f32[8,640,128]{2,1,0:T(8,128)S(1)}, s32[472]{0:T(512)S(1)}, bf16[4,8,128,256]{3,2,1,0:T(8,128)(2,1)S(1)}, f32[24...) custom-call(s32[1]{0:T(128)} %bitcast.where, s32[2,64]{1,0:T(2,128)} %bitcast.2, ...), custom_call_target="tpu_custom_call" | custom-call | tf_op jit(solution)/shard_map/start/pallas_call | solution.py:528
  12.0 4.7 %collective-permute-start = (f32[192,128]{1,0:T(8,128)S(1)}, f32[192,128]{1,0:T(8,128)S(1)}, u32[]{:S(2)}, u32[]{:S(2)}) collective-permute-start(f32[192,128]{1,0:T(8,128)S(1)} %get-tuple-element.21), channel_id=1, source_target_pairs={{0,8},{8,16},{16,24},{24,32},{32,40},{40,48},{48,56},{56,64},{64,7... | collective-permute-start | bytes 294920 | tf_op jit(solution)/shard_map/ppermute | solution.py:507
  16.7 1.3 %collective-permute-start.1 = (f32[192,128]{1,0:T(8,128)S(1)}, f32[192,128]{1,0:T(8,128)S(1)}, u32[]{:S(2)}, u32[]{:S(2)}) collective-permute-start(f32[192,128]{1,0:T(8,128)S(1)} %get-tuple-element.22), channel_id=1, source_target_pairs={{8,0},{16,8},{24,16},{32,24},{40,32},{48,40},{56,48},{64,56},{72,6... | collective-permute-start | bytes 294920 | tf_op jit(solution)/shard_map/ppermute | solution.py:508
  18.0 3.6 %inner.1 = (f32[8,640,128]{2,1,0:T(8,128)S(1)}, f32[8,640,128]{2,1,0:T(8,128)S(1)}) custom-call(s32[472]{0:T(512)S(1)} %get-tuple-element.15.index, f32[24,1024]{1,0:T(8,128)S(1)} %get-tuple-element.16.cells, f32[8,640,128]{2,1,0:T(8,128)S(1)} %get-tuple-element.17.field, bf16[4,8,128,256]{3,2,1,0:T(8,128)(2,1)S(1)} %get-tuple-element.18.parts, ...), custom_call_target="tpu_custom_call" | custom-call | tf_op jit(solution)/shard_map/inner/pallas_call | solution.py:574
  21.6 0.4 collective-permute-done.above
  21.9 2.0 %collective-permute-done.1.below = f32[192,128]{1,0:T(8,128)S(1)} collective-permute-done((f32[192,128]{1,0:T(8,128)S(1)}, f32[192,128]{1,0:T(8,128)S(1)}, u32[]{:S(2)}, u32[]{:S(2)}) %collective-permute-start.1) | collective-permute-done | bytes 98336 | tf_op jit(solution)/shard_map/ppermute | solution.py:508
  24.0 0.0 collective-permute-done.3.tiles_below
  24.0 0.0 collective-permute-done.2.tiles_above
  24.0 2.2 %middle.1 = (f32[8,640,128]{2,1,0:T(8,128)S(1)}, f32[8,640,128]{2,1,0:T(8,128)S(1)}, f32[8,640,128]{2,1,0:T(8,128)S(1)}, f32[2,128]{1,0:T(2,128)S(1)}) custom-call(s32[472]{0:T(512)S(1)} %get-tuple-element.15.index, f32[24,1024]{1,0:T(8,128)S(1)} %get-tuple-element.16.cells, f32[8,640,128]{2,1,0:T(8,128)S(1)} %get-tuple-element.17.field, ...), custom_call_target="tpu_custom_call" | custom-call | tf_op jit(solution)/shard_map/middle/pallas_call | solution.py:589
  26.2 66.9 %all_to_all.5.everyone = f32[32,2,128]{2,1,0:T(2,128)S(1)} all-to-all(f32[32,2,128]{2,1,0:T(2,128)S(1)} %broadcast_in_dim.3), channel_id=1, replica_groups=mesh['groups'=2,'space'=32,'rhs'=8] {'space'}, dimensions={0} | all-to-all | bytes 65536 | tf_op jit(solution)/shard_map/all_to_all | solution.py:605
  93.0 3.2 %finish.1 = (f32[64,8,1024]{2,1,0:T(8,128)}, f32[64,8,1024]{2,1,0:T(8,128)}) custom-call(s32[472]{0:T(512)S(1)} %get-tuple-element.15.index, f32[32,2,128]{2,1,0:T(2,128)S(1)} %all_to_all.5.everyone, f32[8,640,128]{2,1,0:T(8,128)S(1)} %get-tuple-element.17.field, f32[8,640,128]{2,1,0:T(8,128)S(1)} %get-tuple-element.20.pre, ...), custom_call_target="tpu_custom_call" | custom-call | tf_op jit(solution)/shard_map/finish/pallas_call | solution.py:609
  (1 shorter events, 0.0 us)
Async XLA Ops:
  1.9 22.1 %collective-permute-start.3 = (f32[1,8,128,128]{3,2,1,0:T(8,128)S(1)}, f32[1,8,128,128]{3,2,1,0:T(8,128)S(1)}, u32[]{:S(2)}, u32[]{:S(2)}) collective-permute-start(f32[1,8,128,128]{3,2,1,0:T(8,128)S(1)} %get-tuple-element.28), channel_id=1, source_target_pairs={{8,0},{16,8},{24,16},{32,24},{40,32},{48,40},{56,48},{64,56},{72,6... | collective-permute-start | bytes 1572872 | tf_op jit(solution)/shard_map/ppermute | solution.py:508
  3.2 20.7 %collective-permute-start.2 = (f32[1,8,128,128]{3,2,1,0:T(8,128)S(1)}, f32[1,8,128,128]{3,2,1,0:T(8,128)S(1)}, u32[]{:S(2)}, u32[]{:S(2)}) collective-permute-start(f32[1,8,128,128]{3,2,1,0:T(8,128)S(1)} %get-tuple-element.29), channel_id=1, source_target_pairs={{0,8},{8,16},{16,24},{24,32},{32,40},{40,48},{48,56},{56,64},{64,7... | collective-permute-start | bytes 1572872 | tf_op jit(solution)/shard_map/ppermute | solution.py:507
  12.0 10.0 %collective-permute-start = (f32[192,128]{1,0:T(8,128)S(1)}, f32[192,128]{1,0:T(8,128)S(1)}, u32[]{:S(2)}, u32[]{:S(2)}) collective-permute-start(f32[192,128]{1,0:T(8,128)S(1)} %get-tuple-element.21), channel_id=1, source_target_pairs={{0,8},{8,16},{16,24},{24,32},{32,40},{40,48},{48,56},{56,64},{64,7... | collective-permute-start | bytes 294920 | tf_op jit(solution)/shard_map/ppermute | solution.py:507
  16.7 7.3 %collective-permute-start.1 = (f32[192,128]{1,0:T(8,128)S(1)}, f32[192,128]{1,0:T(8,128)S(1)}, u32[]{:S(2)}, u32[]{:S(2)}) collective-permute-start(f32[192,128]{1,0:T(8,128)S(1)} %get-tuple-element.22), channel_id=1, source_target_pairs={{8,0},{16,8},{24,16},{32,24},{40,32},{48,40},{56,48},{64,56},{72,6... | collective-permute-start | bytes 294920 | tf_op jit(solution)/shard_map/ppermute | solution.py:508

commit v6 on v5

--- a/solution.py
+++ b/solution.py
@@ -10,6 +10,7 @@
 LEAKAGE = 0.05
 FOCAL_CURRENT = 16.0
 TILE = 128
+HALF = TILE // 2
 CHUNK = 16
 GROUP = 4
 MIB = 1024 * 1024
@@ -104,6 +105,39 @@
     north, south, west, east = edges
     diag = valid * (LEAKAGE + grounded) + (1.0 - valid) + north + south + west + east
     return diag, north, south, west, east
+
+
+def below_diagonal():
+    row = lax.broadcasted_iota(jnp.int32, (HALF, TILE), 0)
+    lane = lax.broadcasted_iota(jnp.int32, (HALF, TILE), 1)
+    return lane < row, lane == row + HALF
+
+
+def pack_kernel(tiles_hbm, up_ref, down_ref, tiles, sems, *, rows):
+    copies = [pltpu.make_async_copy(tiles_hbm.at[r], tiles.at[n], sems.at[n]) for n, r in enumerate((0, rows - 1))]
+    for copy in copies:
+        copy.start()
+    moved, diagonal = below_diagonal()
+    count = tiles.shape[1]
+    for n, packed in enumerate((up_ref, down_ref)):
+        copies[n].wait()
+        for t in range(count):
+            upper, lower = tiles[n, t, :HALF, :], tiles[n, t, HALF:, :]
+            packed[t * HALF : (t + 1) * HALF, :] = jnp.where(moved, pltpu.roll(lower, HALF, 1), upper)
+            at = count * HALF + t
+            packed[at : at + 1, :] = jnp.sum(jnp.where(diagonal, lower, 0.0), axis=0, keepdims=True)
+
+
+def unpacked(packed, t, count):
+    x = packed[t * HALF : (t + 1) * HALF, :]
+    diagonal = packed[count * HALF + t : count * HALF + t + 1, :]
+    moved, _ = below_diagonal()
+    top = jnp.where(moved, 0.0, x)
+    bottom = pltpu.roll(jnp.where(moved, x, 0.0), HALF, 1)
+    half = jnp.concatenate([top, bottom], axis=0)
+    row = lax.broadcasted_iota(jnp.int32, (TILE, TILE), 0)
+    lane = lax.broadcasted_iota(jnp.int32, (TILE, TILE), 1)
+    return jnp.where(row == lane, jnp.where(row < HALF, half, diagonal), half + half.T)
 
 
 def start_kernel(
@@ -376,7 +410,7 @@
             at = pl.ds(c * (CHUNK * RIM) + row, CHUNK, stride=RIM)
             to = pl.ds(c * (CHUNK * RIM) + row + 2, CHUNK, stride=RIM)
             for t in range(cols // TILE):
-                pair = jnp.concatenate(cut(tiles[0, t]), axis=1)
+                pair = jnp.concatenate(cut(unpacked(tiles, t, cols // TILE)), axis=1)
                 outer.at[t][to, :] = times_tile(outer.at[t][at, :], pair)
         for r, n in ((0, 0), (rows - 1, 3)):
             at = pl.ds(c * (CHUNK * rows) + r, CHUNK, stride=rows)
@@ -524,7 +558,16 @@
     def shaped(shape, dtype=f32):
         return jax.ShapeDtypeStruct(shape, dtype)
 
-    tiles_above, tiles_below = neighbours(tile_inverse[:1], tile_inverse[rows - 1 :])
+    up, down = pl.pallas_call(
+        functools.partial(pack_kernel, rows=rows),
+        in_specs=[hbm()],
+        out_specs=[vmem()] * 2,
+        out_shape=[shaped((cols // TILE * (HALF + 1), TILE))] * 2,
+        scratch_shapes=[pltpu.VMEM((2, *per_row), f32), pltpu.SemaphoreType.DMA((2,))],
+        compiler_params=limit,
+        name="pack",
+    )(pltpu.with_memory_space_constraint(tile_inverse, pltpu.HBM))
+    tiles_above, tiles_below = neighbours(up, down)
     field, pre, index, parts, cells, up, down = pl.pallas_call(
         functools.partial(start_kernel, **sizes),
         in_specs=[smem(), *[hbm()] * 8],

time: 97 us -> 98.2 us (1.012)
  local copies, waits for them, and re-layouts: 1.28 us -> 0.01 us
  Pallas kernels: 12.3 us -> 13.5 us
  blocking collectives: 66.9 us -> 68.1 us
    pallas_call x0 -> x1, Pallas kernels: none -> 1.35 us  [on_device(): pl.pallas_call(functools.partial(pack_kernel, rows=rows), in_specs=[hbm()...]
    slice x1 -> x0, local copies, waits for them, and re-layouts: 1.27 us -> none  [on_device(): tile_inverse[:1]]
    all_to_all x1, blocking collectives: 66.9 us -> 68.1 us  [on_device(): lax.all_to_all(copies, 'space', split_axis=0, concat_axis=0, tiled=True)]
  transfers between devices with their start and end apart: 4 -> 4, of which waited for: 2 -> 1; matrix products, arithmetic and copies ran while one was open for 0% -> 0% of each run, Pallas kernels for 7% -> 7%
where the time goes in v6:
time: 98.2 us; the launch traced here: 97.9 us
  blocking collectives  68.1 us (69%)
  Pallas kernels  13.5 us (14%)
  starting transfers between devices  13.2 us (13%)
  waiting for transfers between devices  2.42 us (2%)
    all_to_all x1, blocking collectives, on_device(): lax.all_to_all(copies, 'space', split_axis=0, concat_axis=0, tiled=True)  68.1 us
    ppermute x2, starting transfers between devices, neighbours(): lax.ppermute(down, 'space', [(i, (i + 1) % count) for i in range(ends)])  10.6 us
    pallas_call x1, Pallas kernels, on_device(): pl.pallas_call(functools.partial(inner_kernel, **sizes), in_specs=[smem()...  3.5 us
    pallas_call x1, Pallas kernels, on_device(): pl.pallas_call(functools.partial(finish_kernel, rows=rows, cols=cols, pai...  3.25 us
    pallas_call x1, Pallas kernels, on_device(): pl.pallas_call(functools.partial(start_kernel, **sizes), in_specs=[smem()...  3.25 us
    ppermute x2, starting transfers between devices, neighbours(): lax.ppermute(up, 'space', [((i + 1) % count, i) for i in range(ends)])  2.62 us
    ppermute x2, waiting for transfers between devices, neighbours(): lax.ppermute(up, 'space', [((i + 1) % count, i) for i in range(ends)])  2.41 us
    pallas_call x1, Pallas kernels, on_device(): pl.pallas_call(functools.partial(middle_kernel, **sizes), in_specs=[smem(...  2.17 us
  transfers between devices with their start and end apart: 4, of which 1 were waited for; matrix products, arithmetic and copies ran while one was open for 0% of the time, Pallas kernels for 7%

profile of v6, /device:TPU:40, one launch (start us, length us, event | category | flops | bytes accessed | tf_op | source)
XLA Modules:
  0.0 97.9 jit_solution(16574243889422810887)
XLA Ops:
  0.6 1.4 %pack.1 = (f32[520,128]{1,0:T(8,128)S(1)}, f32[520,128]{1,0:T(8,128)S(1)}) custom-call(f32[8,8,128,128]{3,2,1,0:T(8,128)} %tiles_hbm.5), custom_call_target="tpu_custom_call" | custom-call | tf_op jit(solution)/shard_map/pack/pallas_call | solution.py:561
  2.0 4.7 %collective-permute-start.2 = (f32[520,128]{1,0:T(8,128)S(1)}, f32[520,128]{1,0:T(8,128)S(1)}, u32[]{:S(2)}, u32[]{:S(2)}) collective-permute-start(f32[520,128]{1,0:T(8,128)S(1)} %get-tuple-element.25), channel_id=1, source_target_pairs={{0,8},{8,16},{16,24},{24,32},{32,40},{40,48},{48,56},{56,64},{64,7... | collective-permute-start | bytes 798728 | tf_op jit(solution)/shard_map/ppermute | solution.py:541
  6.7 1.3 %collective-permute-start.3 = (f32[520,128]{1,0:T(8,128)S(1)}, f32[520,128]{1,0:T(8,128)S(1)}, u32[]{:S(2)}, u32[]{:S(2)}) collective-permute-start(f32[520,128]{1,0:T(8,128)S(1)} %get-tuple-element.26), channel_id=1, source_target_pairs={{8,0},{16,8},{24,16},{32,24},{40,32},{48,40},{56,48},{64,56},{72,6... | collective-permute-start | bytes 798728 | tf_op jit(solution)/shard_map/ppermute | solution.py:542
  8.0 3.2 %start.1 = (f32[8,640,128]{2,1,0:T(8,128)S(1)}, f32[8,640,128]{2,1,0:T(8,128)S(1)}, s32[472]{0:T(512)S(1)}, bf16[4,8,128,256]{3,2,1,0:T(8,128)(2,1)S(1)}, f32[24...) custom-call(s32[1]{0:T(128)} %bitcast.where, s32[2,64]{1,0:T(2,128)} %bitcast.2, ...), custom_call_target="tpu_custom_call" | custom-call | tf_op jit(solution)/shard_map/start/pallas_call | solution.py:571
  11.3 5.8 %collective-permute-start = (f32[192,128]{1,0:T(8,128)S(1)}, f32[192,128]{1,0:T(8,128)S(1)}, u32[]{:S(2)}, u32[]{:S(2)}) collective-permute-start(f32[192,128]{1,0:T(8,128)S(1)} %get-tuple-element.23), channel_id=1, source_target_pairs={{0,8},{8,16},{16,24},{24,32},{32,40},{40,48},{48,56},{56,64},{64,7... | collective-permute-start | bytes 294920 | tf_op jit(solution)/shard_map/ppermute | solution.py:541
  17.1 1.3 %collective-permute-start.1 = (f32[192,128]{1,0:T(8,128)S(1)}, f32[192,128]{1,0:T(8,128)S(1)}, u32[]{:S(2)}, u32[]{:S(2)}) collective-permute-start(f32[192,128]{1,0:T(8,128)S(1)} %get-tuple-element.24), channel_id=1, source_target_pairs={{8,0},{16,8},{24,16},{32,24},{40,32},{48,40},{56,48},{64,56},{72,6... | collective-permute-start | bytes 294920 | tf_op jit(solution)/shard_map/ppermute | solution.py:542
  18.4 3.5 %inner.1 = (f32[8,640,128]{2,1,0:T(8,128)S(1)}, f32[8,640,128]{2,1,0:T(8,128)S(1)}) custom-call(s32[472]{0:T(512)S(1)} %get-tuple-element.17.index, f32[24,1024]{1,0:T(8,128)S(1)} %get-tuple-element.18.cells, f32[8,640,128]{2,1,0:T(8,128)S(1)} %get-tuple-element.19.field, bf16[4,8,128,256]{3,2,1,0:T(8,128)(2,1)S(1)} %get-tuple-element.20.parts, ...), custom_call_target="tpu_custom_call" | custom-call | tf_op jit(solution)/shard_map/inner/pallas_call | solution.py:617
  22.0 0.0 collective-permute-done.above
  22.0 2.4 %collective-permute-done.1.below = f32[192,128]{1,0:T(8,128)S(1)} collective-permute-done((f32[192,128]{1,0:T(8,128)S(1)}, f32[192,128]{1,0:T(8,128)S(1)}, u32[]{:S(2)}, u32[]{:S(2)}) %collective-permute-start.1) | collective-permute-done | bytes 98336 | tf_op jit(solution)/shard_map/ppermute | solution.py:542
  24.4 0.0 collective-permute-done.2.tiles_above
  24.4 0.0 collective-permute-done.3.tiles_below
  24.4 2.2 %middle.1 = (f32[8,640,128]{2,1,0:T(8,128)S(1)}, f32[8,640,128]{2,1,0:T(8,128)S(1)}, f32[8,640,128]{2,1,0:T(8,128)S(1)}, f32[2,128]{1,0:T(2,128)S(1)}) custom-call(s32[472]{0:T(512)S(1)} %get-tuple-element.17.index, f32[24,1024]{1,0:T(8,128)S(1)} %get-tuple-element.18.cells, f32[8,640,128]{2,1,0:T(8,128)S(1)} %get-tuple-element.19.field, ...), custom_call_target="tpu_custom_call" | custom-call | tf_op jit(solution)/shard_map/middle/pallas_call | solution.py:632
  26.6 68.1 %all_to_all.5.everyone = f32[32,2,128]{2,1,0:T(2,128)S(1)} all-to-all(f32[32,2,128]{2,1,0:T(2,128)S(1)} %broadcast_in_dim.3), channel_id=1, replica_groups=mesh['groups'=2,'space'=32,'rhs'=8] {'space'}, dimensions={0} | all-to-all | bytes 65536 | tf_op jit(solution)/shard_map/all_to_all | solution.py:648
  94.7 3.2 %finish.1 = (f32[64,8,1024]{2,1,0:T(8,128)}, f32[64,8,1024]{2,1,0:T(8,128)}) custom-call(s32[472]{0:T(512)S(1)} %get-tuple-element.17.index, f32[32,2,128]{2,1,0:T(2,128)S(1)} %all_to_all.5.everyone, f32[8,640,128]{2,1,0:T(8,128)S(1)} %get-tuple-element.19.field, f32[8,640,128]{2,1,0:T(8,128)S(1)} %get-tuple-element.22.pre, ...), custom_call_target="tpu_custom_call" | custom-call | tf_op jit(solution)/shard_map/finish/pallas_call | solution.py:652
  (1 shorter events, 0.0 us)
Async XLA Ops:
  2.0 22.4 %collective-permute-start.2 = (f32[520,128]{1,0:T(8,128)S(1)}, f32[520,128]{1,0:T(8,128)S(1)}, u32[]{:S(2)}, u32[]{:S(2)}) collective-permute-start(f32[520,128]{1,0:T(8,128)S(1)} %get-tuple-element.25), channel_id=1, source_target_pairs={{0,8},{8,16},{16,24},{24,32},{32,40},{40,48},{48,56},{56,64},{64,7... | collective-permute-start | bytes 798728 | tf_op jit(solution)/shard_map/ppermute | solution.py:541
  6.7 17.7 %collective-permute-start.3 = (f32[520,128]{1,0:T(8,128)S(1)}, f32[520,128]{1,0:T(8,128)S(1)}, u32[]{:S(2)}, u32[]{:S(2)}) collective-permute-start(f32[520,128]{1,0:T(8,128)S(1)} %get-tuple-element.26), channel_id=1, source_target_pairs={{8,0},{16,8},{24,16},{32,24},{40,32},{48,40},{56,48},{64,56},{72,6... | collective-permute-start | bytes 798728 | tf_op jit(solution)/shard_map/ppermute | solution.py:542
  11.3 10.7 %collective-permute-start = (f32[192,128]{1,0:T(8,128)S(1)}, f32[192,128]{1,0:T(8,128)S(1)}, u32[]{:S(2)}, u32[]{:S(2)}) collective-permute-start(f32[192,128]{1,0:T(8,128)S(1)} %get-tuple-element.23), channel_id=1, source_target_pairs={{0,8},{8,16},{16,24},{24,32},{32,40},{40,48},{48,56},{56,64},{64,7... | collective-permute-start | bytes 294920 | tf_op jit(solution)/shard_map/ppermute | solution.py:541
  17.1 7.2 %collective-permute-start.1 = (f32[192,128]{1,0:T(8,128)S(1)}, f32[192,128]{1,0:T(8,128)S(1)}, u32[]{:S(2)}, u32[]{:S(2)}) collective-permute-start(f32[192,128]{1,0:T(8,128)S(1)} %get-tuple-element.24), channel_id=1, source_target_pairs={{8,0},{16,8},{24,16},{32,24},{40,32},{48,40},{56,48},{64,56},{72,6... | collective-permute-start | bytes 294920 | tf_op jit(solution)/shard_map/ppermute | solution.py:542

commit v7 on v6

--- a/solution.py
+++ b/solution.py
@@ -6,6 +6,7 @@
 from jax.experimental import pallas as pl
 from jax.experimental.pallas import tpu as pltpu
 from jax.sharding import PartitionSpec as P
+
 
 LEAKAGE = 0.05
 FOCAL_CURRENT = 16.0
@@ -61,9 +62,10 @@
     lax.fori_loop(first, chunks, one, 0)
 
 
-def split_rows(src, dst, which, tiles_hbm, tiles, sems, parts, rows):
+def split_rows(src, dst, which, tiles, parts, rows, copies=None):
     for n, r in enumerate(which):
-        pltpu.make_async_copy(tiles_hbm.at[r], tiles.at[n], sems.at[n]).wait()
+        if copies is not None:
+            copies[n].wait()
         at = pl.ds(r, CHUNK, stride=rows)
         for t in range(src.shape[0]):
             pair = jnp.concatenate(cut(tiles[n, t]), axis=1)
@@ -155,6 +157,7 @@
     index,
     parts,
     cells,
+    inner_tiles,
     up_ref,
     down_ref,
     focal,
@@ -168,6 +171,7 @@
     focal_sem,
     small_sems,
     tile_sems,
+    inner_sem,
     *,
     rows,
     cols,
@@ -191,8 +195,12 @@
     ]
     for copy in arrivals:
         copy.start()
-    for n, r in enumerate(outer_rows(rows)):
-        pltpu.make_async_copy(tiles_hbm.at[r], tiles.at[n], tile_sems.at[n]).start()
+    tile_copies = [
+        pltpu.make_async_copy(tiles_hbm.at[r], tiles.at[n], tile_sems.at[n]) for n, r in enumerate(outer_rows(rows))
+    ]
+    inner_copy = pltpu.make_async_copy(tiles_hbm.at[2 : rows - 2], inner_tiles, inner_sem)
+    for copy in (*tile_copies, inner_copy):
+        copy.start()
 
     base_row = where[0]
     cells_of_pairs.wait()
@@ -247,7 +255,7 @@
     grounded = ground_mask[...].astype(jnp.float32) * ground_value[...]
     cells[2 * rows : 3 * rows, :] = grounded
 
-    split_rows(field, pre, outer_rows(rows), tiles_hbm, tiles, tile_sems, parts, rows)
+    split_rows(field, pre, outer_rows(rows), tiles, parts, rows, tile_copies)
     apply_tiles(field, pre, [(r, parts, n) for n, r in enumerate(outer_rows(rows))], rows, chunks, 1)
 
     for rim, first, outermost in ((up_ref, 0, 0), (down_ref, rows - 2, rows - 1)):
@@ -275,14 +283,13 @@
         return 0
 
     lax.fori_loop(1, count, selected, 0)
+    inner_copy.wait()
 
 
 def inner_kernel(
-    index, cells, field, parts, tiles_hbm, outer_pre, pre, second, image, tiles, inner_parts, sems, *, rows, cols, pairs, slots
+    index, cells, field, parts, tiles, outer_pre, pre, second, image, inner_parts, *, rows, cols, pairs, slots
 ):
     rest = range(2, rows - 2)
-    for n, r in enumerate(rest):
-        pltpu.make_async_copy(tiles_hbm.at[r], tiles.at[n], sems.at[n]).start()
     count = index[pairs + 5 * slots]
     chunks = (count + CHUNK - 1) // CHUNK
     active, valid, grounded = (cells[n * rows : (n + 1) * rows, :] for n in range(3))
@@ -290,7 +297,7 @@
     weights = weights_of(active, valid, grounded, stacked(active, zero, zero), stacked(valid, zero, zero))
 
     keep_rows(outer_pre, pre, outer_rows(rows), rows, chunks)
-    split_rows(field, pre, rest, tiles_hbm, tiles, sems, inner_parts, rows)
+    split_rows(field, pre, rest, tiles, inner_parts, rows)
     inner = [(r, inner_parts, n) for n, r in enumerate(rest)]
     apply_tiles(field, pre, inner, rows, chunks, 1)
 
@@ -538,8 +545,8 @@
 def neighbours(up, down):
     count = lax.axis_size("space")
     ends = count - 1
+    below = lax.ppermute(up, "space", [((i + 1) % count, i) for i in range(ends)])
     above = lax.ppermute(down, "space", [(i, (i + 1) % count) for i in range(ends)])
-    below = lax.ppermute(up, "space", [((i + 1) % count, i) for i in range(ends)])
     return above, below
 
 
@@ -568,16 +575,17 @@
         name="pack",
     )(pltpu.with_memory_space_constraint(tile_inverse, pltpu.HBM))
     tiles_above, tiles_below = neighbours(up, down)
-    field, pre, index, parts, cells, up, down = pl.pallas_call(
+    field, pre, index, parts, cells, inner_tiles, up, down = pl.pallas_call(
         functools.partial(start_kernel, **sizes),
         in_specs=[smem(), *[hbm()] * 8],
-        out_specs=[vmem(), vmem(), smem(), *[vmem()] * 4],
+        out_specs=[vmem(), vmem(), smem(), *[vmem()] * 5],
         out_shape=[
             shaped(fields),
             shaped(fields),
             shaped((pairs + 5 * slots + 8,), jnp.int32),
             shaped((4, *per_row[:2], 2 * TILE), jnp.bfloat16),
             shaped((3 * rows, cols)),
+            shaped((rows - 4, *per_row)),
             shaped(rim),
             shaped(rim),
         ],
@@ -593,6 +601,7 @@
             pltpu.SemaphoreType.DMA,
             pltpu.SemaphoreType.DMA((6,)),
             pltpu.SemaphoreType.DMA((4,)),
+            pltpu.SemaphoreType.DMA,
         ],
         compiler_params=limit,
         name="start",
@@ -616,18 +625,16 @@
 
     pre, inner_second = pl.pallas_call(
         functools.partial(inner_kernel, **sizes),
-        in_specs=[smem(), *[vmem()] * 3, hbm(), vmem()],
+        in_specs=[smem(), *[vmem()] * 5],
         out_specs=[vmem()] * 2,
         out_shape=[shaped(fields)] * 2,
         scratch_shapes=[
             pltpu.VMEM(fields, f32),
-            pltpu.VMEM((rows - 4, *per_row), f32),
             pltpu.VMEM((rows - 4, *per_row[:2], 2 * TILE), jnp.bfloat16),
-            pltpu.SemaphoreType.DMA((rows - 4,)),
         ],
         compiler_params=limit,
         name="inner",
-    )(index, cells, field, parts, pltpu.with_memory_space_constraint(tile_inverse, pltpu.HBM), pre)
+    )(index, cells, field, parts, inner_tiles, pre)
 
     image, second, last, sums = pl.pallas_call(
         functools.partial(middle_kernel, **sizes),

time: 98.2 us -> 98.2 us (level)
  waiting for transfers between devices: 2.42 us -> 3.99 us
  Pallas kernels: 13.5 us -> 12.2 us
    ppermute x2, waiting for transfers between devices: 2.41 us -> 3.99 us  [neighbours(): lax.ppermute(up, 'space', [((i + 1) % count, i) for i in range(ends)])]
    pallas_call x1, Pallas kernels: 3.5 us -> 2.16 us  [on_device(): pl.pallas_call(functools.partial(inner_kernel, **sizes), in_specs=[smem()...]
  transfers between devices with their start and end apart: 4 -> 4, of which waited for: 1 -> 1; matrix products, arithmetic and copies ran while one was open for 0% -> 0% of each run, Pallas kernels for 7% -> 6%
where the time goes in v7:
time: 98.2 us; the launch traced here: 97.8 us
  blocking collectives  67.8 us (69%)
  starting transfers between devices  13.2 us (13%)
  Pallas kernels  12.2 us (12%)
  waiting for transfers between devices  3.99 us (4%)
    all_to_all x1, blocking collectives, on_device(): lax.all_to_all(copies, 'space', split_axis=0, concat_axis=0, tiled=True)  67.8 us
    ppermute x2, starting transfers between devices, neighbours(): lax.ppermute(down, 'space', [(i, (i + 1) % count) for i in range(ends)])  10.6 us
    ppermute x2, waiting for transfers between devices, neighbours(): lax.ppermute(up, 'space', [((i + 1) % count, i) for i in range(ends)])  3.99 us
    pallas_call x1, Pallas kernels, on_device(): pl.pallas_call(functools.partial(start_kernel, **sizes), in_specs=[smem()...  3.26 us
    pallas_call x1, Pallas kernels, on_device(): pl.pallas_call(functools.partial(finish_kernel, rows=rows, cols=cols, pai...  3.25 us
    ppermute x2, starting transfers between devices, neighbours(): lax.ppermute(up, 'space', [((i + 1) % count, i) for i in range(ends)])  2.62 us
    pallas_call x1, Pallas kernels, on_device(): pl.pallas_call(functools.partial(middle_kernel, **sizes), in_specs=[smem(...  2.18 us
    pallas_call x1, Pallas kernels, on_device(): pl.pallas_call(functools.partial(inner_kernel, **sizes), in_specs=[smem()...  2.16 us
  transfers between devices with their start and end apart: 4, of which 1 were waited for; matrix products, arithmetic and copies ran while one was open for 0% of the time, Pallas kernels for 6%

profile of v7, /device:TPU:40, one launch (start us, length us, event | category | flops | bytes accessed | tf_op | source)
XLA Modules:
  0.0 97.8 jit_solution(6330379057132379864)
XLA Ops:
  0.6 1.4 %pack.1 = (f32[520,128]{1,0:T(8,128)S(1)}, f32[520,128]{1,0:T(8,128)S(1)}) custom-call(f32[8,8,128,128]{3,2,1,0:T(8,128)} %tiles_hbm.3), custom_call_target="tpu_custom_call" | custom-call | tf_op jit(solution)/shard_map/pack/pallas_call | solution.py:568
  2.0 4.7 %collective-permute-start.2 = (f32[520,128]{1,0:T(8,128)S(1)}, f32[520,128]{1,0:T(8,128)S(1)}, u32[]{:S(2)}, u32[]{:S(2)}) collective-permute-start(f32[520,128]{1,0:T(8,128)S(1)} %get-tuple-element.27), channel_id=1, source_target_pairs={{0,8},{8,16},{16,24},{24,32},{32,40},{40,48},{48,56},{56,64},{64,7... | collective-permute-start | bytes 798728 | tf_op jit(solution)/shard_map/ppermute | solution.py:549
  6.7 1.3 %collective-permute-start.3 = (f32[520,128]{1,0:T(8,128)S(1)}, f32[520,128]{1,0:T(8,128)S(1)}, u32[]{:S(2)}, u32[]{:S(2)}) collective-permute-start(f32[520,128]{1,0:T(8,128)S(1)} %get-tuple-element.28), channel_id=1, source_target_pairs={{8,0},{16,8},{24,16},{32,24},{40,32},{48,40},{56,48},{64,56},{72,6... | collective-permute-start | bytes 798728 | tf_op jit(solution)/shard_map/ppermute | solution.py:548
  8.0 3.3 %start.1 = (f32[8,640,128]{2,1,0:T(8,128)S(1)}, f32[8,640,128]{2,1,0:T(8,128)S(1)}, s32[472]{0:T(512)S(1)}, bf16[4,8,128,256]{3,2,1,0:T(8,128)(2,1)S(1)}, f32[24...) custom-call(s32[1]{0:T(128)} %bitcast.where, ...), custom_call_target="tpu_custom_call" | custom-call | tf_op jit(solution)/shard_map/start/pallas_call | solution.py:578
  11.3 5.8 %collective-permute-start = (f32[192,128]{1,0:T(8,128)S(1)}, f32[192,128]{1,0:T(8,128)S(1)}, u32[]{:S(2)}, u32[]{:S(2)}) collective-permute-start(f32[192,128]{1,0:T(8,128)S(1)} %get-tuple-element.25), channel_id=1, source_target_pairs={{0,8},{8,16},{16,24},{24,32},{32,40},{40,48},{48,56},{56,64},{64,7... | collective-permute-start | bytes 294920 | tf_op jit(solution)/shard_map/ppermute | solution.py:549
  17.1 1.3 %collective-permute-start.1 = (f32[192,128]{1,0:T(8,128)S(1)}, f32[192,128]{1,0:T(8,128)S(1)}, u32[]{:S(2)}, u32[]{:S(2)}) collective-permute-start(f32[192,128]{1,0:T(8,128)S(1)} %get-tuple-element.26), channel_id=1, source_target_pairs={{8,0},{16,8},{24,16},{32,24},{40,32},{48,40},{56,48},{64,56},{72,6... | collective-permute-start | bytes 294920 | tf_op jit(solution)/shard_map/ppermute | solution.py:548
  18.5 2.2 %inner.1 = (f32[8,640,128]{2,1,0:T(8,128)S(1)}, f32[8,640,128]{2,1,0:T(8,128)S(1)}) custom-call(s32[472]{0:T(512)S(1)} %get-tuple-element.18.index, f32[24,1024]{1,0:T(8,128)S(1)} %get-tuple-element.19.cells, f32[8,640,128]{2,1,0:T(8,128)S(1)} %get-tuple-element.20.field, bf16[4,8,128,256]{3,2,1,0:T(8,128)(2,1)S(1)} %get-tuple-element.21.parts, ...), custom_call_target="tpu_custom_call" | custom-call | tf_op jit(solution)/shard_map/inner/pallas_call | solution.py:626
  20.6 0.0 collective-permute-done.above
  20.6 4.0 %collective-permute-done.1.below = f32[192,128]{1,0:T(8,128)S(1)} collective-permute-done((f32[192,128]{1,0:T(8,128)S(1)}, f32[192,128]{1,0:T(8,128)S(1)}, u32[]{:S(2)}, u32[]{:S(2)}) %collective-permute-start.1) | collective-permute-done | bytes 98336 | tf_op jit(solution)/shard_map/ppermute | solution.py:548
  24.6 0.0 collective-permute-done.2.tiles_above
  24.6 0.0 collective-permute-done.3.tiles_below
  24.6 2.2 %middle.1 = (f32[8,640,128]{2,1,0:T(8,128)S(1)}, f32[8,640,128]{2,1,0:T(8,128)S(1)}, f32[8,640,128]{2,1,0:T(8,128)S(1)}, f32[2,128]{1,0:T(2,128)S(1)}) custom-call(s32[472]{0:T(512)S(1)} %get-tuple-element.18.index, f32[24,1024]{1,0:T(8,128)S(1)} %get-tuple-element.19.cells, f32[8,640,128]{2,1,0:T(8,128)S(1)} %get-tuple-element.20.field, ...), custom_call_target="tpu_custom_call" | custom-call | tf_op jit(solution)/shard_map/middle/pallas_call | solution.py:639
  26.8 67.8 %all_to_all.5.everyone = f32[32,2,128]{2,1,0:T(2,128)S(1)} all-to-all(f32[32,2,128]{2,1,0:T(2,128)S(1)} %broadcast_in_dim.3), channel_id=1, replica_groups=mesh['groups'=2,'space'=32,'rhs'=8] {'space'}, dimensions={0} | all-to-all | bytes 65536 | tf_op jit(solution)/shard_map/all_to_all | solution.py:655
  94.6 3.2 %finish.1 = (f32[64,8,1024]{2,1,0:T(8,128)}, f32[64,8,1024]{2,1,0:T(8,128)}) custom-call(s32[472]{0:T(512)S(1)} %get-tuple-element.18.index, f32[32,2,128]{2,1,0:T(2,128)S(1)} %all_to_all.5.everyone, f32[8,640,128]{2,1,0:T(8,128)S(1)} %get-tuple-element.20.field, f32[8,640,128]{2,1,0:T(8,128)S(1)} %get-tuple-element.24.pre, ...), custom_call_target="tpu_custom_call" | custom-call | tf_op jit(solution)/shard_map/finish/pallas_call | solution.py:659
  (1 shorter events, 0.0 us)
Async XLA Ops:
  2.0 22.6 %collective-permute-start.2 = (f32[520,128]{1,0:T(8,128)S(1)}, f32[520,128]{1,0:T(8,128)S(1)}, u32[]{:S(2)}, u32[]{:S(2)}) collective-permute-start(f32[520,128]{1,0:T(8,128)S(1)} %get-tuple-element.27), channel_id=1, source_target_pairs={{0,8},{8,16},{16,24},{24,32},{32,40},{40,48},{48,56},{56,64},{64,7... | collective-permute-start | bytes 798728 | tf_op jit(solution)/shard_map/ppermute | solution.py:549
  6.7 17.9 %collective-permute-start.3 = (f32[520,128]{1,0:T(8,128)S(1)}, f32[520,128]{1,0:T(8,128)S(1)}, u32[]{:S(2)}, u32[]{:S(2)}) collective-permute-start(f32[520,128]{1,0:T(8,128)S(1)} %get-tuple-element.28), channel_id=1, source_target_pairs={{8,0},{16,8},{24,16},{32,24},{40,32},{48,40},{56,48},{64,56},{72,6... | collective-permute-start | bytes 798728 | tf_op jit(solution)/shard_map/ppermute | solution.py:548
  11.3 9.3 %collective-permute-start = (f32[192,128]{1,0:T(8,128)S(1)}, f32[192,128]{1,0:T(8,128)S(1)}, u32[]{:S(2)}, u32[]{:S(2)}) collective-permute-start(f32[192,128]{1,0:T(8,128)S(1)} %get-tuple-element.25), channel_id=1, source_target_pairs={{0,8},{8,16},{16,24},{24,32},{32,40},{40,48},{48,56},{56,64},{64,7... | collective-permute-start | bytes 294920 | tf_op jit(solution)/shard_map/ppermute | solution.py:549
  17.1 7.5 %collective-permute-start.1 = (f32[192,128]{1,0:T(8,128)S(1)}, f32[192,128]{1,0:T(8,128)S(1)}, u32[]{:S(2)}, u32[]{:S(2)}) collective-permute-start(f32[192,128]{1,0:T(8,128)S(1)} %get-tuple-element.26), channel_id=1, source_target_pairs={{8,0},{16,8},{24,16},{32,24},{40,32},{48,40},{56,48},{64,56},{72,6... | collective-permute-start | bytes 294920 | tf_op jit(solution)/shard_map/ppermute | solution.py:548

commit v8 on v7

--- a/solution.py
+++ b/solution.py
@@ -6,7 +6,6 @@
 from jax.experimental import pallas as pl
 from jax.experimental.pallas import tpu as pltpu
 from jax.sharding import PartitionSpec as P
-
 
 LEAKAGE = 0.05
 FOCAL_CURRENT = 16.0
@@ -115,24 +114,21 @@
     return lane < row, lane == row + HALF
 
 
-def pack_kernel(tiles_hbm, up_ref, down_ref, tiles, sems, *, rows):
-    copies = [pltpu.make_async_copy(tiles_hbm.at[r], tiles.at[n], sems.at[n]) for n, r in enumerate((0, rows - 1))]
-    for copy in copies:
-        copy.start()
+def pack(tiles, n, packed, first):
     moved, diagonal = below_diagonal()
     count = tiles.shape[1]
-    for n, packed in enumerate((up_ref, down_ref)):
-        copies[n].wait()
-        for t in range(count):
-            upper, lower = tiles[n, t, :HALF, :], tiles[n, t, HALF:, :]
-            packed[t * HALF : (t + 1) * HALF, :] = jnp.where(moved, pltpu.roll(lower, HALF, 1), upper)
-            at = count * HALF + t
-            packed[at : at + 1, :] = jnp.sum(jnp.where(diagonal, lower, 0.0), axis=0, keepdims=True)
-
-
-def unpacked(packed, t, count):
-    x = packed[t * HALF : (t + 1) * HALF, :]
-    diagonal = packed[count * HALF + t : count * HALF + t + 1, :]
+    for t in range(count):
+        upper, lower = tiles[n, t, :HALF, :], tiles[n, t, HALF:, :]
+        at = first + t * HALF
+        packed[at : at + HALF, :] = jnp.where(moved, pltpu.roll(lower, HALF, 1), upper)
+        at = first + count * HALF + t
+        packed[at : at + 1, :] = jnp.sum(jnp.where(diagonal, lower, 0.0), axis=0, keepdims=True)
+
+
+def unpacked(packed, first, t, count):
+    x = packed[first + t * HALF : first + (t + 1) * HALF, :]
+    at = first + count * HALF + t
+    diagonal = packed[at : at + 1, :]
     moved, _ = below_diagonal()
     top = jnp.where(moved, 0.0, x)
     bottom = pltpu.roll(jnp.where(moved, x, 0.0), HALF, 1)
@@ -259,6 +255,7 @@
     apply_tiles(field, pre, [(r, parts, n) for n, r in enumerate(outer_rows(rows))], rows, chunks, 1)
 
     for rim, first, outermost in ((up_ref, 0, 0), (down_ref, rows - 2, rows - 1)):
+        pack(tiles, 0 if first == 0 else 3, rim, 2 * pairs + cols // TILE * RIM)
         two = slice(first, first + 2)
         for t in range(cols // TILE):
             lanes = slice(t * TILE, (t + 1) * TILE)
@@ -319,8 +316,6 @@
     parts,
     above,
     below,
-    tiles_above,
-    tiles_below,
     inner_second,
     image,
     second,
@@ -413,11 +408,11 @@
     keep_rows(inner_second, second, range(1, rows - 1), rows, chunks, 1)
 
     def outer_tiles(c, _):
-        for tiles, row in ((tiles_above, 4), (tiles_below, 5)):
+        for rim, row in ((above, 4), (below, 5)):
             at = pl.ds(c * (CHUNK * RIM) + row, CHUNK, stride=RIM)
             to = pl.ds(c * (CHUNK * RIM) + row + 2, CHUNK, stride=RIM)
             for t in range(cols // TILE):
-                pair = jnp.concatenate(cut(unpacked(tiles, t, cols // TILE)), axis=1)
+                pair = jnp.concatenate(cut(unpacked(rim, 2 * pairs + cols // TILE * RIM, t, cols // TILE)), axis=1)
                 outer.at[t][to, :] = times_tile(outer.at[t][at, :], pair)
         for r, n in ((0, 0), (rows - 1, 3)):
             at = pl.ds(c * (CHUNK * rows) + r, CHUNK, stride=rows)
@@ -545,8 +540,10 @@
 def neighbours(up, down):
     count = lax.axis_size("space")
     ends = count - 1
-    below = lax.ppermute(up, "space", [((i + 1) % count, i) for i in range(ends)])
-    above = lax.ppermute(down, "space", [(i, (i + 1) % count) for i in range(ends)])
+    with jax.named_scope("up"):
+        below = lax.ppermute(up, "space", [((i + 1) % count, i) for i in range(ends)])
+    with jax.named_scope("down"):
+        above = lax.ppermute(down, "space", [(i, (i + 1) % count) for i in range(ends)])
     return above, below
 
 
@@ -557,7 +554,7 @@
     devices = lax.axis_size("space")
     f32 = jnp.float32
     sizes = dict(rows=rows, cols=cols, pairs=pairs, slots=slots)
-    strip, fields, rim = (rows, cols), (cols // TILE, slots * rows, TILE), (2 * pairs + cols // TILE * RIM, TILE)
+    strip, fields, rim = (rows, cols), (cols // TILE, slots * rows, TILE), (2 * pairs + cols // TILE * (RIM + HALF + 1), TILE)
     per_row = tile_inverse.shape[1:]
     limit = pltpu.CompilerParams(vmem_limit_bytes=24 * MIB)
     base_row = (lax.axis_index("space") * rows).astype(jnp.int32).reshape(1)
@@ -565,16 +562,6 @@
     def shaped(shape, dtype=f32):
         return jax.ShapeDtypeStruct(shape, dtype)
 
-    up, down = pl.pallas_call(
-        functools.partial(pack_kernel, rows=rows),
-        in_specs=[hbm()],
-        out_specs=[vmem()] * 2,
-        out_shape=[shaped((cols // TILE * (HALF + 1), TILE))] * 2,
-        scratch_shapes=[pltpu.VMEM((2, *per_row), f32), pltpu.SemaphoreType.DMA((2,))],
-        compiler_params=limit,
-        name="pack",
-    )(pltpu.with_memory_space_constraint(tile_inverse, pltpu.HBM))
-    tiles_above, tiles_below = neighbours(up, down)
     field, pre, index, parts, cells, inner_tiles, up, down = pl.pallas_call(
         functools.partial(start_kernel, **sizes),
         in_specs=[smem(), *[hbm()] * 8],
@@ -638,7 +625,7 @@
 
     image, second, last, sums = pl.pallas_call(
         functools.partial(middle_kernel, **sizes),
-        in_specs=[smem(), *[vmem()] * 9],
+        in_specs=[smem(), *[vmem()] * 7],
         out_specs=[vmem()] * 4,
         out_shape=[*[shaped(fields)] * 3, shaped((2, 2 * pairs))],
         scratch_shapes=[
@@ -650,7 +637,7 @@
         ],
         compiler_params=limit,
         name="middle",
-    )(index, cells, field, pre, parts, above, below, tiles_above, tiles_below, inner_second)
+    )(index, cells, field, pre, parts, above, below, inner_second)
     copies = jnp.broadcast_to(sums, (devices, *sums.shape))
     everyone = lax.all_to_all(copies, "space", split_axis=0, concat_axis=0, tiled=True)
 

time: 98.2 us -> 95.8 us (0.976)
  starting transfers between devices: 13.2 us -> 6.12 us
  waiting for transfers between devices: 3.99 us -> 9.58 us
  blocking collectives: 67.8 us -> 66.8 us
    ppermute x2 -> x1, starting transfers between devices: 10.6 us -> 4.81 us  [neighbours(): lax.ppermute(down, 'space', [(i, (i + 1) % count) for i in range(ends)])]
    ppermute x2 -> x1, waiting for transfers between devices: 0.01 us -> 4.7 us  [neighbours(): lax.ppermute(down, 'space', [(i, (i + 1) % count) for i in range(ends)])]
    pallas_call x1 -> x0, Pallas kernels: 1.35 us -> none  [on_device(): pl.pallas_call(functools.partial(pack_kernel, rows=rows), in_specs=[hbm()...]
    ppermute x2 -> x1, starting transfers between devices: 2.62 us -> 1.31 us  [neighbours(): lax.ppermute(up, 'space', [((i + 1) % count, i) for i in range(ends)])]
    ppermute x2 -> x1, waiting for transfers between devices: 3.99 us -> 4.88 us  [neighbours(): lax.ppermute(up, 'space', [((i + 1) % count, i) for i in range(ends)])]
  transfers between devices with their start and end apart: 4 -> 2, of which waited for: 1 -> 2; matrix products, arithmetic and copies ran while one was open for 0% -> 0% of each run, Pallas kernels for 6% -> 2%
where the time goes in v8:
time: 95.8 us; the launch traced here: 94.8 us
  blocking collectives  66.8 us (70%)
  Pallas kernels  11.6 us (12%)
  waiting for transfers between devices  9.58 us (10%)
  starting transfers between devices  6.12 us (6%)
    all_to_all x1, blocking collectives, on_device(): lax.all_to_all(copies, 'space', split_axis=0, concat_axis=0, tiled=True)  66.8 us
    ppermute x1, waiting for transfers between devices, neighbours(): lax.ppermute(up, 'space', [((i + 1) % count, i) for i in range(ends)])  4.88 us
    ppermute x1, starting transfers between devices, neighbours(): lax.ppermute(down, 'space', [(i, (i + 1) % count) for i in range(ends)])  4.81 us
    ppermute x1, waiting for transfers between devices, neighbours(): lax.ppermute(down, 'space', [(i, (i + 1) % count) for i in range(ends)])  4.7 us
    pallas_call x1, Pallas kernels, on_device(): pl.pallas_call(functools.partial(start_kernel, **sizes), in_specs=[smem()...  3.53 us
    pallas_call x1, Pallas kernels, on_device(): pl.pallas_call(functools.partial(finish_kernel, rows=rows, cols=cols, pai...  3.25 us
    pallas_call x1, Pallas kernels, on_device(): pl.pallas_call(functools.partial(middle_kernel, **sizes), in_specs=[smem(...  2.57 us
    pallas_call x1, Pallas kernels, on_device(): pl.pallas_call(functools.partial(inner_kernel, **sizes), in_specs=[smem()...  2.24 us
  transfers between devices with their start and end apart: 2, of which 2 were waited for; matrix products, arithmetic and copies ran while one was open for 0% of the time, Pallas kernels for 2%

profile of v8, /device:TPU:40, one launch (start us, length us, event | category | flops | bytes accessed | tf_op | source)
XLA Modules:
  0.0 94.8 jit_solution(14539048495256709853)
XLA Ops:
  0.6 3.5 %start.1 = (f32[8,640,128]{2,1,0:T(8,128)S(1)}, f32[8,640,128]{2,1,0:T(8,128)S(1)}, s32[472]{0:T(512)S(1)}, bf16[4,8,128,256]{3,2,1,0:T(8,128)(2,1)S(1)}, f32[24...) custom-call(s32[1]{0:T(128)} %bitcast.where, ...), custom_call_target="tpu_custom_call" | custom-call | tf_op jit(solution)/shard_map/start/pallas_call | solution.py:565
  4.2 4.8 %collective-permute-start = (f32[712,128]{1,0:T(8,128)S(1)}, f32[712,128]{1,0:T(8,128)S(1)}, u32[]{:S(2)}, u32[]{:S(2)}) collective-permute-start(f32[712,128]{1,0:T(8,128)S(1)} %get-tuple-element.23), channel_id=1, source_target_pairs={{0,8},{8,16},{16,24},{24,32},{32,40},{40,48},{48,56},{56,64},{64,7... | collective-permute-start | bytes 1093640 | tf_op jit(solution)/shard_map/down/ppermute | solution.py:546
  9.0 1.3 %collective-permute-start.1 = (f32[712,128]{1,0:T(8,128)S(1)}, f32[712,128]{1,0:T(8,128)S(1)}, u32[]{:S(2)}, u32[]{:S(2)}) collective-permute-start(f32[712,128]{1,0:T(8,128)S(1)} %get-tuple-element.24), channel_id=1, source_target_pairs={{8,0},{16,8},{24,16},{32,24},{40,32},{48,40},{56,48},{64,56},{72,6... | collective-permute-start | bytes 1093640 | tf_op jit(solution)/shard_map/up/ppermute | solution.py:544
  10.3 2.2 %inner.1 = (f32[8,640,128]{2,1,0:T(8,128)S(1)}, f32[8,640,128]{2,1,0:T(8,128)S(1)}) custom-call(s32[472]{0:T(512)S(1)} %get-tuple-element.16.index, f32[24,1024]{1,0:T(8,128)S(1)} %get-tuple-element.17.cells, f32[8,640,128]{2,1,0:T(8,128)S(1)} %get-tuple-element.18.field, bf16[4,8,128,256]{3,2,1,0:T(8,128)(2,1)S(1)} %get-tuple-element.19.parts, ...), custom_call_target="tpu_custom_call" | custom-call | tf_op jit(solution)/shard_map/inner/pallas_call | solution.py:613
  12.6 4.7 %collective-permute-done.above = f32[712,128]{1,0:T(8,128)S(1)} collective-permute-done((f32[712,128]{1,0:T(8,128)S(1)}, f32[712,128]{1,0:T(8,128)S(1)}, u32[]{:S(2)}, u32[]{:S(2)}) %collective-permute-start) | collective-permute-done | bytes 364576 | tf_op jit(solution)/shard_map/down/ppermute | solution.py:546
  17.3 4.9 %collective-permute-done.1.below = f32[712,128]{1,0:T(8,128)S(1)} collective-permute-done((f32[712,128]{1,0:T(8,128)S(1)}, f32[712,128]{1,0:T(8,128)S(1)}, u32[]{:S(2)}, u32[]{:S(2)}) %collective-permute-start.1) | collective-permute-done | bytes 364576 | tf_op jit(solution)/shard_map/up/ppermute | solution.py:544
  22.1 2.6 %middle.1 = (f32[8,640,128]{2,1,0:T(8,128)S(1)}, f32[8,640,128]{2,1,0:T(8,128)S(1)}, f32[8,640,128]{2,1,0:T(8,128)S(1)}, f32[2,128]{1,0:T(2,128)S(1)}) custom-call(s32[472]{0:T(512)S(1)} %get-tuple-element.16.index, f32[24,1024]{1,0:T(8,128)S(1)} %get-tuple-element.17.cells, f32[8,640,128]{2,1,0:T(8,128)S(1)} %get-tuple-element.18.field, ...), custom_call_target="tpu_custom_call" | custom-call | tf_op jit(solution)/shard_map/middle/pallas_call | solution.py:626
  24.7 66.8 %all_to_all.5.everyone = f32[32,2,128]{2,1,0:T(2,128)S(1)} all-to-all(f32[32,2,128]{2,1,0:T(2,128)S(1)} %broadcast_in_dim.3), channel_id=1, replica_groups=mesh['groups'=2,'space'=32,'rhs'=8] {'space'}, dimensions={0} | all-to-all | bytes 65536 | tf_op jit(solution)/shard_map/all_to_all | solution.py:642
  91.6 3.2 %finish.1 = (f32[64,8,1024]{2,1,0:T(8,128)}, f32[64,8,1024]{2,1,0:T(8,128)}) custom-call(s32[472]{0:T(512)S(1)} %get-tuple-element.16.index, f32[32,2,128]{2,1,0:T(2,128)S(1)} %all_to_all.5.everyone, f32[8,640,128]{2,1,0:T(8,128)S(1)} %get-tuple-element.18.field, f32[8,640,128]{2,1,0:T(8,128)S(1)} %get-tuple-element.22.pre, ...), custom_call_target="tpu_custom_call" | custom-call | tf_op jit(solution)/shard_map/finish/pallas_call | solution.py:646
  (1 shorter events, 0.0 us)
Async XLA Ops:
  4.2 13.1 %collective-permute-start = (f32[712,128]{1,0:T(8,128)S(1)}, f32[712,128]{1,0:T(8,128)S(1)}, u32[]{:S(2)}, u32[]{:S(2)}) collective-permute-start(f32[712,128]{1,0:T(8,128)S(1)} %get-tuple-element.23), channel_id=1, source_target_pairs={{0,8},{8,16},{16,24},{24,32},{32,40},{40,48},{48,56},{56,64},{64,7... | collective-permute-start | bytes 1093640 | tf_op jit(solution)/shard_map/down/ppermute | solution.py:546
  9.0 13.1 %collective-permute-start.1 = (f32[712,128]{1,0:T(8,128)S(1)}, f32[712,128]{1,0:T(8,128)S(1)}, u32[]{:S(2)}, u32[]{:S(2)}) collective-permute-start(f32[712,128]{1,0:T(8,128)S(1)} %get-tuple-element.24), channel_id=1, source_target_pairs={{8,0},{16,8},{24,16},{32,24},{40,32},{48,40},{56,48},{64,56},{72,6... | collective-permute-start | bytes 1093640 | tf_op jit(solution)/shard_map/up/ppermute | solution.py:544
